TPU v7x, 256 devices: a whole 4x4x8 slice. The times are simulated.
256 devices in a mesh: expert: 64 (over z_hi, y, x), shard: 4 (over z_lo, core).
Axes of the slice: x: 4, y: 4, z: 8 (z_hi: 4, z_lo: 2; z = z_hi * 2 + z_lo), core: 2. Of those that a mesh axis runs over, the one named last changes fastest.
Arguments:
- w_gate: float32 [64, 2048, 1024], P('expert', 'shard'), may hold values from -0.1875 to 0.1875
- avg_gate: float32 [64, 2048, 1024], P('expert', 'shard'), may hold values from -0.125 to 0.125
- w_up: float32 [64, 2048, 1024], P('expert', 'shard'), may hold values from -0.1875 to 0.1875
- avg_up: float32 [64, 2048, 1024], P('expert', 'shard'), may hold values from -0.125 to 0.125
- mix_share: float32 [64], P('expert'), may hold values from 0.2 to 0.8
- router_weight: float32 [2048, 64], P('shard', 'expert'), may hold values from -0.125 to 0.125
- router_gain: float32 [2048], P('shard'), may hold values from 0.25 to 1.75
Outputs:
- serve_gate: bfloat16 [64, 2048, 1024], P('expert')
- serve_up: bfloat16 [64, 2048, 1024], P('expert')
- scale_gate: float32 [64, 1024], P('expert')
- scale_up: float32 [64, 1024], P('expert')
- serve_router: bfloat16 [2048, 64], replicated
All inputs are finite; a program needn't handle non-finite values.
Results may differ from a plain program's by a relative error of at most 0.001.
Values may be sent and summed in bfloat16 or wider, within the bound.
No kernel may reach another device: no remote copies, remote signals or barrier semaphores. Data moves between devices by JAX's collectives and lax.ppermute only.
A program may use at most 64 MiB of HBM per device.

v0:
```python
import functools

import jax
import jax.numpy as jnp
from jax import lax
from jax.experimental import pallas as pl
from jax.experimental.pallas import tpu as pltpu
from jax.sharding import PartitionSpec as P


CORE, CHIP = 1, 2
GATE = (64, 256, 192)
UP = (256, 128, 64, 64)
LOADS = 8
MIB = 1 << 20
VMEM = pl.BlockSpec(memory_space=pltpu.VMEM)
HBM = pl.BlockSpec(memory_space=pltpu.HBM)
SMEM = pl.BlockSpec(memory_space=pltpu.SMEM)


def swap(x, axis, mask):
    n = lax.axis_size(axis)
    return lax.ppermute(x, axis, [(i, i ^ mask) for i in range(n)])


def call(body, out, ins, mib, flops, **kw):
    return pl.pallas_call(
        body,
        out_shape=out,
        compiler_params=pltpu.CompilerParams(vmem_limit_bytes=mib * MIB),
        cost_estimate=pl.CostEstimate(flops=flops, bytes_accessed=4 * MIB, transcendentals=0),
        in_specs=ins,
        **kw,
    )


def mean_body(share_ref, w_ref, avg_ref, fresh_ref, sums_ref, w_buf, avg_buf, sem):
    rows = w_buf.shape[0]
    step = rows // LOADS

    def copies(k):
        at = pl.ds(k * step, step)
        return (
            pltpu.make_async_copy(w_ref.at[0, at], w_buf.at[at], sem.at[0, k]),
            pltpu.make_async_copy(avg_ref.at[0, at], avg_buf.at[at], sem.at[1, k]),
        )

    for k in range(LOADS):
        for c in copies(k):
            c.start()
    share = share_ref[0]
    rest = 1.0 - share
    total = jnp.zeros((8, w_buf.shape[1]), jnp.float32)
    for k in range(LOADS):
        for c in copies(k):
            c.wait()

        def tile(i, total):
            at = pl.ds(pl.multiple_of(k * step + i * 8, 8), 8)
            fresh = share * w_buf[at] + rest * avg_buf[at]
            fresh_ref[at] = fresh
            return total + fresh * fresh

        total = lax.fori_loop(0, step // 8, tile, total, unroll=True)
    sums_ref[...] = jnp.sum(total, axis=0, keepdims=True)


def mean_of(share, w, avg, mib):
    _, rows, columns = w.shape
    return call(
        mean_body,
        (pltpu.VMEM((rows, columns), jnp.float32), pltpu.VMEM((1, columns), jnp.float32)),
        [SMEM, HBM, HBM],
        mib,
        4 << 20,
        out_specs=(VMEM, VMEM),
        scratch_shapes=[
            pltpu.VMEM((rows, columns), jnp.float32),
            pltpu.VMEM((rows, columns), jnp.float32),
            pltpu.SemaphoreType.DMA((2, LOADS)),
        ],
    )(share, w, avg)


def narrow_body(first, blocks, scaled, fresh_ref, pair_ref, other_ref, *outs):
    columns = fresh_ref.shape[1]
    scale = jnp.sqrt(pair_ref[:, :columns] + other_ref[:, :columns])
    if scaled:
        outs[-1][...] = scale
    inverse = 1.0 / scale
    at = first
    for rows, out in zip(blocks, outs):
        for i in range(rows // 16):
            out[0, pl.ds(i * 16, 16)] = (fresh_ref[pl.ds(at + i * 16, 16)] * inverse).astype(out.dtype)
        at += rows


def narrow(fresh, totals, first, blocks, scaled):
    columns = fresh.shape[1]
    outs = [pltpu.VMEM((1, rows, columns), jnp.bfloat16) for rows in blocks]
    if scaled:
        outs.append(jax.ShapeDtypeStruct((1, columns), jnp.float32))
    return call(
        functools.partial(narrow_body, first, blocks, scaled),
        tuple(outs),
        [VMEM, VMEM, VMEM],
        2,
        2 << 20,
        out_specs=(VMEM,) * len(outs),
    )(fresh, *totals)


def place_body(places, *refs):
    out, sem = refs[-2], refs[-1]
    me = lax.axis_index("shard")
    copies = []
    for k, (mask, at, rows, shard_rows) in enumerate(places):
        start = pl.multiple_of((me ^ mask) * shard_rows + at, 16)
        copies.append(pltpu.make_async_copy(refs[k].at[0], out.at[0, pl.ds(start, rows)], sem.at[k]))
    for c in copies:
        c.start()
    for c in copies:
        c.wait()


def place(pieces, shape, into=None):
    blocks = [p[0] for p in pieces]
    places = tuple((m, at, b.shape[1], total) for b, m, at, total in pieces)
    n = len(blocks)
    again = into is not None
    return call(
        functools.partial(place_body, places),
        jax.ShapeDtypeStruct(shape, blocks[0].dtype),
        [VMEM] * n + [HBM] * again,
        6,
        1 << 20,
        out_specs=HBM,
        scratch_shapes=[pltpu.SemaphoreType.DMA((n,))],
        **({"input_output_aliases": {n: 0}} if again else {}),
    )(*blocks, *([into] if again else []))


def starts(blocks):
    at, out = 0, []
    for rows in blocks:
        out.append(at)
        at += rows
    return out


def from_all(own):
    chips = [swap(b, "shard", CHIP) for b in own]
    cores = [swap(b, "shard", CORE) for b in own]
    boths = [swap(b, "shard", CORE) for b in chips]
    return {0: own, CORE: cores, CHIP: chips, CORE | CHIP: boths}


BITS = (("shard", CHIP), ("expert", 16), ("expert", 32), ("expert", 1), ("expert", 2), ("expert", 4), ("expert", 8))


def lows_body(*outs):
    for (axis, mask), out in zip(BITS, outs):
        low = jnp.where((lax.axis_index(axis) & mask) == 0, 1.0, 0.0)
        out[...] = jnp.full(out.shape, low, jnp.float32)


def lows_of(rows):
    outs = call(
        lows_body,
        tuple(jax.ShapeDtypeStruct((1, rows), jnp.float32) for _ in BITS),
        [],
        1,
        1 << 10,
        out_specs=(VMEM,) * len(BITS),
    )()
    return dict(zip(BITS, outs))


def in_order(low, own, other, dim):
    low = low.reshape((1,) * (own.ndim - 2) + low.shape) > 0.5
    return jnp.concatenate([jnp.where(low, own, other), jnp.where(low, other, own)], axis=dim)


def router_body(own_ref, other_ref, out_ref):
    z, chips, plane, rows = own_ref.shape
    first = (lax.axis_index("shard") & CORE) == 0
    for k in range(z):
        for chip in range(chips):
            own, other = own_ref[k, chip], other_ref[k, chip]
            for core in range(2):
                at = (chip * 2 + core) * rows
                value = jnp.where(first, own, other) if core == 0 else jnp.where(first, other, own)
                out_ref[pl.ds(k * plane, plane), pl.ds(at, rows)] = value


def router_of(lows, own, other):
    x = in_order(lows["shard", CHIP], own[None, None], other[None, None], 1)
    z1, z2, z3 = (swap(x, "expert", 16 * k) for k in (1, 2, 3))
    bit = lows["expert", 16]
    x = in_order(lows["expert", 32], in_order(bit, x, z1, 0), in_order(bit, z2, z3, 0), 0)
    for mask in (1, 2, 4, 8):
        x = in_order(lows["expert", mask], x, swap(x, "expert", mask), 2)
    other = swap(x, "shard", CORE)
    z, chips, plane, rows = x.shape
    return call(
        router_body,
        jax.ShapeDtypeStruct((z * plane, chips * 2 * rows), x.dtype),
        [VMEM, VMEM],
        2,
        1 << 20,
        out_specs=VMEM,
    )(x, other).T


def per_device(w_gate, avg_gate, w_up, avg_up, mix_share, router_weight, router_gain):
    rows, columns = w_gate.shape[1:]
    shape = (1, lax.axis_size("shard") * rows, columns)
    part = (router_weight.T * router_gain[None]).astype(jnp.bfloat16)
    lows = lows_of(rows)

    fresh_gate, sums_gate = mean_of(mix_share, w_gate, avg_gate, 60)
    pair = sums_gate + swap(sums_gate, "shard", CORE)
    pair = jnp.concatenate([pair, part.astype(jnp.float32)], axis=1)
    totals_gate = pair, swap(pair, "shard", CHIP)
    (gate_0,) = narrow(fresh_gate, totals_gate, 0, GATE[:1], False)
    *gate_rest, scale_gate = narrow(fresh_gate, totals_gate, GATE[0], GATE[1:], True)
    gate = from_all([gate_0, *gate_rest])

    fresh_up, sums_up = mean_of(mix_share, w_up, avg_up, 56)
    pair = sums_up + swap(sums_up, "shard", CORE)
    totals_up = pair, swap(pair, "shard", CHIP)
    *own_up, scale_up = narrow(fresh_up, totals_up, 0, UP, True)
    up = from_all(own_up)

    gate_at, up_at = starts(GATE), starts(UP)
    serve_gate = place(
        [(b, m, at, rows) for m, bs in gate.items() for b, at in zip(bs, gate_at)], shape
    )
    early, late = [], []
    for m, bs in up.items():
        for k, (b, at) in enumerate(zip(bs, up_at)):
            (late if m & CHIP and k >= 2 else early).append((b, m, at, rows))
    serve_up = place(late, shape, place(early, shape))

    other = totals_gate[1][:, columns:].astype(jnp.bfloat16)
    serve_router = router_of(lows, part, other)
    return (serve_gate, serve_up, scale_gate, scale_up, serve_router)


def solution(mesh):
    return jax.shard_map(
        per_device,
        mesh=mesh,
        in_specs=(
            P("expert", "shard", None),
            P("expert", "shard", None),
            P("expert", "shard", None),
            P("expert", "shard", None),
            P("expert"),
            P("shard", "expert"),
            P("shard"),
        ),
        out_specs=(
            P("expert", None, None),
            P("expert", None, None),
            P("expert", None),
            P("expert", None),
            P(),
        ),
        check_vma=False,
    )
```

profile of v0, /device:TPU:1, one launch (start us, length us, event | category | flops | bytes accessed | tf_op | source)
XLA Modules:
  0.0 98.0 jit_solution(14615315048794842120)
XLA Ops:
  1.3 2.3 %shard_map.110 = (f32[512,1024]{1,0:T(8,128)S(1)}, f32[1,1024]{1,0:T(1,128)S(1)}) custom-call(f32[1]{0:T(128)S(6)} %copy.15.share_ref, f32[1,512,1024]{2,1,0:T(8,128)} %w_ref.2, f32[1,512,1024]{2,1,0:T(8,128)} %avg_ref.2), custom_call_target="tpu_custom_call" | custom-call | flops 4194304 | bytes 4194304 | tf_op jit(solution)/shard_map/pallas_call | solution.py:70
  3.6 3.3 %collective-permute-start = (f32[1,1024]{1,0:T(1,128)S(1)}, f32[1,1024]{1,0:T(1,128)S(1)}, u32[]{:S(2)}, u32[]{:S(2)}) collective-permute-start(f32[1,1024]{1,0:T(1,128)S(1)} %get-tuple-element.25), channel_id=1, source_target_pairs={{0,1},{1,0},{2,3},{3,2},{4,5},{5,4},{6,7},{7,6},{8,9},{9,8},{10,11... | collective-permute-start | bytes 12296 | tf_op jit(solution)/shard_map/ppermute | solution.py:23
  6.9 2.3 %shard_map.114 = (f32[512,1024]{1,0:T(8,128)S(1)}, f32[1,1024]{1,0:T(1,128)S(1)}) custom-call(f32[1]{0:T(128)S(6)} %copy.15.share_ref, f32[1,512,1024]{2,1,0:T(8,128)} %w_ref.3, f32[1,512,1024]{2,1,0:T(8,128)} %avg_ref.3), custom_call_target="tpu_custom_call" | custom-call | flops 4194304 | bytes 4194304 | tf_op jit(solution)/shard_map/pallas_call | solution.py:70
  9.3 0.1 collective-permute-start.11
  9.5 0.1 collective-permute-start.1
  9.6 2.4 %collective-permute-done.1.other_ref = f32[1,1536]{1,0:T(1,128)S(1)} collective-permute-done((f32[1,1536]{1,0:T(1,128)S(1)}, f32[1,1536]{1,0:T(1,128)S(1)}, u32[]{:S(2)}, u32[]{:S(2)}) %collective-permute-start.1) | collective-permute-done | bytes 6176 | tf_op jit(solution)/shard_map/ppermute | solution.py:23
  12.1 1.5 %collective-permute-start.25 = (bf16[1,2,1,512]{3,2,1,0:T(2,128)(2,1)S(1)}, bf16[1,2,1,512]{3,2,1,0:T(2,128)(2,1)S(1)}, u32[]{:S(2)}, u32[]{:S(2)}) collective-permute-start(bf16[1,2,1,512]{3,2,1,0:T(2,128)(2,1)S(1)} %constant_dynamic-update-slice_fusion), channel_id=1, source_target_pairs={{0,64},{4,68},{8,72},{12,76},{16,80},{20,84},{24,88},{28,92},{32,9... | collective-permute-start | bytes 6152 | tf_op jit(solution)/shard_map/ppermute | solution.py:23
  13.6 4.9 %collective-permute-start.26 = (bf16[1,2,1,512]{3,2,1,0:T(2,128)(2,1)S(1)}, bf16[1,2,1,512]{3,2,1,0:T(2,128)(2,1)S(1)}, u32[]{:S(2)}, u32[]{:S(2)}) collective-permute-start(bf16[1,2,1,512]{3,2,1,0:T(2,128)(2,1)S(1)} %constant_dynamic-update-slice_fusion), channel_id=1, source_target_pairs={{0,128},{4,132},{8,136},{12,140},{16,144},{20,148},{24,152},{28,15... | collective-permute-start | bytes 6152 | tf_op jit(solution)/shard_map/ppermute | solution.py:23
  18.6 1.4 %collective-permute-done.26 = bf16[1,2,1,512]{3,2,1,0:T(2,128)(2,1)S(1)} collective-permute-done((bf16[1,2,1,512]{3,2,1,0:T(2,128)(2,1)S(1)}, bf16[1,2,1,512]{3,2,1,0:T(2,128)(2,1)S(1)}, u32[]{:S(2)}, u32[]{:S(2)}) %collective-permute-start.26) | collective-permute-done | bytes 2080 | tf_op jit(solution)/shard_map/ppermute | solution.py:23
  20.0 3.1 %collective-permute-done.27 = bf16[1,2,1,512]{3,2,1,0:T(2,128)(2,1)S(1)} collective-permute-done((bf16[1,2,1,512]{3,2,1,0:T(2,128)(2,1)S(1)}, bf16[1,2,1,512]{3,2,1,0:T(2,128)(2,1)S(1)}, u32[]{:S(2)}, u32[]{:S(2)}) %collective-permute-start.27) | collective-permute-done | bytes 2080 | tf_op jit(solution)/shard_map/ppermute | solution.py:23
  23.2 1.3 %collective-permute-start.28 = (bf16[4,2,1,512]{3,2,1,0:T(2,128)(2,1)S(1)}, bf16[4,2,1,512]{3,2,1,0:T(2,128)(2,1)S(1)}, u32[]{:S(2)}, u32[]{:S(2)}) collective-permute-start(bf16[4,2,1,512]{3,2,1,0:T(2,128)(2,1)S(1)} %pad_maximum_fusion.3), channel_id=1, source_target_pairs={{0,4},{4,0},{8,12},{12,8},{16,20},{20,16},{24,28},{28,24},{32,36},... | collective-permute-start | bytes 24584 | tf_op jit(solution)/shard_map/ppermute | solution.py:23
  24.6 1.5 %collective-permute-done.28 = bf16[4,2,1,512]{3,2,1,0:T(2,128)(2,1)S(1)} collective-permute-done((bf16[4,2,1,512]{3,2,1,0:T(2,128)(2,1)S(1)}, bf16[4,2,1,512]{3,2,1,0:T(2,128)(2,1)S(1)}, u32[]{:S(2)}, u32[]{:S(2)}) %collective-permute-start.28) | collective-permute-done | bytes 8224 | tf_op jit(solution)/shard_map/ppermute | solution.py:23
  26.2 2.8 %collective-permute-start.29 = (bf16[4,2,2,512]{3,2,1,0:T(2,128)(2,1)S(1)}, bf16[4,2,2,512]{3,2,1,0:T(2,128)(2,1)S(1)}, u32[]{:S(2)}, u32[]{:S(2)}) collective-permute-start(bf16[4,2,2,512]{3,2,1,0:T(2,128)(2,1)S(1)} %pad_maximum_fusion.4), channel_id=1, source_target_pairs={{0,8},{4,12},{8,0},{12,4},{16,24},{20,28},{24,16},{28,20},{32,40},... | collective-permute-start | bytes 49160 | tf_op jit(solution)/shard_map/ppermute | solution.py:23
  29.1 0.9 collective-permute-start.12
  30.0 0.4 collective-permute-done.29
  30.5 1.4 %collective-permute-start.30 = (bf16[4,2,4,512]{3,2,1,0:T(4,128)(2,1)S(1)}, bf16[4,2,4,512]{3,2,1,0:T(4,128)(2,1)S(1)}, u32[]{:S(2)}, u32[]{:S(2)}) collective-permute-start(bf16[4,2,4,512]{3,2,1,0:T(4,128)(2,1)S(1)} %pad_maximum_fusion.2), channel_id=1, source_target_pairs={{0,16},{4,20},{8,24},{12,28},{16,0},{20,4},{24,8},{28,12},{32,48},... | collective-permute-start | bytes 98312 | tf_op jit(solution)/shard_map/ppermute | solution.py:23
  31.9 0.7 shard_map.115
  32.6 5.8 %collective-permute-start.19 = (bf16[1,64,1024]{2,1,0:T(8,128)(2,1)S(1)}, bf16[1,64,1024]{2,1,0:T(8,128)(2,1)S(1)}, u32[]{:S(2)}, u32[]{:S(2)}) collective-permute-start(bf16[1,64,1024]{2,1,0:T(8,128)(2,1)S(1)} %get-tuple-element.30.refs_2_), channel_id=1, source_target_pairs={{0,1},{1,0},{2,3},{3,2},{4,5},{5,4},{6,7},{7,6},{8,9},{9,8},{10,11... | collective-permute-start | bytes 393224 | tf_op jit(solution)/shard_map/ppermute | solution.py:23
  38.3 0.7 collective-permute-start.13
  39.1 0.3 collective-permute-start.20
  39.4 0.7 collective-permute-start.14
  40.2 2.7 %collective-permute-start.31 = (bf16[4,2,8,512]{3,2,1,0:T(8,128)(2,1)S(1)}, bf16[4,2,8,512]{3,2,1,0:T(8,128)(2,1)S(1)}, u32[]{:S(2)}, u32[]{:S(2)}) collective-permute-start(bf16[4,2,8,512]{3,2,1,0:T(8,128)(2,1)S(1)} %pad_maximum_fusion.1), channel_id=1, source_target_pairs={{0,32},{4,36},{8,40},{12,44},{16,48},{20,52},{24,56},{28,60},{32,0... | collective-permute-start | bytes 196616 | tf_op jit(solution)/shard_map/ppermute | solution.py:23
  43.0 1.9 %collective-permute-done.31 = bf16[4,2,8,512]{3,2,1,0:T(8,128)(2,1)S(1)} collective-permute-done((bf16[4,2,8,512]{3,2,1,0:T(8,128)(2,1)S(1)}, bf16[4,2,8,512]{3,2,1,0:T(8,128)(2,1)S(1)}, u32[]{:S(2)}, u32[]{:S(2)}) %collective-permute-start.31) | collective-permute-done | bytes 65568 | tf_op jit(solution)/shard_map/ppermute | solution.py:23
  44.9 0.7 collective-permute-start.22
  45.6 1.9 %collective-permute-start.18 = (bf16[1,128,1024]{2,1,0:T(8,128)(2,1)S(1)}, bf16[1,128,1024]{2,1,0:T(8,128)(2,1)S(1)}, u32[]{:S(2)}, u32[]{:S(2)}) collective-permute-start(bf16[1,128,1024]{2,1,0:T(8,128)(2,1)S(1)} %get-tuple-element.33.refs_1_), channel_id=1, source_target_pairs={{0,1},{1,0},{2,3},{3,2},{4,5},{5,4},{6,7},{7,6},{8,9},{9,8},{10,11... | collective-permute-start | bytes 786440 | tf_op jit(solution)/shard_map/ppermute | solution.py:23
  47.6 0.7 collective-permute-start.21
  48.3 0.7 collective-permute-start.5
  49.1 0.7 collective-permute-start.2
  49.8 15.4 %collective-permute-done.5.refs_6_ = bf16[1,64,1024]{2,1,0:T(8,128)(2,1)S(1)} collective-permute-done((bf16[1,64,1024]{2,1,0:T(8,128)(2,1)S(1)}, bf16[1,64,1024]{2,1,0:T(8,128)(2,1)S(1)}, u32[]{:S(2)}, u32[]{:S(2)}) %collective-permute-start.5) | collective-permute-done | bytes 131104 | tf_op jit(solution)/shard_map/ppermute | solution.py:23
  65.2 2.5 %collective-permute-start.32 = (bf16[4,2,16,512]{3,2,1,0:T(8,128)(2,1)S(1)}, bf16[4,2,16,512]{3,2,1,0:T(8,128)(2,1)S(1)}, u32[]{:S(2)}, u32[]{:S(2)}) collective-permute-start(bf16[4,2,16,512]{3,2,1,0:T(8,128)(2,1)S(1)} %pad_maximum_fusion.own_ref), channel_id=1, source_target_pairs={{0,1},{1,0},{2,3},{3,2},{4,5},{5,4},{6,7},{7,6},{8,9},{9,8},{10,11... | collective-permute-start | bytes 393224 | tf_op jit(solution)/shard_map/ppermute | solution.py:23
  67.7 0.7 shard_map.112
  68.4 0.7 collective-permute-start.6
  69.1 0.3 collective-permute-start.15
  69.4 0.7 collective-permute-start.7
  70.1 0.5 collective-permute-start.17
  70.6 0.1 collective-permute-start.16
  70.7 0.4 collective-permute-start.23
  71.1 1.2 %collective-permute-done.16.refs_3_ = bf16[1,64,1024]{2,1,0:T(8,128)(2,1)S(1)} collective-permute-done((bf16[1,64,1024]{2,1,0:T(8,128)(2,1)S(1)}, bf16[1,64,1024]{2,1,0:T(8,128)(2,1)S(1)}, u32[]{:S(2)}, u32[]{:S(2)}) %collective-permute-start.16) | collective-permute-done | bytes 131104 | tf_op jit(solution)/shard_map/ppermute | solution.py:23
  72.3 0.4 collective-permute-start.24
  72.7 17.5 %collective-permute-done.7.refs_8_ = bf16[1,192,1024]{2,1,0:T(8,128)(2,1)S(1)} collective-permute-done((bf16[1,192,1024]{2,1,0:T(8,128)(2,1)S(1)}, bf16[1,192,1024]{2,1,0:T(8,128)(2,1)S(1)}, u32[]{:S(2)}, u32[]{:S(2)}) %collective-permute-start.7) | collective-permute-done | bytes 393248 | tf_op jit(solution)/shard_map/ppermute | solution.py:23
  90.3 0.9 collective-permute-start.3
  91.1 0.5 collective-permute-start.4
  91.6 0.1 collective-permute-start.10
  91.7 0.4 collective-permute-start.8
  92.2 0.7 shard_map.119
  92.9 1.9 %shard_map.116.refs_4_ = bf16[1,2048,1024]{2,1,0:T(8,128)(2,1)} custom-call(bf16[1,256,1024]{2,1,0:T(8,128)(2,1)S(1)} %get-tuple-element.32.refs_0_, bf16[1,128,1024]{2,1,0:T(8,128)(2,1)S(1)} %get-tuple-element.33.refs_1_, bf16[1,64,1024]{2,1,0:T(8,128)(2,1)S(1)} %get-tuple-element.30.refs_2_, bf16[1,64,1024]{2,1,0:T(8,128)(2,1)S(1)} %get-tuple-element.31.refs_3_, ...), custom_call_target="tpu_custom_call" | custom-call | flops 1048576 | bytes 4194304 | tf_op jit(solution)/shard_map/pallas_call | solution.py:131
  94.8 0.8 shard_map.117
  95.7 2.1 %shard_map.113 = bf16[1,2048,1024]{2,1,0:T(8,128)(2,1)} custom-call(bf16[1,64,1024]{2,1,0:T(8,128)(2,1)S(1)} %shard_map.111.refs_0_, bf16[1,256,1024]{2,1,0:T(8,128)(2,1)S(1)} %get-tuple-element.26.refs_1_, bf16[1,192,1024]{2,1,0:T(8,128)(2,1)S(1)} %get-tuple-element.27.refs_2_, bf16[1,64,1024]{2,1,0:T(8,128)(2,1)S(1)} %collective-permute-done.2.refs_3_, ...), custom_call_target="tpu_custom_call" | custom-call | flops 1048576 | bytes 4194304 | tf_op jit(solution)/shard_map/pallas_call | solution.py:131
  (57 shorter events, 0.8 us)
Async XLA Ops:
  3.6 5.8 %copy-start = (f32[512,1]{0,1:T(1,128)S(1)}, f32[512,1]{0,1:T(1,128)}, u32[]{:S(2)}) copy-start(f32[512,1]{0,1:T(1,128)} %param.12) | copy-start | bytes 6148
  3.6 5.7 %copy-start.1 = (f32[512]{0:T(512)S(1)}, f32[512]{0:T(512)}, u32[]{:S(2)}) copy-start(f32[512]{0:T(512)} %param.13) | copy-start | bytes 6148
  3.6 5.8 %collective-permute-start = (f32[1,1024]{1,0:T(1,128)S(1)}, f32[1,1024]{1,0:T(1,128)S(1)}, u32[]{:S(2)}, u32[]{:S(2)}) collective-permute-start(f32[1,1024]{1,0:T(1,128)S(1)} %get-tuple-element.25), channel_id=1, source_target_pairs={{0,1},{1,0},{2,3},{3,2},{4,5},{5,4},{6,7},{7,6},{8,9},{9,8},{10,11... | collective-permute-start | bytes 12296 | tf_op jit(solution)/shard_map/ppermute | solution.py:23
  9.3 19.8 %collective-permute-start.11 = (f32[1,1024]{1,0:T(1,128)S(1)}, f32[1,1024]{1,0:T(1,128)S(1)}, u32[]{:S(2)}, u32[]{:S(2)}) collective-permute-start(f32[1,1024]{1,0:T(1,128)S(1)} %get-tuple-element.29), channel_id=1, source_target_pairs={{0,1},{1,0},{2,3},{3,2},{4,5},{5,4},{6,7},{7,6},{8,9},{9,8},{10,11... | collective-permute-start | bytes 12296 | tf_op jit(solution)/shard_map/ppermute | solution.py:23
  9.5 2.6 %collective-permute-start.1 = (f32[1,1536]{1,0:T(1,128)S(1)}, f32[1,1536]{1,0:T(1,128)S(1)}, u32[]{:S(2)}, u32[]{:S(2)}) collective-permute-start(f32[1,1536]{1,0:T(1,128)S(1)} %pad_maximum_fusion.7.pair_ref), channel_id=1, source_target_pairs={{0,2},{1,3},{2,0},{3,1},{4,6},{5,7},{6,4},{7,5},{8,10},{9,11},{10,... | collective-permute-start | bytes 18440 | tf_op jit(solution)/shard_map/ppermute | solution.py:23
  12.1 6.5 %collective-permute-start.25 = (bf16[1,2,1,512]{3,2,1,0:T(2,128)(2,1)S(1)}, bf16[1,2,1,512]{3,2,1,0:T(2,128)(2,1)S(1)}, u32[]{:S(2)}, u32[]{:S(2)}) collective-permute-start(bf16[1,2,1,512]{3,2,1,0:T(2,128)(2,1)S(1)} %constant_dynamic-update-slice_fusion), channel_id=1, source_target_pairs={{0,64},{4,68},{8,72},{12,76},{16,80},{20,84},{24,88},{28,92},{32,9... | collective-permute-start | bytes 6152 | tf_op jit(solution)/shard_map/ppermute | solution.py:23
  13.6 6.4 %collective-permute-start.26 = (bf16[1,2,1,512]{3,2,1,0:T(2,128)(2,1)S(1)}, bf16[1,2,1,512]{3,2,1,0:T(2,128)(2,1)S(1)}, u32[]{:S(2)}, u32[]{:S(2)}) collective-permute-start(bf16[1,2,1,512]{3,2,1,0:T(2,128)(2,1)S(1)} %constant_dynamic-update-slice_fusion), channel_id=1, source_target_pairs={{0,128},{4,132},{8,136},{12,140},{16,144},{20,148},{24,152},{28,15... | collective-permute-start | bytes 6152 | tf_op jit(solution)/shard_map/ppermute | solution.py:23
  18.6 4.6 %collective-permute-start.27 = (bf16[1,2,1,512]{3,2,1,0:T(2,128)(2,1)S(1)}, bf16[1,2,1,512]{3,2,1,0:T(2,128)(2,1)S(1)}, u32[]{:S(2)}, u32[]{:S(2)}) collective-permute-start(bf16[1,2,1,512]{3,2,1,0:T(2,128)(2,1)S(1)} %constant_dynamic-update-slice_fusion), channel_id=1, source_target_pairs={{0,192},{4,196},{8,200},{12,204},{16,208},{20,212},{24,216},{28,22... | collective-permute-start | bytes 6152 | tf_op jit(solution)/shard_map/ppermute | solution.py:23
  23.2 2.8 %collective-permute-start.28 = (bf16[4,2,1,512]{3,2,1,0:T(2,128)(2,1)S(1)}, bf16[4,2,1,512]{3,2,1,0:T(2,128)(2,1)S(1)}, u32[]{:S(2)}, u32[]{:S(2)}) collective-permute-start(bf16[4,2,1,512]{3,2,1,0:T(2,128)(2,1)S(1)} %pad_maximum_fusion.3), channel_id=1, source_target_pairs={{0,4},{4,0},{8,12},{12,8},{16,20},{20,16},{24,28},{28,24},{32,36},... | collective-permute-start | bytes 24584 | tf_op jit(solution)/shard_map/ppermute | solution.py:23
  26.2 4.2 %collective-permute-start.29 = (bf16[4,2,2,512]{3,2,1,0:T(2,128)(2,1)S(1)}, bf16[4,2,2,512]{3,2,1,0:T(2,128)(2,1)S(1)}, u32[]{:S(2)}, u32[]{:S(2)}) collective-permute-start(bf16[4,2,2,512]{3,2,1,0:T(2,128)(2,1)S(1)} %pad_maximum_fusion.4), channel_id=1, source_target_pairs={{0,8},{4,12},{8,0},{12,4},{16,24},{20,28},{24,16},{28,20},{32,40},... | collective-permute-start | bytes 49160 | tf_op jit(solution)/shard_map/ppermute | solution.py:23
  29.1 2.8 %collective-permute-start.12 = (f32[1,1024]{1,0:T(1,128)S(1)}, f32[1,1024]{1,0:T(1,128)S(1)}, u32[]{:S(2)}, u32[]{:S(2)}) collective-permute-start(f32[1,1024]{1,0:T(1,128)S(1)} %add.7.pair_ref), channel_id=1, source_target_pairs={{0,2},{1,3},{2,0},{3,1},{4,6},{5,7},{6,4},{7,5},{8,10},{9,11},{10,... | collective-permute-start | bytes 12296 | tf_op jit(solution)/shard_map/ppermute | solution.py:23
  30.5 9.6 %collective-permute-start.30 = (bf16[4,2,4,512]{3,2,1,0:T(4,128)(2,1)S(1)}, bf16[4,2,4,512]{3,2,1,0:T(4,128)(2,1)S(1)}, u32[]{:S(2)}, u32[]{:S(2)}) collective-permute-start(bf16[4,2,4,512]{3,2,1,0:T(4,128)(2,1)S(1)} %pad_maximum_fusion.2), channel_id=1, source_target_pairs={{0,16},{4,20},{8,24},{12,28},{16,0},{20,4},{24,8},{28,12},{32,48},... | collective-permute-start | bytes 98312 | tf_op jit(solution)/shard_map/ppermute | solution.py:23
  32.6 13.1 %collective-permute-start.19 = (bf16[1,64,1024]{2,1,0:T(8,128)(2,1)S(1)}, bf16[1,64,1024]{2,1,0:T(8,128)(2,1)S(1)}, u32[]{:S(2)}, u32[]{:S(2)}) collective-permute-start(bf16[1,64,1024]{2,1,0:T(8,128)(2,1)S(1)} %get-tuple-element.30.refs_2_), channel_id=1, source_target_pairs={{0,1},{1,0},{2,3},{3,2},{4,5},{5,4},{6,7},{7,6},{8,9},{9,8},{10,11... | collective-permute-start | bytes 393224 | tf_op jit(solution)/shard_map/ppermute | solution.py:23
  38.3 10.0 %collective-permute-start.13 = (bf16[1,64,1024]{2,1,0:T(8,128)(2,1)S(1)}, bf16[1,64,1024]{2,1,0:T(8,128)(2,1)S(1)}, u32[]{:S(2)}, u32[]{:S(2)}) collective-permute-start(bf16[1,64,1024]{2,1,0:T(8,128)(2,1)S(1)} %get-tuple-element.30.refs_2_), channel_id=1, source_target_pairs={{0,2},{1,3},{2,0},{3,1},{4,6},{5,7},{6,4},{7,5},{8,10},{9,11},{10,... | collective-permute-start | bytes 393224 | tf_op jit(solution)/shard_map/ppermute | solution.py:23
  39.1 8.5 %collective-permute-start.20 = (bf16[1,64,1024]{2,1,0:T(8,128)(2,1)S(1)}, bf16[1,64,1024]{2,1,0:T(8,128)(2,1)S(1)}, u32[]{:S(2)}, u32[]{:S(2)}) collective-permute-start(bf16[1,64,1024]{2,1,0:T(8,128)(2,1)S(1)} %get-tuple-element.31.refs_3_), channel_id=1, source_target_pairs={{0,1},{1,0},{2,3},{3,2},{4,5},{5,4},{6,7},{7,6},{8,9},{9,8},{10,11... | collective-permute-start | bytes 393224 | tf_op jit(solution)/shard_map/ppermute | solution.py:23
  39.4 9.7 %collective-permute-start.14 = (bf16[1,64,1024]{2,1,0:T(8,128)(2,1)S(1)}, bf16[1,64,1024]{2,1,0:T(8,128)(2,1)S(1)}, u32[]{:S(2)}, u32[]{:S(2)}) collective-permute-start(bf16[1,64,1024]{2,1,0:T(8,128)(2,1)S(1)} %get-tuple-element.31.refs_3_), channel_id=1, source_target_pairs={{0,2},{1,3},{2,0},{3,1},{4,6},{5,7},{6,4},{7,5},{8,10},{9,11},{10,... | collective-permute-start | bytes 393224 | tf_op jit(solution)/shard_map/ppermute | solution.py:23
  40.2 4.7 %collective-permute-start.31 = (bf16[4,2,8,512]{3,2,1,0:T(8,128)(2,1)S(1)}, bf16[4,2,8,512]{3,2,1,0:T(8,128)(2,1)S(1)}, u32[]{:S(2)}, u32[]{:S(2)}) collective-permute-start(bf16[4,2,8,512]{3,2,1,0:T(8,128)(2,1)S(1)} %pad_maximum_fusion.1), channel_id=1, source_target_pairs={{0,32},{4,36},{8,40},{12,44},{16,48},{20,52},{24,56},{28,60},{32,0... | collective-permute-start | bytes 196616 | tf_op jit(solution)/shard_map/ppermute | solution.py:23
  44.9 24.5 %collective-permute-start.22 = (bf16[1,128,1024]{2,1,0:T(8,128)(2,1)S(1)}, bf16[1,128,1024]{2,1,0:T(8,128)(2,1)S(1)}, u32[]{:S(2)}, u32[]{:S(2)}) collective-permute-start(bf16[1,128,1024]{2,1,0:T(8,128)(2,1)S(1)} %get-tuple-element.33.refs_1_), channel_id=1, source_target_pairs={{0,2},{1,3},{2,0},{3,1},{4,6},{5,7},{6,4},{7,5},{8,10},{9,11},{10,... | collective-permute-start | bytes 786440 | tf_op jit(solution)/shard_map/ppermute | solution.py:23
  45.6 24.5 %collective-permute-start.18 = (bf16[1,128,1024]{2,1,0:T(8,128)(2,1)S(1)}, bf16[1,128,1024]{2,1,0:T(8,128)(2,1)S(1)}, u32[]{:S(2)}, u32[]{:S(2)}) collective-permute-start(bf16[1,128,1024]{2,1,0:T(8,128)(2,1)S(1)} %get-tuple-element.33.refs_1_), channel_id=1, source_target_pairs={{0,1},{1,0},{2,3},{3,2},{4,5},{5,4},{6,7},{7,6},{8,9},{9,8},{10,11... | collective-permute-start | bytes 786440 | tf_op jit(solution)/shard_map/ppermute | solution.py:23
  47.6 23.1 %collective-permute-start.21 = (bf16[1,256,1024]{2,1,0:T(8,128)(2,1)S(1)}, bf16[1,256,1024]{2,1,0:T(8,128)(2,1)S(1)}, u32[]{:S(2)}, u32[]{:S(2)}) collective-permute-start(bf16[1,256,1024]{2,1,0:T(8,128)(2,1)S(1)} %get-tuple-element.32.refs_0_), channel_id=1, source_target_pairs={{0,2},{1,3},{2,0},{3,1},{4,6},{5,7},{6,4},{7,5},{8,10},{9,11},{10,... | collective-permute-start | bytes 1572872 | tf_op jit(solution)/shard_map/ppermute | solution.py:23
  48.3 16.8 %collective-permute-start.5 = (bf16[1,64,1024]{2,1,0:T(8,128)(2,1)S(1)}, bf16[1,64,1024]{2,1,0:T(8,128)(2,1)S(1)}, u32[]{:S(2)}, u32[]{:S(2)}) collective-permute-start(bf16[1,64,1024]{2,1,0:T(8,128)(2,1)S(1)} %shard_map.111.refs_0_), channel_id=1, source_target_pairs={{0,2},{1,3},{2,0},{3,1},{4,6},{5,7},{6,4},{7,5},{8,10},{9,11},{10,... | collective-permute-start | bytes 393224 | tf_op jit(solution)/shard_map/ppermute | solution.py:23
  49.1 19.3 %collective-permute-start.2 = (bf16[1,64,1024]{2,1,0:T(8,128)(2,1)S(1)}, bf16[1,64,1024]{2,1,0:T(8,128)(2,1)S(1)}, u32[]{:S(2)}, u32[]{:S(2)}) collective-permute-start(bf16[1,64,1024]{2,1,0:T(8,128)(2,1)S(1)} %shard_map.111.refs_0_), channel_id=1, source_target_pairs={{0,1},{1,0},{2,3},{3,2},{4,5},{5,4},{6,7},{7,6},{8,9},{9,8},{10,11... | collective-permute-start | bytes 393224 | tf_op jit(solution)/shard_map/ppermute | solution.py:23
  65.2 3.9 %collective-permute-start.32 = (bf16[4,2,16,512]{3,2,1,0:T(8,128)(2,1)S(1)}, bf16[4,2,16,512]{3,2,1,0:T(8,128)(2,1)S(1)}, u32[]{:S(2)}, u32[]{:S(2)}) collective-permute-start(bf16[4,2,16,512]{3,2,1,0:T(8,128)(2,1)S(1)} %pad_maximum_fusion.own_ref), channel_id=1, source_target_pairs={{0,1},{1,0},{2,3},{3,2},{4,5},{5,4},{6,7},{7,6},{8,9},{9,8},{10,11... | collective-permute-start | bytes 393224 | tf_op jit(solution)/shard_map/ppermute | solution.py:23
  68.4 22.8 %collective-permute-start.6 = (bf16[1,256,1024]{2,1,0:T(8,128)(2,1)S(1)}, bf16[1,256,1024]{2,1,0:T(8,128)(2,1)S(1)}, u32[]{:S(2)}, u32[]{:S(2)}) collective-permute-start(bf16[1,256,1024]{2,1,0:T(8,128)(2,1)S(1)} %get-tuple-element.26.refs_1_), channel_id=1, source_target_pairs={{0,2},{1,3},{2,0},{3,1},{4,6},{5,7},{6,4},{7,5},{8,10},{9,11},{10,... | collective-permute-start | bytes 1572872 | tf_op jit(solution)/shard_map/ppermute | solution.py:23
  69.1 1.5 %collective-permute-start.15 = (bf16[1,64,1024]{2,1,0:T(8,128)(2,1)S(1)}, bf16[1,64,1024]{2,1,0:T(8,128)(2,1)S(1)}, u32[]{:S(2)}, u32[]{:S(2)}) collective-permute-start(bf16[1,64,1024]{2,1,0:T(8,128)(2,1)S(1)} %collective-permute-done.13.refs_0_), channel_id=1, source_target_pairs={{0,1},{1,0},{2,3},{3,2},{4,5},{5,4},{6,7},{7,6},{8,9},{9,8},{10,11... | collective-permute-start | bytes 393224 | tf_op jit(solution)/shard_map/ppermute | solution.py:23
  69.4 20.9 %collective-permute-start.7 = (bf16[1,192,1024]{2,1,0:T(8,128)(2,1)S(1)}, bf16[1,192,1024]{2,1,0:T(8,128)(2,1)S(1)}, u32[]{:S(2)}, u32[]{:S(2)}) collective-permute-start(bf16[1,192,1024]{2,1,0:T(8,128)(2,1)S(1)} %get-tuple-element.27.refs_2_), channel_id=1, source_target_pairs={{0,2},{1,3},{2,0},{3,1},{4,6},{5,7},{6,4},{7,5},{8,10},{9,11},{10,... | collective-permute-start | bytes 1179656 | tf_op jit(solution)/shard_map/ppermute | solution.py:23
  70.1 21.5 %collective-permute-start.17 = (bf16[1,256,1024]{2,1,0:T(8,128)(2,1)S(1)}, bf16[1,256,1024]{2,1,0:T(8,128)(2,1)S(1)}, u32[]{:S(2)}, u32[]{:S(2)}) collective-permute-start(bf16[1,256,1024]{2,1,0:T(8,128)(2,1)S(1)} %get-tuple-element.32.refs_0_), channel_id=1, source_target_pairs={{0,1},{1,0},{2,3},{3,2},{4,5},{5,4},{6,7},{7,6},{8,9},{9,8},{10,11... | collective-permute-start | bytes 1572872 | tf_op jit(solution)/shard_map/ppermute | solution.py:23
  70.6 1.7 %collective-permute-start.16 = (bf16[1,64,1024]{2,1,0:T(8,128)(2,1)S(1)}, bf16[1,64,1024]{2,1,0:T(8,128)(2,1)S(1)}, u32[]{:S(2)}, u32[]{:S(2)}) collective-permute-start(bf16[1,64,1024]{2,1,0:T(8,128)(2,1)S(1)} %collective-permute-done.14.refs_1_), channel_id=1, source_target_pairs={{0,1},{1,0},{2,3},{3,2},{4,5},{5,4},{6,7},{7,6},{8,9},{9,8},{10,11... | collective-permute-start | bytes 393224 | tf_op jit(solution)/shard_map/ppermute | solution.py:23
  70.7 21.0 %collective-permute-start.23 = (bf16[1,256,1024]{2,1,0:T(8,128)(2,1)S(1)}, bf16[1,256,1024]{2,1,0:T(8,128)(2,1)S(1)}, u32[]{:S(2)}, u32[]{:S(2)}) collective-permute-start(bf16[1,256,1024]{2,1,0:T(8,128)(2,1)S(1)} %collective-permute-done.21.refs_8_), channel_id=1, source_target_pairs={{0,1},{1,0},{2,3},{3,2},{4,5},{5,4},{6,7},{7,6},{8,9},{9,8},{10,11... | collective-permute-start | bytes 1572872 | tf_op jit(solution)/shard_map/ppermute | solution.py:23
  72.3 18.8 %collective-permute-start.24 = (bf16[1,128,1024]{2,1,0:T(8,128)(2,1)S(1)}, bf16[1,128,1024]{2,1,0:T(8,128)(2,1)S(1)}, u32[]{:S(2)}, u32[]{:S(2)}) collective-permute-start(bf16[1,128,1024]{2,1,0:T(8,128)(2,1)S(1)} %collective-permute-done.22.refs_9_), channel_id=1, source_target_pairs={{0,1},{1,0},{2,3},{3,2},{4,5},{5,4},{6,7},{7,6},{8,9},{9,8},{10,11... | collective-permute-start | bytes 786440 | tf_op jit(solution)/shard_map/ppermute | solution.py:23
  90.3 5.4 %collective-permute-start.3 = (bf16[1,256,1024]{2,1,0:T(8,128)(2,1)S(1)}, bf16[1,256,1024]{2,1,0:T(8,128)(2,1)S(1)}, u32[]{:S(2)}, u32[]{:S(2)}) collective-permute-start(bf16[1,256,1024]{2,1,0:T(8,128)(2,1)S(1)} %get-tuple-element.26.refs_1_), channel_id=1, source_target_pairs={{0,1},{1,0},{2,3},{3,2},{4,5},{5,4},{6,7},{7,6},{8,9},{9,8},{10,11... | collective-permute-start | bytes 1572872 | tf_op jit(solution)/shard_map/ppermute | solution.py:23
  91.1 4.6 %collective-permute-start.9 = (bf16[1,256,1024]{2,1,0:T(8,128)(2,1)S(1)}, bf16[1,256,1024]{2,1,0:T(8,128)(2,1)S(1)}, u32[]{:S(2)}, u32[]{:S(2)}) collective-permute-start(bf16[1,256,1024]{2,1,0:T(8,128)(2,1)S(1)} %collective-permute-done.6.refs_7_), channel_id=1, source_target_pairs={{0,1},{1,0},{2,3},{3,2},{4,5},{5,4},{6,7},{7,6},{8,9},{9,8},{10,11... | collective-permute-start | bytes 1572872 | tf_op jit(solution)/shard_map/ppermute | solution.py:23
  91.1 4.5 %collective-permute-start.4 = (bf16[1,192,1024]{2,1,0:T(8,128)(2,1)S(1)}, bf16[1,192,1024]{2,1,0:T(8,128)(2,1)S(1)}, u32[]{:S(2)}, u32[]{:S(2)}) collective-permute-start(bf16[1,192,1024]{2,1,0:T(8,128)(2,1)S(1)} %get-tuple-element.27.refs_2_), channel_id=1, source_target_pairs={{0,1},{1,0},{2,3},{3,2},{4,5},{5,4},{6,7},{7,6},{8,9},{9,8},{10,11... | collective-permute-start | bytes 1179656 | tf_op jit(solution)/shard_map/ppermute | solution.py:23
  91.6 4.0 %collective-permute-start.10 = (bf16[1,192,1024]{2,1,0:T(8,128)(2,1)S(1)}, bf16[1,192,1024]{2,1,0:T(8,128)(2,1)S(1)}, u32[]{:S(2)}, u32[]{:S(2)}) collective-permute-start(bf16[1,192,1024]{2,1,0:T(8,128)(2,1)S(1)} %collective-permute-done.7.refs_8_), channel_id=1, source_target_pairs={{0,1},{1,0},{2,3},{3,2},{4,5},{5,4},{6,7},{7,6},{8,9},{9,8},{10,11... | collective-permute-start | bytes 1179656 | tf_op jit(solution)/shard_map/ppermute | solution.py:23
  91.7 3.9 %collective-permute-start.8 = (bf16[1,64,1024]{2,1,0:T(8,128)(2,1)S(1)}, bf16[1,64,1024]{2,1,0:T(8,128)(2,1)S(1)}, u32[]{:S(2)}, u32[]{:S(2)}) collective-permute-start(bf16[1,64,1024]{2,1,0:T(8,128)(2,1)S(1)} %collective-permute-done.5.refs_6_), channel_id=1, source_target_pairs={{0,1},{1,0},{2,3},{3,2},{4,5},{5,4},{6,7},{7,6},{8,9},{9,8},{10,11... | collective-permute-start | bytes 393224 | tf_op jit(solution)/shard_map/ppermute | solution.py:23
where the time goes:
time: 98.1 us; the launch traced here: 98 us
  waiting for transfers between devices  45 us (46%)
  starting transfers between devices  38.9 us (40%)
  Pallas kernels  11.7 us (12%)
  between operations  1.71 us (2%)
    ppermute x33, waiting for transfers between devices, swap(): return lax.ppermute(x, axis, [(i, i ^ mask) for i in range(n)])  45 us
    ppermute x33, starting transfers between devices, swap(): return lax.ppermute(x, axis, [(i, i ^ mask) for i in range(n)])  38.9 us
    pallas_call x3, Pallas kernels, place(): call(functools.partial(place_body, places), jax.ShapeDtypeStruct(shape, b...  4.87 us
    pallas_call x2, Pallas kernels, mean_of(): call(mean_body, (pltpu.VMEM((rows, columns), jnp.float32), pltpu.VMEM((1,...  4.66 us
  transfers between devices with their start and end apart: 33, of which 9 were waited for; matrix products, arithmetic and copies ran while one was open for 1% of the time, Pallas kernels for 7%

commit v1 on v0

--- a/solution.py
+++ b/solution.py
@@ -9,13 +9,13 @@
 
 
 CORE, CHIP = 1, 2
-GATE = (64, 256, 192)
+GATE = (256, 256)
 UP = (256, 128, 64, 64)
 LOADS = 8
 MIB = 1 << 20
 VMEM = pl.BlockSpec(memory_space=pltpu.VMEM)
+SMEM = pl.BlockSpec(memory_space=pltpu.SMEM)
 HBM = pl.BlockSpec(memory_space=pltpu.HBM)
-SMEM = pl.BlockSpec(memory_space=pltpu.SMEM)
 
 
 def swap(x, axis, mask):
@@ -155,7 +155,7 @@
     return {0: own, CORE: cores, CHIP: chips, CORE | CHIP: boths}
 
 
-BITS = (("shard", CHIP), ("expert", 16), ("expert", 32), ("expert", 1), ("expert", 2), ("expert", 4), ("expert", 8))
+BITS = (("shard", CHIP), ("expert", 1), ("expert", 2), ("expert", 4), ("expert", 8))
 
 
 def lows_body(*outs):
@@ -193,13 +193,27 @@
                 out_ref[pl.ds(k * plane, plane), pl.ds(at, rows)] = value
 
 
+def planes_body(*refs):
+    z = lax.axis_index("expert") // 16
+    for k, ref in enumerate(refs[:-1]):
+        refs[-1][z ^ k] = ref[0]
+
+
 def router_of(lows, own, other):
     x = in_order(lows["shard", CHIP], own[None, None], other[None, None], 1)
-    z1, z2, z3 = (swap(x, "expert", 16 * k) for k in (1, 2, 3))
-    bit = lows["expert", 16]
-    x = in_order(lows["expert", 32], in_order(bit, x, z1, 0), in_order(bit, z2, z3, 0), 0)
-    for mask in (1, 2, 4, 8):
-        x = in_order(lows["expert", mask], x, swap(x, "expert", mask), 2)
+    pieces = (x, *(swap(x, "expert", 16 * k) for k in (1, 2, 3)))
+    x = call(
+        planes_body,
+        jax.ShapeDtypeStruct((4, *x.shape[1:]), x.dtype),
+        [VMEM] * 4,
+        1,
+        1 << 10,
+        out_specs=VMEM,
+    )(*pieces)
+    for unit in (1, 4):
+        a, b, c = (swap(x, "expert", unit * k) for k in (1, 2, 3))
+        low = lows["expert", unit]
+        x = in_order(lows["expert", 2 * unit], in_order(low, x, a, 2), in_order(low, b, c, 2), 2)
     other = swap(x, "shard", CORE)
     z, chips, plane, rows = x.shape
     return call(

time: 98.1 us -> 96.2 us (0.981)
  waiting for transfers between devices: 45 us -> 40.4 us
  starting transfers between devices: 38.9 us -> 41.8 us
    ppermute x33 -> x32, waiting for transfers between devices: 45 us -> 40.4 us  [swap(): return lax.ppermute(x, axis, [(i, i ^ mask) for i in range(n)])]
    ppermute x33 -> x32, starting transfers between devices: 38.9 us -> 41.8 us  [swap(): return lax.ppermute(x, axis, [(i, i ^ mask) for i in range(n)])]
  transfers between devices with their start and end apart: 33 -> 32, of which waited for: 9 -> 11; matrix products, arithmetic and copies ran while one was open for 1% -> 1% of each run, Pallas kernels for 7% -> 8%
where the time goes in v1:
time: 96.2 us; the launch traced here: 96.1 us
  starting transfers between devices  41.8 us (43%)
  waiting for transfers between devices  40.4 us (42%)
  Pallas kernels  11.7 us (12%)
  between operations  1.69 us (2%)
    ppermute x32, starting transfers between devices, swap(): return lax.ppermute(x, axis, [(i, i ^ mask) for i in range(n)])  41.8 us
    ppermute x32, waiting for transfers between devices, swap(): return lax.ppermute(x, axis, [(i, i ^ mask) for i in range(n)])  40.4 us
    pallas_call x3, Pallas kernels, place(): call(functools.partial(place_body, places), jax.ShapeDtypeStruct(shape, b...  4.84 us
    pallas_call x2, Pallas kernels, mean_of(): call(mean_body, (pltpu.VMEM((rows, columns), jnp.float32), pltpu.VMEM((1,...  4.66 us
  transfers between devices with their start and end apart: 32, of which 11 were waited for; matrix products, arithmetic and copies ran while one was open for 1% of the time, Pallas kernels for 8%

profile of v1, /device:TPU:1, one launch (start us, length us, event | category | flops | bytes accessed | tf_op | source)
XLA Modules:
  0.0 96.1 jit_solution(11940197745480820791)
XLA Ops:
  1.3 2.3 %shard_map.110 = (f32[512,1024]{1,0:T(8,128)S(1)}, f32[1,1024]{1,0:T(1,128)S(1)}) custom-call(f32[1]{0:T(128)S(6)} %copy.15.share_ref, f32[1,512,1024]{2,1,0:T(8,128)} %w_ref.2, f32[1,512,1024]{2,1,0:T(8,128)} %avg_ref.2), custom_call_target="tpu_custom_call" | custom-call | flops 4194304 | bytes 4194304 | tf_op jit(solution)/shard_map/pallas_call | solution.py:70
  3.6 3.3 %collective-permute-start = (f32[1,1024]{1,0:T(1,128)S(1)}, f32[1,1024]{1,0:T(1,128)S(1)}, u32[]{:S(2)}, u32[]{:S(2)}) collective-permute-start(f32[1,1024]{1,0:T(1,128)S(1)} %get-tuple-element.22), channel_id=1, source_target_pairs={{0,1},{1,0},{2,3},{3,2},{4,5},{5,4},{6,7},{7,6},{8,9},{9,8},{10,11... | collective-permute-start | bytes 12296 | tf_op jit(solution)/shard_map/ppermute | solution.py:23
  6.9 2.3 %shard_map.114 = (f32[512,1024]{1,0:T(8,128)S(1)}, f32[1,1024]{1,0:T(1,128)S(1)}) custom-call(f32[1]{0:T(128)S(6)} %copy.15.share_ref, f32[1,512,1024]{2,1,0:T(8,128)} %w_ref.3, f32[1,512,1024]{2,1,0:T(8,128)} %avg_ref.3), custom_call_target="tpu_custom_call" | custom-call | flops 4194304 | bytes 4194304 | tf_op jit(solution)/shard_map/pallas_call | solution.py:70
  9.3 0.1 collective-permute-start.8
  9.5 0.1 collective-permute-start.1
  9.6 2.4 %collective-permute-done.1.other_ref = f32[1,1536]{1,0:T(1,128)S(1)} collective-permute-done((f32[1,1536]{1,0:T(1,128)S(1)}, f32[1,1536]{1,0:T(1,128)S(1)}, u32[]{:S(2)}, u32[]{:S(2)}) %collective-permute-start.1) | collective-permute-done | bytes 6176 | tf_op jit(solution)/shard_map/ppermute | solution.py:23
  12.1 1.5 %collective-permute-start.22 = (bf16[1,2,1,512]{3,2,1,0:T(2,128)(2,1)S(1)}, bf16[1,2,1,512]{3,2,1,0:T(2,128)(2,1)S(1)}, u32[]{:S(2)}, u32[]{:S(2)}) collective-permute-start(bf16[1,2,1,512]{3,2,1,0:T(2,128)(2,1)S(1)} %constant_dynamic-update-slice_fusion.refs_0_), channel_id=1, source_target_pairs={{0,64},{4,68},{8,72},{12,76},{16,80},{20,84},{24,88},{28,92},{32,9... | collective-permute-start | bytes 6152 | tf_op jit(solution)/shard_map/ppermute | solution.py:23
  13.6 4.9 %collective-permute-start.23 = (bf16[1,2,1,512]{3,2,1,0:T(2,128)(2,1)S(1)}, bf16[1,2,1,512]{3,2,1,0:T(2,128)(2,1)S(1)}, u32[]{:S(2)}, u32[]{:S(2)}) collective-permute-start(bf16[1,2,1,512]{3,2,1,0:T(2,128)(2,1)S(1)} %constant_dynamic-update-slice_fusion.refs_0_), channel_id=1, source_target_pairs={{0,128},{4,132},{8,136},{12,140},{16,144},{20,148},{24,152},{28,15... | collective-permute-start | bytes 6152 | tf_op jit(solution)/shard_map/ppermute | solution.py:23
  18.6 1.4 %collective-permute-done.23.refs_2_ = bf16[1,2,1,512]{3,2,1,0:T(2,128)(2,1)S(1)} collective-permute-done((bf16[1,2,1,512]{3,2,1,0:T(2,128)(2,1)S(1)}, bf16[1,2,1,512]{3,2,1,0:T(2,128)(2,1)S(1)}, u32[]{:S(2)}, u32[]{:S(2)}) %collective-permute-start.23) | collective-permute-done | bytes 2080 | tf_op jit(solution)/shard_map/ppermute | solution.py:23
  20.0 3.1 %collective-permute-done.24.refs_3_ = bf16[1,2,1,512]{3,2,1,0:T(2,128)(2,1)S(1)} collective-permute-done((bf16[1,2,1,512]{3,2,1,0:T(2,128)(2,1)S(1)}, bf16[1,2,1,512]{3,2,1,0:T(2,128)(2,1)S(1)}, u32[]{:S(2)}, u32[]{:S(2)}) %collective-permute-start.24) | collective-permute-done | bytes 2080 | tf_op jit(solution)/shard_map/ppermute | solution.py:23
  23.2 1.3 %collective-permute-start.25 = (bf16[4,2,1,512]{3,2,1,0:T(2,128)(2,1)S(1)}, bf16[4,2,1,512]{3,2,1,0:T(2,128)(2,1)S(1)}, u32[]{:S(2)}, u32[]{:S(2)}) collective-permute-start(bf16[4,2,1,512]{3,2,1,0:T(2,128)(2,1)S(1)} %shard_map.119), channel_id=1, source_target_pairs={{0,4},{4,0},{8,12},{12,8},{16,20},{20,16},{24,28},{28,24},{32,36},... | collective-permute-start | bytes 24584 | tf_op jit(solution)/shard_map/ppermute | solution.py:23
  24.5 2.5 %collective-permute-start.26 = (bf16[4,2,1,512]{3,2,1,0:T(2,128)(2,1)S(1)}, bf16[4,2,1,512]{3,2,1,0:T(2,128)(2,1)S(1)}, u32[]{:S(2)}, u32[]{:S(2)}) collective-permute-start(bf16[4,2,1,512]{3,2,1,0:T(2,128)(2,1)S(1)} %shard_map.119), channel_id=1, source_target_pairs={{0,8},{4,12},{8,0},{12,4},{16,24},{20,28},{24,16},{28,20},{32,40},... | collective-permute-start | bytes 24584 | tf_op jit(solution)/shard_map/ppermute | solution.py:23
  26.9 0.2 collective-permute-start.27
  27.1 1.1 %collective-permute-start.9 = (f32[1,1024]{1,0:T(1,128)S(1)}, f32[1,1024]{1,0:T(1,128)S(1)}, u32[]{:S(2)}, u32[]{:S(2)}) collective-permute-start(f32[1,1024]{1,0:T(1,128)S(1)} %add.7.pair_ref), channel_id=1, source_target_pairs={{0,2},{1,3},{2,0},{3,1},{4,6},{5,7},{6,4},{7,5},{8,10},{9,11},{10,... | collective-permute-start | bytes 12296 | tf_op jit(solution)/shard_map/ppermute | solution.py:23
  28.2 0.3 collective-permute-done.26
  28.5 2.2 %collective-permute-done.27 = bf16[4,2,1,512]{3,2,1,0:T(2,128)(2,1)S(1)} collective-permute-done((bf16[4,2,1,512]{3,2,1,0:T(2,128)(2,1)S(1)}, bf16[4,2,1,512]{3,2,1,0:T(2,128)(2,1)S(1)}, u32[]{:S(2)}, u32[]{:S(2)}) %collective-permute-start.27) | collective-permute-done | bytes 8224 | tf_op jit(solution)/shard_map/ppermute | solution.py:23
  30.8 0.1 broadcast_select_fusion.7
  30.9 1.4 %collective-permute-start.28 = (bf16[4,2,4,512]{3,2,1,0:T(4,128)(2,1)S(1)}, bf16[4,2,4,512]{3,2,1,0:T(4,128)(2,1)S(1)}, u32[]{:S(2)}, u32[]{:S(2)}) collective-permute-start(bf16[4,2,4,512]{3,2,1,0:T(4,128)(2,1)S(1)} %pad_maximum_fusion.3), channel_id=1, source_target_pairs={{0,16},{4,20},{8,24},{12,28},{16,0},{20,4},{24,8},{28,12},{32,48},... | collective-permute-start | bytes 98312 | tf_op jit(solution)/shard_map/ppermute | solution.py:23
  32.3 2.6 %collective-permute-start.29 = (bf16[4,2,4,512]{3,2,1,0:T(4,128)(2,1)S(1)}, bf16[4,2,4,512]{3,2,1,0:T(4,128)(2,1)S(1)}, u32[]{:S(2)}, u32[]{:S(2)}) collective-permute-start(bf16[4,2,4,512]{3,2,1,0:T(4,128)(2,1)S(1)} %pad_maximum_fusion.3), channel_id=1, source_target_pairs={{0,32},{4,36},{8,40},{12,44},{16,48},{20,52},{24,56},{28,60},{32,0... | collective-permute-start | bytes 98312 | tf_op jit(solution)/shard_map/ppermute | solution.py:23
  35.0 0.7 shard_map.115
  35.7 1.0 %collective-permute-start.19 = (bf16[1,128,1024]{2,1,0:T(8,128)(2,1)S(1)}, bf16[1,128,1024]{2,1,0:T(8,128)(2,1)S(1)}, u32[]{:S(2)}, u32[]{:S(2)}) collective-permute-start(bf16[1,128,1024]{2,1,0:T(8,128)(2,1)S(1)} %get-tuple-element.29.refs_1_), channel_id=1, source_target_pairs={{0,2},{1,3},{2,0},{3,1},{4,6},{5,7},{6,4},{7,5},{8,10},{9,11},{10,... | collective-permute-start | bytes 786440 | tf_op jit(solution)/shard_map/ppermute | solution.py:23
  36.6 5.9 %collective-permute-start.15 = (bf16[1,128,1024]{2,1,0:T(8,128)(2,1)S(1)}, bf16[1,128,1024]{2,1,0:T(8,128)(2,1)S(1)}, u32[]{:S(2)}, u32[]{:S(2)}) collective-permute-start(bf16[1,128,1024]{2,1,0:T(8,128)(2,1)S(1)} %get-tuple-element.29.refs_1_), channel_id=1, source_target_pairs={{0,1},{1,0},{2,3},{3,2},{4,5},{5,4},{6,7},{7,6},{8,9},{9,8},{10,11... | collective-permute-start | bytes 786440 | tf_op jit(solution)/shard_map/ppermute | solution.py:23
  42.5 0.8 collective-permute-start.10
  43.3 2.3 %collective-permute-start.17 = (bf16[1,64,1024]{2,1,0:T(8,128)(2,1)S(1)}, bf16[1,64,1024]{2,1,0:T(8,128)(2,1)S(1)}, u32[]{:S(2)}, u32[]{:S(2)}) collective-permute-start(bf16[1,64,1024]{2,1,0:T(8,128)(2,1)S(1)} %get-tuple-element.27.refs_3_), channel_id=1, source_target_pairs={{0,1},{1,0},{2,3},{3,2},{4,5},{5,4},{6,7},{7,6},{8,9},{9,8},{10,11... | collective-permute-start | bytes 393224 | tf_op jit(solution)/shard_map/ppermute | solution.py:23
  45.9 1.0 %collective-permute-start.18 = (bf16[1,256,1024]{2,1,0:T(8,128)(2,1)S(1)}, bf16[1,256,1024]{2,1,0:T(8,128)(2,1)S(1)}, u32[]{:S(2)}, u32[]{:S(2)}) collective-permute-start(bf16[1,256,1024]{2,1,0:T(8,128)(2,1)S(1)} %get-tuple-element.28.refs_0_), channel_id=1, source_target_pairs={{0,2},{1,3},{2,0},{3,1},{4,6},{5,7},{6,4},{7,5},{8,10},{9,11},{10,... | collective-permute-start | bytes 1572872 | tf_op jit(solution)/shard_map/ppermute | solution.py:23
  46.9 0.7 collective-permute-start.11
  47.6 0.5 collective-permute-done.10.refs_0_
  48.1 4.0 %collective-permute-start.31 = (bf16[4,2,16,512]{3,2,1,0:T(8,128)(2,1)S(1)}, bf16[4,2,16,512]{3,2,1,0:T(8,128)(2,1)S(1)}, u32[]{:S(2)}, u32[]{:S(2)}) collective-permute-start(bf16[4,2,16,512]{3,2,1,0:T(8,128)(2,1)S(1)} %pad_maximum_fusion.own_ref), channel_id=1, source_target_pairs={{0,1},{1,0},{2,3},{3,2},{4,5},{5,4},{6,7},{7,6},{8,9},{9,8},{10,11... | collective-permute-start | bytes 393224 | tf_op jit(solution)/shard_map/ppermute | solution.py:23
  52.1 0.6 shard_map.112
  52.8 10.1 %collective-permute-done.11.refs_1_ = bf16[1,64,1024]{2,1,0:T(8,128)(2,1)S(1)} collective-permute-done((bf16[1,64,1024]{2,1,0:T(8,128)(2,1)S(1)}, bf16[1,64,1024]{2,1,0:T(8,128)(2,1)S(1)}, u32[]{:S(2)}, u32[]{:S(2)}) %collective-permute-start.11) | collective-permute-done | bytes 131104 | tf_op jit(solution)/shard_map/ppermute | solution.py:23
  62.9 1.8 %collective-permute-start.14 = (bf16[1,256,1024]{2,1,0:T(8,128)(2,1)S(1)}, bf16[1,256,1024]{2,1,0:T(8,128)(2,1)S(1)}, u32[]{:S(2)}, u32[]{:S(2)}) collective-permute-start(bf16[1,256,1024]{2,1,0:T(8,128)(2,1)S(1)} %get-tuple-element.28.refs_0_), channel_id=1, source_target_pairs={{0,1},{1,0},{2,3},{3,2},{4,5},{5,4},{6,7},{7,6},{8,9},{9,8},{10,11... | collective-permute-start | bytes 1572872 | tf_op jit(solution)/shard_map/ppermute | solution.py:23
  64.7 0.7 collective-permute-start.5
  65.5 0.7 collective-permute-start.4
  66.2 0.6 collective-permute-start.12
  66.8 1.0 %collective-permute-done.12.refs_2_ = bf16[1,64,1024]{2,1,0:T(8,128)(2,1)S(1)} collective-permute-done((bf16[1,64,1024]{2,1,0:T(8,128)(2,1)S(1)}, bf16[1,64,1024]{2,1,0:T(8,128)(2,1)S(1)}, u32[]{:S(2)}, u32[]{:S(2)}) %collective-permute-start.12) | collective-permute-done | bytes 131104 | tf_op jit(solution)/shard_map/ppermute | solution.py:23
  67.7 0.4 collective-permute-start.21
  68.1 0.1 collective-permute-start.20
  68.3 1.0 %collective-permute-done.21.refs_11_ = bf16[1,128,1024]{2,1,0:T(8,128)(2,1)S(1)} collective-permute-done((bf16[1,128,1024]{2,1,0:T(8,128)(2,1)S(1)}, bf16[1,128,1024]{2,1,0:T(8,128)(2,1)S(1)}, u32[]{:S(2)}, u32[]{:S(2)}) %collective-permute-start.21) | collective-permute-done | bytes 262176 | tf_op jit(solution)/shard_map/ppermute | solution.py:23
  69.3 0.4 collective-permute-start.3
  69.6 0.1 collective-permute-start.2
  69.8 8.4 %collective-permute-done.5.refs_5_ = bf16[1,256,1024]{2,1,0:T(8,128)(2,1)S(1)} collective-permute-done((bf16[1,256,1024]{2,1,0:T(8,128)(2,1)S(1)}, bf16[1,256,1024]{2,1,0:T(8,128)(2,1)S(1)}, u32[]{:S(2)}, u32[]{:S(2)}) %collective-permute-start.5) | collective-permute-done | bytes 524320 | tf_op jit(solution)/shard_map/ppermute | solution.py:23
  78.2 1.3 %collective-permute-start.7 = (bf16[1,256,1024]{2,1,0:T(8,128)(2,1)S(1)}, bf16[1,256,1024]{2,1,0:T(8,128)(2,1)S(1)}, u32[]{:S(2)}, u32[]{:S(2)}) collective-permute-start(bf16[1,256,1024]{2,1,0:T(8,128)(2,1)S(1)} %collective-permute-done.5.refs_5_), channel_id=1, source_target_pairs={{0,1},{1,0},{2,3},{3,2},{4,5},{5,4},{6,7},{7,6},{8,9},{9,8},{10,11... | collective-permute-start | bytes 1572872 | tf_op jit(solution)/shard_map/ppermute | solution.py:23
  79.5 9.9 %collective-permute-done.4.refs_4_ = bf16[1,256,1024]{2,1,0:T(8,128)(2,1)S(1)} collective-permute-done((bf16[1,256,1024]{2,1,0:T(8,128)(2,1)S(1)}, bf16[1,256,1024]{2,1,0:T(8,128)(2,1)S(1)}, u32[]{:S(2)}, u32[]{:S(2)}) %collective-permute-start.4) | collective-permute-done | bytes 524320 | tf_op jit(solution)/shard_map/ppermute | solution.py:23
  89.4 0.9 collective-permute-start.6
  90.3 0.7 shard_map.120
  91.0 1.9 %shard_map.116.refs_4_ = bf16[1,2048,1024]{2,1,0:T(8,128)(2,1)} custom-call(bf16[1,256,1024]{2,1,0:T(8,128)(2,1)S(1)} %get-tuple-element.28.refs_0_, bf16[1,128,1024]{2,1,0:T(8,128)(2,1)S(1)} %get-tuple-element.29.refs_1_, bf16[1,64,1024]{2,1,0:T(8,128)(2,1)S(1)} %get-tuple-element.26.refs_2_, bf16[1,64,1024]{2,1,0:T(8,128)(2,1)S(1)} %get-tuple-element.27.refs_3_, ...), custom_call_target="tpu_custom_call" | custom-call | flops 1048576 | bytes 4194304 | tf_op jit(solution)/shard_map/pallas_call | solution.py:131
  93.0 0.8 shard_map.117
  93.8 2.1 %shard_map.113 = bf16[1,2048,1024]{2,1,0:T(8,128)(2,1)} custom-call(bf16[1,256,1024]{2,1,0:T(8,128)(2,1)S(1)} %shard_map.111.refs_0_, bf16[1,256,1024]{2,1,0:T(8,128)(2,1)S(1)} %get-tuple-element.23.refs_1_, bf16[1,256,1024]{2,1,0:T(8,128)(2,1)S(1)} %collective-permute-done.2.refs_2_, bf16[1,256,1024]{2,1,0:T(8,128)(2,1)S(1)} %collective-permute-done.3.refs_3_, ...), custom_call_target="tpu_custom_call" | custom-call | flops 1048576 | bytes 4194304 | tf_op jit(solution)/shard_map/pallas_call | solution.py:131
  (49 shorter events, 0.6 us)
Async XLA Ops:
  3.6 5.8 %copy-start = (f32[512,1]{0,1:T(1,128)S(1)}, f32[512,1]{0,1:T(1,128)}, u32[]{:S(2)}) copy-start(f32[512,1]{0,1:T(1,128)} %param.12) | copy-start | bytes 6148
  3.6 5.7 %copy-start.1 = (f32[512]{0:T(512)S(1)}, f32[512]{0:T(512)}, u32[]{:S(2)}) copy-start(f32[512]{0:T(512)} %param.13) | copy-start | bytes 6148
  3.6 5.8 %collective-permute-start = (f32[1,1024]{1,0:T(1,128)S(1)}, f32[1,1024]{1,0:T(1,128)S(1)}, u32[]{:S(2)}, u32[]{:S(2)}) collective-permute-start(f32[1,1024]{1,0:T(1,128)S(1)} %get-tuple-element.22), channel_id=1, source_target_pairs={{0,1},{1,0},{2,3},{3,2},{4,5},{5,4},{6,7},{7,6},{8,9},{9,8},{10,11... | collective-permute-start | bytes 12296 | tf_op jit(solution)/shard_map/ppermute | solution.py:23
  9.3 17.9 %collective-permute-start.8 = (f32[1,1024]{1,0:T(1,128)S(1)}, f32[1,1024]{1,0:T(1,128)S(1)}, u32[]{:S(2)}, u32[]{:S(2)}) collective-permute-start(f32[1,1024]{1,0:T(1,128)S(1)} %get-tuple-element.25), channel_id=1, source_target_pairs={{0,1},{1,0},{2,3},{3,2},{4,5},{5,4},{6,7},{7,6},{8,9},{9,8},{10,11... | collective-permute-start | bytes 12296 | tf_op jit(solution)/shard_map/ppermute | solution.py:23
  9.5 2.6 %collective-permute-start.1 = (f32[1,1536]{1,0:T(1,128)S(1)}, f32[1,1536]{1,0:T(1,128)S(1)}, u32[]{:S(2)}, u32[]{:S(2)}) collective-permute-start(f32[1,1536]{1,0:T(1,128)S(1)} %pad_maximum_fusion.6.pair_ref), channel_id=1, source_target_pairs={{0,2},{1,3},{2,0},{3,1},{4,6},{5,7},{6,4},{7,5},{8,10},{9,11},{10,... | collective-permute-start | bytes 18440 | tf_op jit(solution)/shard_map/ppermute | solution.py:23
  12.1 6.5 %collective-permute-start.22 = (bf16[1,2,1,512]{3,2,1,0:T(2,128)(2,1)S(1)}, bf16[1,2,1,512]{3,2,1,0:T(2,128)(2,1)S(1)}, u32[]{:S(2)}, u32[]{:S(2)}) collective-permute-start(bf16[1,2,1,512]{3,2,1,0:T(2,128)(2,1)S(1)} %constant_dynamic-update-slice_fusion.refs_0_), channel_id=1, source_target_pairs={{0,64},{4,68},{8,72},{12,76},{16,80},{20,84},{24,88},{28,92},{32,9... | collective-permute-start | bytes 6152 | tf_op jit(solution)/shard_map/ppermute | solution.py:23
  13.6 6.4 %collective-permute-start.23 = (bf16[1,2,1,512]{3,2,1,0:T(2,128)(2,1)S(1)}, bf16[1,2,1,512]{3,2,1,0:T(2,128)(2,1)S(1)}, u32[]{:S(2)}, u32[]{:S(2)}) collective-permute-start(bf16[1,2,1,512]{3,2,1,0:T(2,128)(2,1)S(1)} %constant_dynamic-update-slice_fusion.refs_0_), channel_id=1, source_target_pairs={{0,128},{4,132},{8,136},{12,140},{16,144},{20,148},{24,152},{28,15... | collective-permute-start | bytes 6152 | tf_op jit(solution)/shard_map/ppermute | solution.py:23
  18.6 4.6 %collective-permute-start.24 = (bf16[1,2,1,512]{3,2,1,0:T(2,128)(2,1)S(1)}, bf16[1,2,1,512]{3,2,1,0:T(2,128)(2,1)S(1)}, u32[]{:S(2)}, u32[]{:S(2)}) collective-permute-start(bf16[1,2,1,512]{3,2,1,0:T(2,128)(2,1)S(1)} %constant_dynamic-update-slice_fusion.refs_0_), channel_id=1, source_target_pairs={{0,192},{4,196},{8,200},{12,204},{16,208},{20,212},{24,216},{28,22... | collective-permute-start | bytes 6152 | tf_op jit(solution)/shard_map/ppermute | solution.py:23
  23.2 5.1 %collective-permute-start.25 = (bf16[4,2,1,512]{3,2,1,0:T(2,128)(2,1)S(1)}, bf16[4,2,1,512]{3,2,1,0:T(2,128)(2,1)S(1)}, u32[]{:S(2)}, u32[]{:S(2)}) collective-permute-start(bf16[4,2,1,512]{3,2,1,0:T(2,128)(2,1)S(1)} %shard_map.119), channel_id=1, source_target_pairs={{0,4},{4,0},{8,12},{12,8},{16,20},{20,16},{24,28},{28,24},{32,36},... | collective-permute-start | bytes 24584 | tf_op jit(solution)/shard_map/ppermute | solution.py:23
  24.5 4.1 %collective-permute-start.26 = (bf16[4,2,1,512]{3,2,1,0:T(2,128)(2,1)S(1)}, bf16[4,2,1,512]{3,2,1,0:T(2,128)(2,1)S(1)}, u32[]{:S(2)}, u32[]{:S(2)}) collective-permute-start(bf16[4,2,1,512]{3,2,1,0:T(2,128)(2,1)S(1)} %shard_map.119), channel_id=1, source_target_pairs={{0,8},{4,12},{8,0},{12,4},{16,24},{20,28},{24,16},{28,20},{32,40},... | collective-permute-start | bytes 24584 | tf_op jit(solution)/shard_map/ppermute | solution.py:23
  26.9 3.8 %collective-permute-start.27 = (bf16[4,2,1,512]{3,2,1,0:T(2,128)(2,1)S(1)}, bf16[4,2,1,512]{3,2,1,0:T(2,128)(2,1)S(1)}, u32[]{:S(2)}, u32[]{:S(2)}) collective-permute-start(bf16[4,2,1,512]{3,2,1,0:T(2,128)(2,1)S(1)} %shard_map.119), channel_id=1, source_target_pairs={{0,12},{4,8},{8,4},{12,0},{16,28},{20,24},{24,20},{28,16},{32,44},... | collective-permute-start | bytes 24584 | tf_op jit(solution)/shard_map/ppermute | solution.py:23
  27.1 7.8 %collective-permute-start.9 = (f32[1,1024]{1,0:T(1,128)S(1)}, f32[1,1024]{1,0:T(1,128)S(1)}, u32[]{:S(2)}, u32[]{:S(2)}) collective-permute-start(f32[1,1024]{1,0:T(1,128)S(1)} %add.7.pair_ref), channel_id=1, source_target_pairs={{0,2},{1,3},{2,0},{3,1},{4,6},{5,7},{6,4},{7,5},{8,10},{9,11},{10,... | collective-permute-start | bytes 12296 | tf_op jit(solution)/shard_map/ppermute | solution.py:23
  30.9 11.6 %collective-permute-start.28 = (bf16[4,2,4,512]{3,2,1,0:T(4,128)(2,1)S(1)}, bf16[4,2,4,512]{3,2,1,0:T(4,128)(2,1)S(1)}, u32[]{:S(2)}, u32[]{:S(2)}) collective-permute-start(bf16[4,2,4,512]{3,2,1,0:T(4,128)(2,1)S(1)} %pad_maximum_fusion.3), channel_id=1, source_target_pairs={{0,16},{4,20},{8,24},{12,28},{16,0},{20,4},{24,8},{28,12},{32,48},... | collective-permute-start | bytes 98312 | tf_op jit(solution)/shard_map/ppermute | solution.py:23
  32.3 10.2 %collective-permute-start.29 = (bf16[4,2,4,512]{3,2,1,0:T(4,128)(2,1)S(1)}, bf16[4,2,4,512]{3,2,1,0:T(4,128)(2,1)S(1)}, u32[]{:S(2)}, u32[]{:S(2)}) collective-permute-start(bf16[4,2,4,512]{3,2,1,0:T(4,128)(2,1)S(1)} %pad_maximum_fusion.3), channel_id=1, source_target_pairs={{0,32},{4,36},{8,40},{12,44},{16,48},{20,52},{24,56},{28,60},{32,0... | collective-permute-start | bytes 98312 | tf_op jit(solution)/shard_map/ppermute | solution.py:23
  34.9 8.4 %collective-permute-start.30 = (bf16[4,2,4,512]{3,2,1,0:T(4,128)(2,1)S(1)}, bf16[4,2,4,512]{3,2,1,0:T(4,128)(2,1)S(1)}, u32[]{:S(2)}, u32[]{:S(2)}) collective-permute-start(bf16[4,2,4,512]{3,2,1,0:T(4,128)(2,1)S(1)} %pad_maximum_fusion.3), channel_id=1, source_target_pairs={{0,48},{4,52},{8,56},{12,60},{16,32},{20,36},{24,40},{28,44},{32,1... | collective-permute-start | bytes 98312 | tf_op jit(solution)/shard_map/ppermute | solution.py:23
  35.7 29.8 %collective-permute-start.19 = (bf16[1,128,1024]{2,1,0:T(8,128)(2,1)S(1)}, bf16[1,128,1024]{2,1,0:T(8,128)(2,1)S(1)}, u32[]{:S(2)}, u32[]{:S(2)}) collective-permute-start(bf16[1,128,1024]{2,1,0:T(8,128)(2,1)S(1)} %get-tuple-element.29.refs_1_), channel_id=1, source_target_pairs={{0,2},{1,3},{2,0},{3,1},{4,6},{5,7},{6,4},{7,5},{8,10},{9,11},{10,... | collective-permute-start | bytes 786440 | tf_op jit(solution)/shard_map/ppermute | solution.py:23
  36.6 29.5 %collective-permute-start.15 = (bf16[1,128,1024]{2,1,0:T(8,128)(2,1)S(1)}, bf16[1,128,1024]{2,1,0:T(8,128)(2,1)S(1)}, u32[]{:S(2)}, u32[]{:S(2)}) collective-permute-start(bf16[1,128,1024]{2,1,0:T(8,128)(2,1)S(1)} %get-tuple-element.29.refs_1_), channel_id=1, source_target_pairs={{0,1},{1,0},{2,3},{3,2},{4,5},{5,4},{6,7},{7,6},{8,9},{9,8},{10,11... | collective-permute-start | bytes 786440 | tf_op jit(solution)/shard_map/ppermute | solution.py:23
  42.5 3.4 %collective-permute-start.16 = (bf16[1,64,1024]{2,1,0:T(8,128)(2,1)S(1)}, bf16[1,64,1024]{2,1,0:T(8,128)(2,1)S(1)}, u32[]{:S(2)}, u32[]{:S(2)}) collective-permute-start(bf16[1,64,1024]{2,1,0:T(8,128)(2,1)S(1)} %get-tuple-element.26.refs_2_), channel_id=1, source_target_pairs={{0,1},{1,0},{2,3},{3,2},{4,5},{5,4},{6,7},{7,6},{8,9},{9,8},{10,11... | collective-permute-start | bytes 393224 | tf_op jit(solution)/shard_map/ppermute | solution.py:23
  42.5 5.6 %collective-permute-start.10 = (bf16[1,64,1024]{2,1,0:T(8,128)(2,1)S(1)}, bf16[1,64,1024]{2,1,0:T(8,128)(2,1)S(1)}, u32[]{:S(2)}, u32[]{:S(2)}) collective-permute-start(bf16[1,64,1024]{2,1,0:T(8,128)(2,1)S(1)} %get-tuple-element.26.refs_2_), channel_id=1, source_target_pairs={{0,2},{1,3},{2,0},{3,1},{4,6},{5,7},{6,4},{7,5},{8,10},{9,11},{10,... | collective-permute-start | bytes 393224 | tf_op jit(solution)/shard_map/ppermute | solution.py:23
  43.3 3.5 %collective-permute-start.17 = (bf16[1,64,1024]{2,1,0:T(8,128)(2,1)S(1)}, bf16[1,64,1024]{2,1,0:T(8,128)(2,1)S(1)}, u32[]{:S(2)}, u32[]{:S(2)}) collective-permute-start(bf16[1,64,1024]{2,1,0:T(8,128)(2,1)S(1)} %get-tuple-element.27.refs_3_), channel_id=1, source_target_pairs={{0,1},{1,0},{2,3},{3,2},{4,5},{5,4},{6,7},{7,6},{8,9},{9,8},{10,11... | collective-permute-start | bytes 393224 | tf_op jit(solution)/shard_map/ppermute | solution.py:23
  45.9 22.2 %collective-permute-start.18 = (bf16[1,256,1024]{2,1,0:T(8,128)(2,1)S(1)}, bf16[1,256,1024]{2,1,0:T(8,128)(2,1)S(1)}, u32[]{:S(2)}, u32[]{:S(2)}) collective-permute-start(bf16[1,256,1024]{2,1,0:T(8,128)(2,1)S(1)} %get-tuple-element.28.refs_0_), channel_id=1, source_target_pairs={{0,2},{1,3},{2,0},{3,1},{4,6},{5,7},{6,4},{7,5},{8,10},{9,11},{10,... | collective-permute-start | bytes 1572872 | tf_op jit(solution)/shard_map/ppermute | solution.py:23
  46.9 16.0 %collective-permute-start.11 = (bf16[1,64,1024]{2,1,0:T(8,128)(2,1)S(1)}, bf16[1,64,1024]{2,1,0:T(8,128)(2,1)S(1)}, u32[]{:S(2)}, u32[]{:S(2)}) collective-permute-start(bf16[1,64,1024]{2,1,0:T(8,128)(2,1)S(1)} %get-tuple-element.27.refs_3_), channel_id=1, source_target_pairs={{0,2},{1,3},{2,0},{3,1},{4,6},{5,7},{6,4},{7,5},{8,10},{9,11},{10,... | collective-permute-start | bytes 393224 | tf_op jit(solution)/shard_map/ppermute | solution.py:23
  48.1 16.6 %collective-permute-start.31 = (bf16[4,2,16,512]{3,2,1,0:T(8,128)(2,1)S(1)}, bf16[4,2,16,512]{3,2,1,0:T(8,128)(2,1)S(1)}, u32[]{:S(2)}, u32[]{:S(2)}) collective-permute-start(bf16[4,2,16,512]{3,2,1,0:T(8,128)(2,1)S(1)} %pad_maximum_fusion.own_ref), channel_id=1, source_target_pairs={{0,1},{1,0},{2,3},{3,2},{4,5},{5,4},{6,7},{7,6},{8,9},{9,8},{10,11... | collective-permute-start | bytes 393224 | tf_op jit(solution)/shard_map/ppermute | solution.py:23
  62.9 6.8 %collective-permute-start.14 = (bf16[1,256,1024]{2,1,0:T(8,128)(2,1)S(1)}, bf16[1,256,1024]{2,1,0:T(8,128)(2,1)S(1)}, u32[]{:S(2)}, u32[]{:S(2)}) collective-permute-start(bf16[1,256,1024]{2,1,0:T(8,128)(2,1)S(1)} %get-tuple-element.28.refs_0_), channel_id=1, source_target_pairs={{0,1},{1,0},{2,3},{3,2},{4,5},{5,4},{6,7},{7,6},{8,9},{9,8},{10,11... | collective-permute-start | bytes 1572872 | tf_op jit(solution)/shard_map/ppermute | solution.py:23
  64.7 13.5 %collective-permute-start.5 = (bf16[1,256,1024]{2,1,0:T(8,128)(2,1)S(1)}, bf16[1,256,1024]{2,1,0:T(8,128)(2,1)S(1)}, u32[]{:S(2)}, u32[]{:S(2)}) collective-permute-start(bf16[1,256,1024]{2,1,0:T(8,128)(2,1)S(1)} %get-tuple-element.23.refs_1_), channel_id=1, source_target_pairs={{0,2},{1,3},{2,0},{3,1},{4,6},{5,7},{6,4},{7,5},{8,10},{9,11},{10,... | collective-permute-start | bytes 1572872 | tf_op jit(solution)/shard_map/ppermute | solution.py:23
  65.5 24.0 %collective-permute-start.4 = (bf16[1,256,1024]{2,1,0:T(8,128)(2,1)S(1)}, bf16[1,256,1024]{2,1,0:T(8,128)(2,1)S(1)}, u32[]{:S(2)}, u32[]{:S(2)}) collective-permute-start(bf16[1,256,1024]{2,1,0:T(8,128)(2,1)S(1)} %shard_map.111.refs_0_), channel_id=1, source_target_pairs={{0,2},{1,3},{2,0},{3,1},{4,6},{5,7},{6,4},{7,5},{8,10},{9,11},{10,... | collective-permute-start | bytes 1572872 | tf_op jit(solution)/shard_map/ppermute | solution.py:23
  66.2 1.6 %collective-permute-start.12 = (bf16[1,64,1024]{2,1,0:T(8,128)(2,1)S(1)}, bf16[1,64,1024]{2,1,0:T(8,128)(2,1)S(1)}, u32[]{:S(2)}, u32[]{:S(2)}) collective-permute-start(bf16[1,64,1024]{2,1,0:T(8,128)(2,1)S(1)} %collective-permute-done.10.refs_0_), channel_id=1, source_target_pairs={{0,1},{1,0},{2,3},{3,2},{4,5},{5,4},{6,7},{7,6},{8,9},{9,8},{10,11... | collective-permute-start | bytes 393224 | tf_op jit(solution)/shard_map/ppermute | solution.py:23
  67.7 1.5 %collective-permute-start.21 = (bf16[1,128,1024]{2,1,0:T(8,128)(2,1)S(1)}, bf16[1,128,1024]{2,1,0:T(8,128)(2,1)S(1)}, u32[]{:S(2)}, u32[]{:S(2)}) collective-permute-start(bf16[1,128,1024]{2,1,0:T(8,128)(2,1)S(1)} %collective-permute-done.19.refs_9_), channel_id=1, source_target_pairs={{0,1},{1,0},{2,3},{3,2},{4,5},{5,4},{6,7},{7,6},{8,9},{9,8},{10,11... | collective-permute-start | bytes 786440 | tf_op jit(solution)/shard_map/ppermute | solution.py:23
  68.1 22.2 %collective-permute-start.20 = (bf16[1,256,1024]{2,1,0:T(8,128)(2,1)S(1)}, bf16[1,256,1024]{2,1,0:T(8,128)(2,1)S(1)}, u32[]{:S(2)}, u32[]{:S(2)}) collective-permute-start(bf16[1,256,1024]{2,1,0:T(8,128)(2,1)S(1)} %collective-permute-done.18.refs_8_), channel_id=1, source_target_pairs={{0,1},{1,0},{2,3},{3,2},{4,5},{5,4},{6,7},{7,6},{8,9},{9,8},{10,11... | collective-permute-start | bytes 1572872 | tf_op jit(solution)/shard_map/ppermute | solution.py:23
  69.3 24.5 %collective-permute-start.3 = (bf16[1,256,1024]{2,1,0:T(8,128)(2,1)S(1)}, bf16[1,256,1024]{2,1,0:T(8,128)(2,1)S(1)}, u32[]{:S(2)}, u32[]{:S(2)}) collective-permute-start(bf16[1,256,1024]{2,1,0:T(8,128)(2,1)S(1)} %get-tuple-element.23.refs_1_), channel_id=1, source_target_pairs={{0,1},{1,0},{2,3},{3,2},{4,5},{5,4},{6,7},{7,6},{8,9},{9,8},{10,11... | collective-permute-start | bytes 1572872 | tf_op jit(solution)/shard_map/ppermute | solution.py:23
  69.6 24.2 %collective-permute-start.2 = (bf16[1,256,1024]{2,1,0:T(8,128)(2,1)S(1)}, bf16[1,256,1024]{2,1,0:T(8,128)(2,1)S(1)}, u32[]{:S(2)}, u32[]{:S(2)}) collective-permute-start(bf16[1,256,1024]{2,1,0:T(8,128)(2,1)S(1)} %shard_map.111.refs_0_), channel_id=1, source_target_pairs={{0,1},{1,0},{2,3},{3,2},{4,5},{5,4},{6,7},{7,6},{8,9},{9,8},{10,11... | collective-permute-start | bytes 1572872 | tf_op jit(solution)/shard_map/ppermute | solution.py:23
  78.2 15.6 %collective-permute-start.7 = (bf16[1,256,1024]{2,1,0:T(8,128)(2,1)S(1)}, bf16[1,256,1024]{2,1,0:T(8,128)(2,1)S(1)}, u32[]{:S(2)}, u32[]{:S(2)}) collective-permute-start(bf16[1,256,1024]{2,1,0:T(8,128)(2,1)S(1)} %collective-permute-done.5.refs_5_), channel_id=1, source_target_pairs={{0,1},{1,0},{2,3},{3,2},{4,5},{5,4},{6,7},{7,6},{8,9},{9,8},{10,11... | collective-permute-start | bytes 1572872 | tf_op jit(solution)/shard_map/ppermute | solution.py:23
  89.4 4.4 %collective-permute-start.6 = (bf16[1,256,1024]{2,1,0:T(8,128)(2,1)S(1)}, bf16[1,256,1024]{2,1,0:T(8,128)(2,1)S(1)}, u32[]{:S(2)}, u32[]{:S(2)}) collective-permute-start(bf16[1,256,1024]{2,1,0:T(8,128)(2,1)S(1)} %collective-permute-done.4.refs_4_), channel_id=1, source_target_pairs={{0,1},{1,0},{2,3},{3,2},{4,5},{5,4},{6,7},{7,6},{8,9},{9,8},{10,11... | collective-permute-start | bytes 1572872 | tf_op jit(solution)/shard_map/ppermute | solution.py:23
  90.3 2.7 %collective-permute-start.13 = (bf16[1,64,1024]{2,1,0:T(8,128)(2,1)S(1)}, bf16[1,64,1024]{2,1,0:T(8,128)(2,1)S(1)}, u32[]{:S(2)}, u32[]{:S(2)}) collective-permute-start(bf16[1,64,1024]{2,1,0:T(8,128)(2,1)S(1)} %collective-permute-done.11.refs_1_), channel_id=1, source_target_pairs={{0,1},{1,0},{2,3},{3,2},{4,5},{5,4},{6,7},{7,6},{8,9},{9,8},{10,11... | collective-permute-start | bytes 393224 | tf_op jit(solution)/shard_map/ppermute | solution.py:23

commit v2 on v1

--- a/solution.py
+++ b/solution.py
@@ -9,7 +9,7 @@
 
 
 CORE, CHIP = 1, 2
-GATE = (256, 256)
+GATE = (64, 192, 256)
 UP = (256, 128, 64, 64)
 LOADS = 8
 MIB = 1 << 20
@@ -82,27 +82,33 @@
     )(share, w, avg)
 
 
-def narrow_body(first, blocks, scaled, fresh_ref, pair_ref, other_ref, *outs):
+def narrow_body(first, blocks, whole, fresh_ref, pair_ref, other_ref, *outs):
     columns = fresh_ref.shape[1]
-    scale = jnp.sqrt(pair_ref[:, :columns] + other_ref[:, :columns])
-    if scaled:
-        outs[-1][...] = scale
-    inverse = 1.0 / scale
+    inverse = 1.0 / jnp.sqrt(pair_ref[:, :columns] + other_ref[:, :columns])
+
+    def rows_of(at):
+        return (fresh_ref[pl.ds(at, 16)] * inverse).astype(jnp.bfloat16)
+
+    if whole:
+        for at in range(0, first, 16):
+            outs[-1][0, pl.ds(at, 16)] = rows_of(at)
     at = first
     for rows, out in zip(blocks, outs):
-        for i in range(rows // 16):
-            out[0, pl.ds(i * 16, 16)] = (fresh_ref[pl.ds(at + i * 16, 16)] * inverse).astype(out.dtype)
+        for i in range(0, rows, 16):
+            value = rows_of(at + i)
+            out[0, pl.ds(i, 16)] = value
+            if whole:
+                outs[-1][0, pl.ds(at + i, 16)] = value
         at += rows
 
 
-def narrow(fresh, totals, first, blocks, scaled):
-    columns = fresh.shape[1]
-    outs = [pltpu.VMEM((1, rows, columns), jnp.bfloat16) for rows in blocks]
-    if scaled:
-        outs.append(jax.ShapeDtypeStruct((1, columns), jnp.float32))
+def narrow(fresh, totals, first, blocks, whole):
+    rows, columns = fresh.shape
+    sizes = [*blocks, rows] if whole else blocks
+    outs = tuple(pltpu.VMEM((1, n, columns), jnp.bfloat16) for n in sizes)
     return call(
-        functools.partial(narrow_body, first, blocks, scaled),
-        tuple(outs),
+        functools.partial(narrow_body, first, blocks, whole),
+        outs,
         [VMEM, VMEM, VMEM],
         2,
         2 << 20,
@@ -123,9 +129,9 @@
         c.wait()
 
 
-def place(pieces, shape, into=None):
+def place(pieces, shard_rows, shape, into=None):
     blocks = [p[0] for p in pieces]
-    places = tuple((m, at, b.shape[1], total) for b, m, at, total in pieces)
+    places = tuple((m, at, b.shape[1], shard_rows) for b, m, at in pieces)
     n = len(blocks)
     again = into is not None
     return call(
@@ -148,11 +154,13 @@
     return out
 
 
-def from_all(own):
-    chips = [swap(b, "shard", CHIP) for b in own]
-    cores = [swap(b, "shard", CORE) for b in own]
+def from_all(blocks, whole):
+    chips = [swap(b, "shard", CHIP) for b in blocks]
     boths = [swap(b, "shard", CORE) for b in chips]
-    return {0: own, CORE: cores, CHIP: chips, CORE | CHIP: boths}
+    at = starts([b.shape[1] for b in blocks])
+    near = [(whole, 0, 0), (swap(whole, "shard", CORE), CORE, 0)]
+    far = [[(c, CHIP, n), (b, CORE | CHIP, n)] for c, b, n in zip(chips, boths, at)]
+    return near, far
 
 
 BITS = (("shard", CHIP), ("expert", 1), ("expert", 2), ("expert", 4), ("expert", 8))
@@ -193,15 +201,28 @@
                 out_ref[pl.ds(k * plane, plane), pl.ds(at, rows)] = value
 
 
+def turned(x):
+    experts, shards = lax.axis_size("expert"), lax.axis_size("shard")
+    pairs = []
+    for e in range(experts):
+        for s in range(shards):
+            to = (e + (16 if s & CHIP else -16)) % experts
+            pairs.append((e * shards + s, to * shards + s))
+    return lax.ppermute(x, ("expert", "shard"), pairs)
+
+
 def planes_body(*refs):
     z = lax.axis_index("expert") // 16
+    up = (lax.axis_index("shard") & CHIP) == 0
     for k, ref in enumerate(refs[:-1]):
-        refs[-1][z ^ k] = ref[0]
+        refs[-1][jnp.where(up, z + k, z + 4 - k) % 4] = ref[0]
 
 
 def router_of(lows, own, other):
-    x = in_order(lows["shard", CHIP], own[None, None], other[None, None], 1)
-    pieces = (x, *(swap(x, "expert", 16 * k) for k in (1, 2, 3)))
+    pieces = [in_order(lows["shard", CHIP], own[None, None], other[None, None], 1)]
+    for _ in range(3):
+        pieces.append(turned(pieces[-1]))
+    x = pieces[0]
     x = call(
         planes_body,
         jax.ShapeDtypeStruct((4, *x.shape[1:]), x.dtype),
@@ -226,6 +247,11 @@
     )(x, other).T
 
 
+def scale_of(totals, columns):
+    pair, other = totals
+    return jnp.sqrt(pair[:, :columns] + other[:, :columns])
+
+
 def per_device(w_gate, avg_gate, w_up, avg_up, mix_share, router_weight, router_gain):
     rows, columns = w_gate.shape[1:]
     shape = (1, lax.axis_size("shard") * rows, columns)
@@ -236,25 +262,20 @@
     pair = sums_gate + swap(sums_gate, "shard", CORE)
     pair = jnp.concatenate([pair, part.astype(jnp.float32)], axis=1)
     totals_gate = pair, swap(pair, "shard", CHIP)
-    (gate_0,) = narrow(fresh_gate, totals_gate, 0, GATE[:1], False)
-    *gate_rest, scale_gate = narrow(fresh_gate, totals_gate, GATE[0], GATE[1:], True)
-    gate = from_all([gate_0, *gate_rest])
+    scale_gate = scale_of(totals_gate, columns)
+    gate = narrow(fresh_gate, totals_gate, 0, GATE[:1], False)
+    *rest, whole = narrow(fresh_gate, totals_gate, GATE[0], GATE[1:], True)
+    near, far = from_all([*gate, *rest], whole)
+    serve_gate = place(sum(far, near), rows, shape)
 
     fresh_up, sums_up = mean_of(mix_share, w_up, avg_up, 56)
     pair = sums_up + swap(sums_up, "shard", CORE)
     totals_up = pair, swap(pair, "shard", CHIP)
-    *own_up, scale_up = narrow(fresh_up, totals_up, 0, UP, True)
-    up = from_all(own_up)
-
-    gate_at, up_at = starts(GATE), starts(UP)
-    serve_gate = place(
-        [(b, m, at, rows) for m, bs in gate.items() for b, at in zip(bs, gate_at)], shape
-    )
-    early, late = [], []
-    for m, bs in up.items():
-        for k, (b, at) in enumerate(zip(bs, up_at)):
-            (late if m & CHIP and k >= 2 else early).append((b, m, at, rows))
-    serve_up = place(late, shape, place(early, shape))
+    scale_up = scale_of(totals_up, columns)
+    *up, whole = narrow(fresh_up, totals_up, 0, UP, True)
+    near, far = from_all(up, whole)
+    serve_up = place(sum(far[:2], near), rows, shape)
+    serve_up = place(sum(far[2:], []), rows, shape, serve_up)
 
     other = totals_gate[1][:, columns:].astype(jnp.bfloat16)
     serve_router = router_of(lows, part, other)

time: 96.2 us -> 102 us (1.060)
  waiting for transfers between devices: 40.4 us -> 43.4 us
  starting transfers between devices: 41.8 us -> 44 us
  other arithmetic: 0.5 us -> 1.71 us
  Pallas kernels: 11.7 us -> 10.5 us
    ppermute x0 -> x3, starting transfers between devices: none -> 8.2 us  [turned(): return lax.ppermute(x, ('expert', 'shard'), pairs)]
    ppermute x32 -> x27, starting transfers between devices: 41.8 us -> 35.8 us  [swap(): return lax.ppermute(x, axis, [(i, i ^ mask) for i in range(n)])]
    ppermute x0 -> x3, waiting for transfers between devices: none -> 4.09 us  [turned(): return lax.ppermute(x, ('expert', 'shard'), pairs)]
    sqrt x0 -> x2, other arithmetic: none -> 1.21 us  [scale_of(): return jnp.sqrt(pair[:, :columns] + other[:, :columns])]
    ppermute x32 -> x27, waiting for transfers between devices: 40.4 us -> 39.3 us  [swap(): return lax.ppermute(x, axis, [(i, i ^ mask) for i in range(n)])]
    pallas_call x3, Pallas kernels: 1.4 us -> 0.33 us  [narrow(): call(functools.partial(narrow_body, first, blocks, whole), outs, [VMEM, V...]
  transfers between devices with their start and end apart: 32 -> 30, of which waited for: 11 -> 10; matrix products, arithmetic and copies ran while one was open for 1% -> 2% of each run, Pallas kernels for 8% -> 6%
where the time goes in v2:
time: 102 us; the launch traced here: 101 us
  starting transfers between devices  44 us (43%)
  waiting for transfers between devices  43.4 us (43%)
  Pallas kernels  10.5 us (10%)
  other arithmetic  1.71 us (2%)
  between operations  1.71 us (2%)
    ppermute x27, waiting for transfers between devices, swap(): return lax.ppermute(x, axis, [(i, i ^ mask) for i in range(n)])  39.3 us
    ppermute x27, starting transfers between devices, swap(): return lax.ppermute(x, axis, [(i, i ^ mask) for i in range(n)])  35.8 us
    ppermute x3, starting transfers between devices, turned(): return lax.ppermute(x, ('expert', 'shard'), pairs)  8.2 us
    pallas_call x3, Pallas kernels, place(): call(functools.partial(place_body, places), jax.ShapeDtypeStruct(shape, b...  4.79 us
    pallas_call x2, Pallas kernels, mean_of(): call(mean_body, (pltpu.VMEM((rows, columns), jnp.float32), pltpu.VMEM((1,...  4.67 us
    ppermute x3, waiting for transfers between devices, turned(): return lax.ppermute(x, ('expert', 'shard'), pairs)  4.09 us
  transfers between devices with their start and end apart: 30, of which 10 were waited for; matrix products, arithmetic and copies ran while one was open for 2% of the time, Pallas kernels for 6%

profile of v2, /device:TPU:1, one launch (start us, length us, event | category | flops | bytes accessed | tf_op | source)
XLA Modules:
  0.0 101.4 jit_solution(1546647076401336553)
XLA Ops:
  1.3 2.3 %shard_map.110 = (f32[512,1024]{1,0:T(8,128)S(1)}, f32[1,1024]{1,0:T(1,128)S(1)}) custom-call(f32[1]{0:T(128)S(6)} %copy.15.share_ref, f32[1,512,1024]{2,1,0:T(8,128)} %w_ref.2, f32[1,512,1024]{2,1,0:T(8,128)} %avg_ref.2), custom_call_target="tpu_custom_call" | custom-call | flops 4194304 | bytes 4194304 | tf_op jit(solution)/shard_map/pallas_call | solution.py:70
  3.6 3.3 %collective-permute-start = (f32[1,1024]{1,0:T(1,128)S(1)}, f32[1,1024]{1,0:T(1,128)S(1)}, u32[]{:S(2)}, u32[]{:S(2)}) collective-permute-start(f32[1,1024]{1,0:T(1,128)S(1)} %get-tuple-element.23), channel_id=1, source_target_pairs={{0,1},{1,0},{2,3},{3,2},{4,5},{5,4},{6,7},{7,6},{8,9},{9,8},{10,11... | collective-permute-start | bytes 12296 | tf_op jit(solution)/shard_map/ppermute | solution.py:23
  7.0 0.8 collective-permute-done
  7.8 0.1 collective-permute-start.1
  7.9 2.4 %collective-permute-done.1.other_ref = f32[1,1536]{1,0:T(1,128)S(1)} collective-permute-done((f32[1,1536]{1,0:T(1,128)S(1)}, f32[1,1536]{1,0:T(1,128)S(1)}, u32[]{:S(2)}, u32[]{:S(2)}) %collective-permute-start.1) | collective-permute-done | bytes 6176 | tf_op jit(solution)/shard_map/ppermute | solution.py:23
  10.4 4.4 %collective-permute-start.20 = (bf16[1,2,1,512]{3,2,1,0:T(2,128)(2,1)S(1)}, bf16[1,2,1,512]{3,2,1,0:T(2,128)(2,1)S(1)}, u32[]{:S(2)}, u32[]{:S(2)}) collective-permute-start(bf16[1,2,1,512]{3,2,1,0:T(2,128)(2,1)S(1)} %constant_dynamic-update-slice_fusion.refs_0_), channel_id=1, source_target_pairs={{0,192},{1,193},{2,66},{3,67},{4,196},{5,197},{6,70},{7,71},{8,200... | collective-permute-start | bytes 6152 | tf_op jit(solution)/shard_map/ppermute | solution.py:211
  14.8 0.8 collective-permute-done.20.refs_1_
  15.5 3.8 %collective-permute-start.21 = (bf16[1,2,1,512]{3,2,1,0:T(2,128)(2,1)S(1)}, bf16[1,2,1,512]{3,2,1,0:T(2,128)(2,1)S(1)}, u32[]{:S(2)}, u32[]{:S(2)}) collective-permute-start(bf16[1,2,1,512]{3,2,1,0:T(2,128)(2,1)S(1)} %collective-permute-done.20.refs_1_), channel_id=1, source_target_pairs={{0,192},{1,193},{2,66},{3,67},{4,196},{5,197},{6,70},{7,71},{8,200... | collective-permute-start | bytes 6152 | tf_op jit(solution)/shard_map/ppermute | solution.py:211
  19.4 2.3 %shard_map.114 = (f32[512,1024]{1,0:T(8,128)S(1)}, f32[1,1024]{1,0:T(1,128)S(1)}) custom-call(f32[1]{0:T(128)S(6)} %copy.15.share_ref, f32[1,512,1024]{2,1,0:T(8,128)} %w_ref.3, f32[1,512,1024]{2,1,0:T(8,128)} %avg_ref.3), custom_call_target="tpu_custom_call" | custom-call | flops 4194304 | bytes 4194304 | tf_op jit(solution)/shard_map/pallas_call | solution.py:70
  21.7 3.0 %collective-permute-start.9 = (f32[1,1024]{1,0:T(1,128)S(1)}, f32[1,1024]{1,0:T(1,128)S(1)}, u32[]{:S(2)}, u32[]{:S(2)}) collective-permute-start(f32[1,1024]{1,0:T(1,128)S(1)} %get-tuple-element.28), channel_id=1, source_target_pairs={{0,1},{1,0},{2,3},{3,2},{4,5},{5,4},{6,7},{7,6},{8,9},{9,8},{10,11... | collective-permute-start | bytes 12296 | tf_op jit(solution)/shard_map/ppermute | solution.py:23
  24.7 3.3 %collective-permute-done.22.refs_3_ = bf16[1,2,1,512]{3,2,1,0:T(2,128)(2,1)S(1)} collective-permute-done((bf16[1,2,1,512]{3,2,1,0:T(2,128)(2,1)S(1)}, bf16[1,2,1,512]{3,2,1,0:T(2,128)(2,1)S(1)}, u32[]{:S(2)}, u32[]{:S(2)}) %collective-permute-start.22) | collective-permute-done | bytes 2080 | tf_op jit(solution)/shard_map/ppermute | solution.py:211
  28.1 1.3 %collective-permute-start.23 = (bf16[4,2,1,512]{3,2,1,0:T(2,128)(2,1)S(1)}, bf16[4,2,1,512]{3,2,1,0:T(2,128)(2,1)S(1)}, u32[]{:S(2)}, u32[]{:S(2)}) collective-permute-start(bf16[4,2,1,512]{3,2,1,0:T(2,128)(2,1)S(1)} %shard_map.119), channel_id=1, source_target_pairs={{0,4},{4,0},{8,12},{12,8},{16,20},{20,16},{24,28},{28,24},{32,36},... | collective-permute-start | bytes 24584 | tf_op jit(solution)/shard_map/ppermute | solution.py:23
  29.4 2.5 %collective-permute-start.24 = (bf16[4,2,1,512]{3,2,1,0:T(2,128)(2,1)S(1)}, bf16[4,2,1,512]{3,2,1,0:T(2,128)(2,1)S(1)}, u32[]{:S(2)}, u32[]{:S(2)}) collective-permute-start(bf16[4,2,1,512]{3,2,1,0:T(2,128)(2,1)S(1)} %shard_map.119), channel_id=1, source_target_pairs={{0,8},{4,12},{8,0},{12,4},{16,24},{20,28},{24,16},{28,20},{32,40},... | collective-permute-start | bytes 24584 | tf_op jit(solution)/shard_map/ppermute | solution.py:23
  31.8 0.2 collective-permute-start.25
  32.1 0.1 collective-permute-start.10
  32.2 1.3 %collective-permute-done.24 = bf16[4,2,1,512]{3,2,1,0:T(2,128)(2,1)S(1)} collective-permute-done((bf16[4,2,1,512]{3,2,1,0:T(2,128)(2,1)S(1)}, bf16[4,2,1,512]{3,2,1,0:T(2,128)(2,1)S(1)}, u32[]{:S(2)}, u32[]{:S(2)}) %collective-permute-start.24) | collective-permute-done | bytes 8224 | tf_op jit(solution)/shard_map/ppermute | solution.py:23
  33.5 2.3 %collective-permute-done.25 = bf16[4,2,1,512]{3,2,1,0:T(2,128)(2,1)S(1)} collective-permute-done((bf16[4,2,1,512]{3,2,1,0:T(2,128)(2,1)S(1)}, bf16[4,2,1,512]{3,2,1,0:T(2,128)(2,1)S(1)}, u32[]{:S(2)}, u32[]{:S(2)}) %collective-permute-start.25) | collective-permute-done | bytes 8224 | tf_op jit(solution)/shard_map/ppermute | solution.py:23
  35.8 0.1 broadcast_select_fusion.7
  36.0 1.4 %collective-permute-start.26 = (bf16[4,2,4,512]{3,2,1,0:T(4,128)(2,1)S(1)}, bf16[4,2,4,512]{3,2,1,0:T(4,128)(2,1)S(1)}, u32[]{:S(2)}, u32[]{:S(2)}) collective-permute-start(bf16[4,2,4,512]{3,2,1,0:T(4,128)(2,1)S(1)} %pad_maximum_fusion.3), channel_id=1, source_target_pairs={{0,16},{4,20},{8,24},{12,28},{16,0},{20,4},{24,8},{28,12},{32,48},... | collective-permute-start | bytes 98312 | tf_op jit(solution)/shard_map/ppermute | solution.py:23
  37.4 2.6 %collective-permute-start.27 = (bf16[4,2,4,512]{3,2,1,0:T(4,128)(2,1)S(1)}, bf16[4,2,4,512]{3,2,1,0:T(4,128)(2,1)S(1)}, u32[]{:S(2)}, u32[]{:S(2)}) collective-permute-start(bf16[4,2,4,512]{3,2,1,0:T(4,128)(2,1)S(1)} %pad_maximum_fusion.3), channel_id=1, source_target_pairs={{0,32},{4,36},{8,40},{12,44},{16,48},{20,52},{24,56},{28,60},{32,0... | collective-permute-start | bytes 98312 | tf_op jit(solution)/shard_map/ppermute | solution.py:23
  40.0 0.2 shard_map.115
  40.2 0.1 collective-permute-start.16
  40.3 4.9 %collective-permute-start.15 = (bf16[1,512,1024]{2,1,0:T(8,128)(2,1)S(1)}, bf16[1,512,1024]{2,1,0:T(8,128)(2,1)S(1)}, u32[]{:S(2)}, u32[]{:S(2)}) collective-permute-start(bf16[1,512,1024]{2,1,0:T(8,128)(2,1)S(1)} %get-tuple-element.31.refs_0_), channel_id=1, source_target_pairs={{0,1},{1,0},{2,3},{3,2},{4,5},{5,4},{6,7},{7,6},{8,9},{9,8},{10,11... | collective-permute-start | bytes 3145736 | tf_op jit(solution)/shard_map/ppermute | solution.py:23
  45.2 0.6 collective-permute-start.18
  45.8 1.0 collective-permute-start.11
  46.8 0.5 collective-permute-start.13
  47.2 0.1 broadcast_select_fusion.11
  47.4 11.2 %collective-permute-done.11.refs_0_ = bf16[1,64,1024]{2,1,0:T(8,128)(2,1)S(1)} collective-permute-done((bf16[1,64,1024]{2,1,0:T(8,128)(2,1)S(1)}, bf16[1,64,1024]{2,1,0:T(8,128)(2,1)S(1)}, u32[]{:S(2)}, u32[]{:S(2)}) %collective-permute-start.11) | collective-permute-done | bytes 131104 | tf_op jit(solution)/shard_map/ppermute | solution.py:23
  58.6 2.8 %collective-permute-done.13.refs_2_ = bf16[1,64,1024]{2,1,0:T(8,128)(2,1)S(1)} collective-permute-done((bf16[1,64,1024]{2,1,0:T(8,128)(2,1)S(1)}, bf16[1,64,1024]{2,1,0:T(8,128)(2,1)S(1)}, u32[]{:S(2)}, u32[]{:S(2)}) %collective-permute-start.13) | collective-permute-done | bytes 131104 | tf_op jit(solution)/shard_map/ppermute | solution.py:23
  61.4 5.9 %collective-permute-start.29 = (bf16[4,2,16,512]{3,2,1,0:T(8,128)(2,1)S(1)}, bf16[4,2,16,512]{3,2,1,0:T(8,128)(2,1)S(1)}, u32[]{:S(2)}, u32[]{:S(2)}) collective-permute-start(bf16[4,2,16,512]{3,2,1,0:T(8,128)(2,1)S(1)} %pad_maximum_fusion.own_ref), channel_id=1, source_target_pairs={{0,1},{1,0},{2,3},{3,2},{4,5},{5,4},{6,7},{7,6},{8,9},{9,8},{10,11... | collective-permute-start | bytes 393224 | tf_op jit(solution)/shard_map/ppermute | solution.py:23
  67.3 3.6 %collective-permute-start.12 = (bf16[1,64,1024]{2,1,0:T(8,128)(2,1)S(1)}, bf16[1,64,1024]{2,1,0:T(8,128)(2,1)S(1)}, u32[]{:S(2)}, u32[]{:S(2)}) collective-permute-start(bf16[1,64,1024]{2,1,0:T(8,128)(2,1)S(1)} %collective-permute-done.11.refs_0_), channel_id=1, source_target_pairs={{0,1},{1,0},{2,3},{3,2},{4,5},{5,4},{6,7},{7,6},{8,9},{9,8},{10,11... | collective-permute-start | bytes 393224 | tf_op jit(solution)/shard_map/ppermute | solution.py:23
  70.8 0.1 shard_map.111
  71.0 0.1 collective-permute-start.5
  71.1 1.4 %collective-permute-start.7 = (bf16[1,256,1024]{2,1,0:T(8,128)(2,1)S(1)}, bf16[1,256,1024]{2,1,0:T(8,128)(2,1)S(1)}, u32[]{:S(2)}, u32[]{:S(2)}) collective-permute-start(bf16[1,256,1024]{2,1,0:T(8,128)(2,1)S(1)} %get-tuple-element.26), channel_id=1, source_target_pairs={{0,2},{1,3},{2,0},{3,1},{4,6},{5,7},{6,4},{7,5},{8,10},{9,11},{10,... | collective-permute-start | bytes 1572872 | tf_op jit(solution)/shard_map/ppermute | solution.py:23
  72.5 0.6 collective-permute-start.2
  73.1 0.1 collective-permute-start.17
  73.2 8.5 %collective-permute-done.5.refs_4_ = bf16[1,192,1024]{2,1,0:T(8,128)(2,1)S(1)} collective-permute-done((bf16[1,192,1024]{2,1,0:T(8,128)(2,1)S(1)}, bf16[1,192,1024]{2,1,0:T(8,128)(2,1)S(1)}, u32[]{:S(2)}, u32[]{:S(2)}) %collective-permute-start.5) | collective-permute-done | bytes 393248 | tf_op jit(solution)/shard_map/ppermute | solution.py:23
  81.7 1.3 %collective-permute-start.19 = (bf16[1,128,1024]{2,1,0:T(8,128)(2,1)S(1)}, bf16[1,128,1024]{2,1,0:T(8,128)(2,1)S(1)}, u32[]{:S(2)}, u32[]{:S(2)}) collective-permute-start(bf16[1,128,1024]{2,1,0:T(8,128)(2,1)S(1)} %collective-permute-done.18.refs_4_), channel_id=1, source_target_pairs={{0,1},{1,0},{2,3},{3,2},{4,5},{5,4},{6,7},{7,6},{8,9},{9,8},{10,11... | collective-permute-start | bytes 786440 | tf_op jit(solution)/shard_map/ppermute | solution.py:23
  83.1 9.9 %collective-permute-done.7.refs_6_ = bf16[1,256,1024]{2,1,0:T(8,128)(2,1)S(1)} collective-permute-done((bf16[1,256,1024]{2,1,0:T(8,128)(2,1)S(1)}, bf16[1,256,1024]{2,1,0:T(8,128)(2,1)S(1)}, u32[]{:S(2)}, u32[]{:S(2)}) %collective-permute-start.7) | collective-permute-done | bytes 524320 | tf_op jit(solution)/shard_map/ppermute | solution.py:23
  93.0 0.9 collective-permute-start.8
  93.8 0.6 add_sqrt_fusion
  94.5 0.5 collective-permute-start.14
  95.0 0.1 collective-permute-start.4
  95.1 0.6 fusion
  95.7 0.7 shard_map.120
  96.4 1.9 %shard_map.116.refs_4_ = bf16[1,2048,1024]{2,1,0:T(8,128)(2,1)} custom-call(bf16[1,512,1024]{2,1,0:T(8,128)(2,1)S(1)} %get-tuple-element.31.refs_0_, bf16[1,512,1024]{2,1,0:T(8,128)(2,1)S(1)} %collective-permute-done.15.refs_1_, bf16[1,256,1024]{2,1,0:T(8,128)(2,1)S(1)} %collective-permute-done.16.refs_2_, ...), custom_call_target="tpu_custom_call" | custom-call | flops 1048576 | bytes 4194304 | tf_op jit(solution)/shard_map/pallas_call | solution.py:137
  98.3 0.8 shard_map.117
  99.2 2.1 %shard_map.113 = bf16[1,2048,1024]{2,1,0:T(8,128)(2,1)} custom-call(bf16[1,512,1024]{2,1,0:T(8,128)(2,1)S(1)} %get-tuple-element.24.refs_0_, bf16[1,512,1024]{2,1,0:T(8,128)(2,1)S(1)} %collective-permute-done.2.refs_1_, bf16[1,64,1024]{2,1,0:T(8,128)(2,1)S(1)} %collective-permute-done.3.refs_2_, bf16[1,64,1024]{2,1,0:T(8,128)(2,1)S(1)} %collective-permute-done.4.refs_3_, ...), custom_call_target="tpu_custom_call" | custom-call | flops 1048576 | bytes 4194304 | tf_op jit(solution)/shard_map/pallas_call | solution.py:137
  (47 shorter events, 0.5 us)
Async XLA Ops:
  1.3 5.7 %copy-start = (f32[512,1]{0,1:T(1,128)S(1)}, f32[512,1]{0,1:T(1,128)}, u32[]{:S(2)}) copy-start(f32[512,1]{0,1:T(1,128)} %param.12) | copy-start | bytes 6148
  1.3 5.7 %copy-start.1 = (f32[512]{0:T(512)S(1)}, f32[512]{0:T(512)}, u32[]{:S(2)}) copy-start(f32[512]{0:T(512)} %param.13) | copy-start | bytes 6148
  3.6 4.1 %collective-permute-start = (f32[1,1024]{1,0:T(1,128)S(1)}, f32[1,1024]{1,0:T(1,128)S(1)}, u32[]{:S(2)}, u32[]{:S(2)}) collective-permute-start(f32[1,1024]{1,0:T(1,128)S(1)} %get-tuple-element.23), channel_id=1, source_target_pairs={{0,1},{1,0},{2,3},{3,2},{4,5},{5,4},{6,7},{7,6},{8,9},{9,8},{10,11... | collective-permute-start | bytes 12296 | tf_op jit(solution)/shard_map/ppermute | solution.py:23
  7.8 2.6 %collective-permute-start.1 = (f32[1,1536]{1,0:T(1,128)S(1)}, f32[1,1536]{1,0:T(1,128)S(1)}, u32[]{:S(2)}, u32[]{:S(2)}) collective-permute-start(f32[1,1536]{1,0:T(1,128)S(1)} %pad_maximum_fusion.6.pair_ref), channel_id=1, source_target_pairs={{0,2},{1,3},{2,0},{3,1},{4,6},{5,7},{6,4},{7,5},{8,10},{9,11},{10,... | collective-permute-start | bytes 18440 | tf_op jit(solution)/shard_map/ppermute | solution.py:23
  10.4 5.1 %collective-permute-start.20 = (bf16[1,2,1,512]{3,2,1,0:T(2,128)(2,1)S(1)}, bf16[1,2,1,512]{3,2,1,0:T(2,128)(2,1)S(1)}, u32[]{:S(2)}, u32[]{:S(2)}) collective-permute-start(bf16[1,2,1,512]{3,2,1,0:T(2,128)(2,1)S(1)} %constant_dynamic-update-slice_fusion.refs_0_), channel_id=1, source_target_pairs={{0,192},{1,193},{2,66},{3,67},{4,196},{5,197},{6,70},{7,71},{8,200... | collective-permute-start | bytes 6152 | tf_op jit(solution)/shard_map/ppermute | solution.py:211
  15.5 9.2 %collective-permute-start.21 = (bf16[1,2,1,512]{3,2,1,0:T(2,128)(2,1)S(1)}, bf16[1,2,1,512]{3,2,1,0:T(2,128)(2,1)S(1)}, u32[]{:S(2)}, u32[]{:S(2)}) collective-permute-start(bf16[1,2,1,512]{3,2,1,0:T(2,128)(2,1)S(1)} %collective-permute-done.20.refs_1_), channel_id=1, source_target_pairs={{0,192},{1,193},{2,66},{3,67},{4,196},{5,197},{6,70},{7,71},{8,200... | collective-permute-start | bytes 6152 | tf_op jit(solution)/shard_map/ppermute | solution.py:211
  21.7 10.4 %collective-permute-start.9 = (f32[1,1024]{1,0:T(1,128)S(1)}, f32[1,1024]{1,0:T(1,128)S(1)}, u32[]{:S(2)}, u32[]{:S(2)}) collective-permute-start(f32[1,1024]{1,0:T(1,128)S(1)} %get-tuple-element.28), channel_id=1, source_target_pairs={{0,1},{1,0},{2,3},{3,2},{4,5},{5,4},{6,7},{7,6},{8,9},{9,8},{10,11... | collective-permute-start | bytes 12296 | tf_op jit(solution)/shard_map/ppermute | solution.py:23
  24.7 3.4 %collective-permute-start.22 = (bf16[1,2,1,512]{3,2,1,0:T(2,128)(2,1)S(1)}, bf16[1,2,1,512]{3,2,1,0:T(2,128)(2,1)S(1)}, u32[]{:S(2)}, u32[]{:S(2)}) collective-permute-start(bf16[1,2,1,512]{3,2,1,0:T(2,128)(2,1)S(1)} %collective-permute-done.21.refs_2_), channel_id=1, source_target_pairs={{0,192},{1,193},{2,66},{3,67},{4,196},{5,197},{6,70},{7,71},{8,200... | collective-permute-start | bytes 6152 | tf_op jit(solution)/shard_map/ppermute | solution.py:211
  28.1 4.1 %collective-permute-start.23 = (bf16[4,2,1,512]{3,2,1,0:T(2,128)(2,1)S(1)}, bf16[4,2,1,512]{3,2,1,0:T(2,128)(2,1)S(1)}, u32[]{:S(2)}, u32[]{:S(2)}) collective-permute-start(bf16[4,2,1,512]{3,2,1,0:T(2,128)(2,1)S(1)} %shard_map.119), channel_id=1, source_target_pairs={{0,4},{4,0},{8,12},{12,8},{16,20},{20,16},{24,28},{28,24},{32,36},... | collective-permute-start | bytes 24584 | tf_op jit(solution)/shard_map/ppermute | solution.py:23
  29.4 4.1 %collective-permute-start.24 = (bf16[4,2,1,512]{3,2,1,0:T(2,128)(2,1)S(1)}, bf16[4,2,1,512]{3,2,1,0:T(2,128)(2,1)S(1)}, u32[]{:S(2)}, u32[]{:S(2)}) collective-permute-start(bf16[4,2,1,512]{3,2,1,0:T(2,128)(2,1)S(1)} %shard_map.119), channel_id=1, source_target_pairs={{0,8},{4,12},{8,0},{12,4},{16,24},{20,28},{24,16},{28,20},{32,40},... | collective-permute-start | bytes 24584 | tf_op jit(solution)/shard_map/ppermute | solution.py:23
  31.8 3.9 %collective-permute-start.25 = (bf16[4,2,1,512]{3,2,1,0:T(2,128)(2,1)S(1)}, bf16[4,2,1,512]{3,2,1,0:T(2,128)(2,1)S(1)}, u32[]{:S(2)}, u32[]{:S(2)}) collective-permute-start(bf16[4,2,1,512]{3,2,1,0:T(2,128)(2,1)S(1)} %shard_map.119), channel_id=1, source_target_pairs={{0,12},{4,8},{8,4},{12,0},{16,28},{20,24},{24,20},{28,16},{32,44},... | collective-permute-start | bytes 24584 | tf_op jit(solution)/shard_map/ppermute | solution.py:23
  32.1 8.0 %collective-permute-start.10 = (f32[1,1024]{1,0:T(1,128)S(1)}, f32[1,1024]{1,0:T(1,128)S(1)}, u32[]{:S(2)}, u32[]{:S(2)}) collective-permute-start(f32[1,1024]{1,0:T(1,128)S(1)} %add.13.pair_ref), channel_id=1, source_target_pairs={{0,2},{1,3},{2,0},{3,1},{4,6},{5,7},{6,4},{7,5},{8,10},{9,11},{10,... | collective-permute-start | bytes 12296 | tf_op jit(solution)/shard_map/ppermute | solution.py:23
  36.0 9.2 %collective-permute-start.26 = (bf16[4,2,4,512]{3,2,1,0:T(4,128)(2,1)S(1)}, bf16[4,2,4,512]{3,2,1,0:T(4,128)(2,1)S(1)}, u32[]{:S(2)}, u32[]{:S(2)}) collective-permute-start(bf16[4,2,4,512]{3,2,1,0:T(4,128)(2,1)S(1)} %pad_maximum_fusion.3), channel_id=1, source_target_pairs={{0,16},{4,20},{8,24},{12,28},{16,0},{20,4},{24,8},{28,12},{32,48},... | collective-permute-start | bytes 98312 | tf_op jit(solution)/shard_map/ppermute | solution.py:23
  37.4 8.4 %collective-permute-start.27 = (bf16[4,2,4,512]{3,2,1,0:T(4,128)(2,1)S(1)}, bf16[4,2,4,512]{3,2,1,0:T(4,128)(2,1)S(1)}, u32[]{:S(2)}, u32[]{:S(2)}) collective-permute-start(bf16[4,2,4,512]{3,2,1,0:T(4,128)(2,1)S(1)} %pad_maximum_fusion.3), channel_id=1, source_target_pairs={{0,32},{4,36},{8,40},{12,44},{16,48},{20,52},{24,56},{28,60},{32,0... | collective-permute-start | bytes 98312 | tf_op jit(solution)/shard_map/ppermute | solution.py:23
  40.0 6.8 %collective-permute-start.28 = (bf16[4,2,4,512]{3,2,1,0:T(4,128)(2,1)S(1)}, bf16[4,2,4,512]{3,2,1,0:T(4,128)(2,1)S(1)}, u32[]{:S(2)}, u32[]{:S(2)}) collective-permute-start(bf16[4,2,4,512]{3,2,1,0:T(4,128)(2,1)S(1)} %pad_maximum_fusion.3), channel_id=1, source_target_pairs={{0,48},{4,52},{8,56},{12,60},{16,32},{20,36},{24,40},{28,44},{32,1... | collective-permute-start | bytes 98312 | tf_op jit(solution)/shard_map/ppermute | solution.py:23
  40.2 32.9 %collective-permute-start.16 = (bf16[1,256,1024]{2,1,0:T(8,128)(2,1)S(1)}, bf16[1,256,1024]{2,1,0:T(8,128)(2,1)S(1)}, u32[]{:S(2)}, u32[]{:S(2)}) collective-permute-start(bf16[1,256,1024]{2,1,0:T(8,128)(2,1)S(1)} %get-tuple-element.32), channel_id=1, source_target_pairs={{0,2},{1,3},{2,0},{3,1},{4,6},{5,7},{6,4},{7,5},{8,10},{9,11},{10,... | collective-permute-start | bytes 1572872 | tf_op jit(solution)/shard_map/ppermute | solution.py:23
  40.3 54.7 %collective-permute-start.15 = (bf16[1,512,1024]{2,1,0:T(8,128)(2,1)S(1)}, bf16[1,512,1024]{2,1,0:T(8,128)(2,1)S(1)}, u32[]{:S(2)}, u32[]{:S(2)}) collective-permute-start(bf16[1,512,1024]{2,1,0:T(8,128)(2,1)S(1)} %get-tuple-element.31.refs_0_), channel_id=1, source_target_pairs={{0,1},{1,0},{2,3},{3,2},{4,5},{5,4},{6,7},{7,6},{8,9},{9,8},{10,11... | collective-permute-start | bytes 3145736 | tf_op jit(solution)/shard_map/ppermute | solution.py:23
  45.2 25.9 %collective-permute-start.18 = (bf16[1,128,1024]{2,1,0:T(8,128)(2,1)S(1)}, bf16[1,128,1024]{2,1,0:T(8,128)(2,1)S(1)}, u32[]{:S(2)}, u32[]{:S(2)}) collective-permute-start(bf16[1,128,1024]{2,1,0:T(8,128)(2,1)S(1)} %get-tuple-element.33), channel_id=1, source_target_pairs={{0,2},{1,3},{2,0},{3,1},{4,6},{5,7},{6,4},{7,5},{8,10},{9,11},{10,... | collective-permute-start | bytes 786440 | tf_op jit(solution)/shard_map/ppermute | solution.py:23
  45.8 12.8 %collective-permute-start.11 = (bf16[1,64,1024]{2,1,0:T(8,128)(2,1)S(1)}, bf16[1,64,1024]{2,1,0:T(8,128)(2,1)S(1)}, u32[]{:S(2)}, u32[]{:S(2)}) collective-permute-start(bf16[1,64,1024]{2,1,0:T(8,128)(2,1)S(1)} %get-tuple-element.29), channel_id=1, source_target_pairs={{0,2},{1,3},{2,0},{3,1},{4,6},{5,7},{6,4},{7,5},{8,10},{9,11},{10,... | collective-permute-start | bytes 393224 | tf_op jit(solution)/shard_map/ppermute | solution.py:23
  46.8 14.6 %collective-permute-start.13 = (bf16[1,64,1024]{2,1,0:T(8,128)(2,1)S(1)}, bf16[1,64,1024]{2,1,0:T(8,128)(2,1)S(1)}, u32[]{:S(2)}, u32[]{:S(2)}) collective-permute-start(bf16[1,64,1024]{2,1,0:T(8,128)(2,1)S(1)} %get-tuple-element.30), channel_id=1, source_target_pairs={{0,2},{1,3},{2,0},{3,1},{4,6},{5,7},{6,4},{7,5},{8,10},{9,11},{10,... | collective-permute-start | bytes 393224 | tf_op jit(solution)/shard_map/ppermute | solution.py:23
  58.6 8.7 %collective-permute-start.3 = (bf16[1,64,1024]{2,1,0:T(8,128)(2,1)S(1)}, bf16[1,64,1024]{2,1,0:T(8,128)(2,1)S(1)}, u32[]{:S(2)}, u32[]{:S(2)}) collective-permute-start(bf16[1,64,1024]{2,1,0:T(8,128)(2,1)S(1)} %shard_map.112), channel_id=1, source_target_pairs={{0,2},{1,3},{2,0},{3,1},{4,6},{5,7},{6,4},{7,5},{8,10},{9,11},{10,... | collective-permute-start | bytes 393224 | tf_op jit(solution)/shard_map/ppermute | solution.py:23
  61.4 9.6 %collective-permute-start.29 = (bf16[4,2,16,512]{3,2,1,0:T(8,128)(2,1)S(1)}, bf16[4,2,16,512]{3,2,1,0:T(8,128)(2,1)S(1)}, u32[]{:S(2)}, u32[]{:S(2)}) collective-permute-start(bf16[4,2,16,512]{3,2,1,0:T(8,128)(2,1)S(1)} %pad_maximum_fusion.own_ref), channel_id=1, source_target_pairs={{0,1},{1,0},{2,3},{3,2},{4,5},{5,4},{6,7},{7,6},{8,9},{9,8},{10,11... | collective-permute-start | bytes 393224 | tf_op jit(solution)/shard_map/ppermute | solution.py:23
  67.3 5.3 %collective-permute-start.12 = (bf16[1,64,1024]{2,1,0:T(8,128)(2,1)S(1)}, bf16[1,64,1024]{2,1,0:T(8,128)(2,1)S(1)}, u32[]{:S(2)}, u32[]{:S(2)}) collective-permute-start(bf16[1,64,1024]{2,1,0:T(8,128)(2,1)S(1)} %collective-permute-done.11.refs_0_), channel_id=1, source_target_pairs={{0,1},{1,0},{2,3},{3,2},{4,5},{5,4},{6,7},{7,6},{8,9},{9,8},{10,11... | collective-permute-start | bytes 393224 | tf_op jit(solution)/shard_map/ppermute | solution.py:23
  71.0 10.8 %collective-permute-start.5 = (bf16[1,192,1024]{2,1,0:T(8,128)(2,1)S(1)}, bf16[1,192,1024]{2,1,0:T(8,128)(2,1)S(1)}, u32[]{:S(2)}, u32[]{:S(2)}) collective-permute-start(bf16[1,192,1024]{2,1,0:T(8,128)(2,1)S(1)} %get-tuple-element.25), channel_id=1, source_target_pairs={{0,2},{1,3},{2,0},{3,1},{4,6},{5,7},{6,4},{7,5},{8,10},{9,11},{10,... | collective-permute-start | bytes 1179656 | tf_op jit(solution)/shard_map/ppermute | solution.py:23
  71.1 21.9 %collective-permute-start.7 = (bf16[1,256,1024]{2,1,0:T(8,128)(2,1)S(1)}, bf16[1,256,1024]{2,1,0:T(8,128)(2,1)S(1)}, u32[]{:S(2)}, u32[]{:S(2)}) collective-permute-start(bf16[1,256,1024]{2,1,0:T(8,128)(2,1)S(1)} %get-tuple-element.26), channel_id=1, source_target_pairs={{0,2},{1,3},{2,0},{3,1},{4,6},{5,7},{6,4},{7,5},{8,10},{9,11},{10,... | collective-permute-start | bytes 1572872 | tf_op jit(solution)/shard_map/ppermute | solution.py:23
  72.5 26.6 %collective-permute-start.2 = (bf16[1,512,1024]{2,1,0:T(8,128)(2,1)S(1)}, bf16[1,512,1024]{2,1,0:T(8,128)(2,1)S(1)}, u32[]{:S(2)}, u32[]{:S(2)}) collective-permute-start(bf16[1,512,1024]{2,1,0:T(8,128)(2,1)S(1)} %get-tuple-element.24.refs_0_), channel_id=1, source_target_pairs={{0,1},{1,0},{2,3},{3,2},{4,5},{5,4},{6,7},{7,6},{8,9},{9,8},{10,11... | collective-permute-start | bytes 3145736 | tf_op jit(solution)/shard_map/ppermute | solution.py:23
  73.1 21.3 %collective-permute-start.17 = (bf16[1,256,1024]{2,1,0:T(8,128)(2,1)S(1)}, bf16[1,256,1024]{2,1,0:T(8,128)(2,1)S(1)}, u32[]{:S(2)}, u32[]{:S(2)}) collective-permute-start(bf16[1,256,1024]{2,1,0:T(8,128)(2,1)S(1)} %collective-permute-done.16.refs_2_), channel_id=1, source_target_pairs={{0,1},{1,0},{2,3},{3,2},{4,5},{5,4},{6,7},{7,6},{8,9},{9,8},{10,11... | collective-permute-start | bytes 1572872 | tf_op jit(solution)/shard_map/ppermute | solution.py:23
  81.7 12.1 %collective-permute-start.19 = (bf16[1,128,1024]{2,1,0:T(8,128)(2,1)S(1)}, bf16[1,128,1024]{2,1,0:T(8,128)(2,1)S(1)}, u32[]{:S(2)}, u32[]{:S(2)}) collective-permute-start(bf16[1,128,1024]{2,1,0:T(8,128)(2,1)S(1)} %collective-permute-done.18.refs_4_), channel_id=1, source_target_pairs={{0,1},{1,0},{2,3},{3,2},{4,5},{5,4},{6,7},{7,6},{8,9},{9,8},{10,11... | collective-permute-start | bytes 786440 | tf_op jit(solution)/shard_map/ppermute | solution.py:23
  93.0 6.2 %collective-permute-start.8 = (bf16[1,256,1024]{2,1,0:T(8,128)(2,1)S(1)}, bf16[1,256,1024]{2,1,0:T(8,128)(2,1)S(1)}, u32[]{:S(2)}, u32[]{:S(2)}) collective-permute-start(bf16[1,256,1024]{2,1,0:T(8,128)(2,1)S(1)} %collective-permute-done.7.refs_6_), channel_id=1, source_target_pairs={{0,1},{1,0},{2,3},{3,2},{4,5},{5,4},{6,7},{7,6},{8,9},{9,8},{10,11... | collective-permute-start | bytes 1572872 | tf_op jit(solution)/shard_map/ppermute | solution.py:23
  93.8 5.3 %collective-permute-start.6 = (bf16[1,192,1024]{2,1,0:T(8,128)(2,1)S(1)}, bf16[1,192,1024]{2,1,0:T(8,128)(2,1)S(1)}, u32[]{:S(2)}, u32[]{:S(2)}) collective-permute-start(bf16[1,192,1024]{2,1,0:T(8,128)(2,1)S(1)} %collective-permute-done.5.refs_4_), channel_id=1, source_target_pairs={{0,1},{1,0},{2,3},{3,2},{4,5},{5,4},{6,7},{7,6},{8,9},{9,8},{10,11... | collective-permute-start | bytes 1179656 | tf_op jit(solution)/shard_map/ppermute | solution.py:23
  94.5 3.8 %collective-permute-start.14 = (bf16[1,64,1024]{2,1,0:T(8,128)(2,1)S(1)}, bf16[1,64,1024]{2,1,0:T(8,128)(2,1)S(1)}, u32[]{:S(2)}, u32[]{:S(2)}) collective-permute-start(bf16[1,64,1024]{2,1,0:T(8,128)(2,1)S(1)} %collective-permute-done.13.refs_2_), channel_id=1, source_target_pairs={{0,1},{1,0},{2,3},{3,2},{4,5},{5,4},{6,7},{7,6},{8,9},{9,8},{10,11... | collective-permute-start | bytes 393224 | tf_op jit(solution)/shard_map/ppermute | solution.py:23
  95.0 4.2 %collective-permute-start.4 = (bf16[1,64,1024]{2,1,0:T(8,128)(2,1)S(1)}, bf16[1,64,1024]{2,1,0:T(8,128)(2,1)S(1)}, u32[]{:S(2)}, u32[]{:S(2)}) collective-permute-start(bf16[1,64,1024]{2,1,0:T(8,128)(2,1)S(1)} %collective-permute-done.3.refs_2_), channel_id=1, source_target_pairs={{0,1},{1,0},{2,3},{3,2},{4,5},{5,4},{6,7},{7,6},{8,9},{9,8},{10,11... | collective-permute-start | bytes 393224 | tf_op jit(solution)/shard_map/ppermute | solution.py:23

commit v3 on v2

--- a/solution.py
+++ b/solution.py
@@ -34,8 +34,9 @@
     )
 
 
-def mean_body(share_ref, w_ref, avg_ref, fresh_ref, sums_ref, w_buf, avg_buf, sem):
-    rows = w_buf.shape[0]
+def mean_body(extras, share_ref, w_ref, avg_ref, *refs):
+    extra_refs, (fresh_ref, sums_ref, w_buf, avg_buf, extra_buf, sem, extra_sem) = refs[:extras], refs[extras:]
+    rows, columns = w_buf.shape
     step = rows // LOADS
 
     def copies(k):
@@ -45,12 +46,16 @@
             pltpu.make_async_copy(avg_ref.at[0, at], avg_buf.at[at], sem.at[1, k]),
         )
 
+    extra = [pltpu.make_async_copy(r, extra_buf.at[k], extra_sem.at[k]) for k, r in enumerate(extra_refs)]
     for k in range(LOADS):
         for c in copies(k):
             c.start()
+        if k == 0:
+            for c in extra:
+                c.start()
     share = share_ref[0]
     rest = 1.0 - share
-    total = jnp.zeros((8, w_buf.shape[1]), jnp.float32)
+    total = jnp.zeros((8, columns), jnp.float32)
     for k in range(LOADS):
         for c in copies(k):
             c.wait()
@@ -62,29 +67,46 @@
             return total + fresh * fresh
 
         total = lax.fori_loop(0, step // 8, tile, total, unroll=True)
-    sums_ref[...] = jnp.sum(total, axis=0, keepdims=True)
-
-
-def mean_of(share, w, avg, mib):
+    sums_ref[:, pl.ds(0, columns)] = jnp.sum(total, axis=0, keepdims=True)
+    if extras:
+        for c in extra:
+            c.wait()
+        product = (extra_buf[0] * extra_buf[1]).astype(jnp.bfloat16).astype(jnp.float32)
+        sums_ref[:, pl.ds(columns, rows)] = product
+
+
+def mean_of(share, w, avg, mib, *extra):
     _, rows, columns = w.shape
+    n = len(extra)
     return call(
-        mean_body,
-        (pltpu.VMEM((rows, columns), jnp.float32), pltpu.VMEM((1, columns), jnp.float32)),
-        [SMEM, HBM, HBM],
+        functools.partial(mean_body, n),
+        (
+            pltpu.VMEM((rows, columns), jnp.float32),
+            pltpu.VMEM((1, columns + (rows if n else 0)), jnp.float32),
+        ),
+        [SMEM] + [HBM] * (2 + n),
         mib,
         4 << 20,
         out_specs=(VMEM, VMEM),
         scratch_shapes=[
             pltpu.VMEM((rows, columns), jnp.float32),
             pltpu.VMEM((rows, columns), jnp.float32),
+            pltpu.VMEM((2, 1, rows), jnp.float32),
             pltpu.SemaphoreType.DMA((2, LOADS)),
+            pltpu.SemaphoreType.DMA((2,)),
         ],
-    )(share, w, avg)
-
-
-def narrow_body(first, blocks, whole, fresh_ref, pair_ref, other_ref, *outs):
+    )(share, w, avg, *extra)
+
+
+def narrow_body(first, blocks, whole, scales, fresh_ref, *refs):
     columns = fresh_ref.shape[1]
-    inverse = 1.0 / jnp.sqrt(pair_ref[:, :columns] + other_ref[:, :columns])
+    totals, outs = refs[: 2 * max(scales, 1)], refs[2 * max(scales, 1) :]
+    scale = [jnp.sqrt(a[:, :columns] + b[:, :columns]) for a, b in zip(totals[::2], totals[1::2])]
+    inverse = 1.0 / scale[0]
+    if scales:
+        for value, out in zip(scale, outs[-scales:]):
+            out[...] = value
+        outs = outs[:-scales]
 
     def rows_of(at):
         return (fresh_ref[pl.ds(at, 16)] * inverse).astype(jnp.bfloat16)
@@ -102,14 +124,15 @@
         at += rows
 
 
-def narrow(fresh, totals, first, blocks, whole):
+def narrow(fresh, totals, first, blocks, whole, scales=0):
     rows, columns = fresh.shape
     sizes = [*blocks, rows] if whole else blocks
-    outs = tuple(pltpu.VMEM((1, n, columns), jnp.bfloat16) for n in sizes)
+    outs = [pltpu.VMEM((1, n, columns), jnp.bfloat16) for n in sizes]
+    outs += [jax.ShapeDtypeStruct((1, columns), jnp.float32)] * scales
     return call(
-        functools.partial(narrow_body, first, blocks, whole),
-        outs,
-        [VMEM, VMEM, VMEM],
+        functools.partial(narrow_body, first, blocks, whole, scales),
+        tuple(outs),
+        [VMEM] * (1 + len(totals)),
         2,
         2 << 20,
         out_specs=(VMEM,) * len(outs),
@@ -163,7 +186,7 @@
     return near, far
 
 
-BITS = (("shard", CHIP), ("expert", 1), ("expert", 2), ("expert", 4), ("expert", 8))
+BITS = (("shard", CORE), ("shard", CHIP), ("expert", 1), ("expert", 2), ("expert", 4), ("expert", 8))
 
 
 def lows_body(*outs):
@@ -172,10 +195,10 @@
         out[...] = jnp.full(out.shape, low, jnp.float32)
 
 
-def lows_of(rows):
+def lows_of(rows, both):
     outs = call(
         lows_body,
-        tuple(jax.ShapeDtypeStruct((1, rows), jnp.float32) for _ in BITS),
+        tuple(jax.ShapeDtypeStruct((1, rows if b == BITS[0] else both), jnp.float32) for b in BITS),
         [],
         1,
         1 << 10,
@@ -191,24 +214,25 @@
 
 def router_body(own_ref, other_ref, out_ref):
     z, chips, plane, rows = own_ref.shape
-    first = (lax.axis_index("shard") & CORE) == 0
+    made = (lax.axis_index("shard") & CORE) == CORE
     for k in range(z):
         for chip in range(chips):
-            own, other = own_ref[k, chip], other_ref[k, chip]
-            for core in range(2):
-                at = (chip * 2 + core) * rows
-                value = jnp.where(first, own, other) if core == 0 else jnp.where(first, other, own)
-                out_ref[pl.ds(k * plane, plane), pl.ds(at, rows)] = value
-
-
-def turned(x):
+            value = jnp.where(made, own_ref[k, chip], other_ref[k, chip])
+            out_ref[pl.ds(k * plane, plane), pl.ds(chip * rows, rows)] = value
+
+
+def sent(x, to):
     experts, shards = lax.axis_size("expert"), lax.axis_size("shard")
     pairs = []
     for e in range(experts):
-        for s in range(shards):
-            to = (e + (16 if s & CHIP else -16)) % experts
-            pairs.append((e * shards + s, to * shards + s))
+        for s in range(CORE, shards, 2):
+            f, t = to(e, s)
+            pairs.append((e * shards + s, f % experts * shards + t))
     return lax.ppermute(x, ("expert", "shard"), pairs)
+
+
+def turned(x):
+    return sent(x, lambda e, s: (e + (16 if s & CHIP else -16), s))
 
 
 def planes_body(*refs):
@@ -224,45 +248,29 @@
         pieces.append(turned(pieces[-1]))
     x = pieces[0]
     x = call(
-        planes_body,
-        jax.ShapeDtypeStruct((4, *x.shape[1:]), x.dtype),
-        [VMEM] * 4,
-        1,
-        1 << 10,
-        out_specs=VMEM,
+        planes_body, jax.ShapeDtypeStruct((4, *x.shape[1:]), x.dtype), [VMEM] * 4, 1, 1 << 10, out_specs=VMEM
     )(*pieces)
     for unit in (1, 4):
-        a, b, c = (swap(x, "expert", unit * k) for k in (1, 2, 3))
+        a, b, c = (sent(x, lambda e, s, k=k: (e ^ unit * k, s)) for k in (1, 2, 3))
         low = lows["expert", unit]
         x = in_order(lows["expert", 2 * unit], in_order(low, x, a, 2), in_order(low, b, c, 2), 2)
-    other = swap(x, "shard", CORE)
+    other = sent(x, lambda e, s: (e, s ^ CORE))
     z, chips, plane, rows = x.shape
     return call(
-        router_body,
-        jax.ShapeDtypeStruct((z * plane, chips * 2 * rows), x.dtype),
-        [VMEM, VMEM],
-        2,
-        1 << 20,
-        out_specs=VMEM,
+        router_body, jax.ShapeDtypeStruct((z * plane, chips * rows), x.dtype), [VMEM, VMEM], 2, 1 << 20, out_specs=VMEM
     )(x, other).T
-
-
-def scale_of(totals, columns):
-    pair, other = totals
-    return jnp.sqrt(pair[:, :columns] + other[:, :columns])
 
 
 def per_device(w_gate, avg_gate, w_up, avg_up, mix_share, router_weight, router_gain):
     rows, columns = w_gate.shape[1:]
     shape = (1, lax.axis_size("shard") * rows, columns)
-    part = (router_weight.T * router_gain[None]).astype(jnp.bfloat16)
-    lows = lows_of(rows)
-
-    fresh_gate, sums_gate = mean_of(mix_share, w_gate, avg_gate, 60)
-    pair = sums_gate + swap(sums_gate, "shard", CORE)
-    pair = jnp.concatenate([pair, part.astype(jnp.float32)], axis=1)
+    lows = lows_of(rows, 2 * rows)
+
+    fresh_gate, mine = mean_of(mix_share, w_gate, avg_gate, 60, router_weight.T, router_gain[None])
+    near = swap(mine, "shard", CORE)
+    router = in_order(lows["shard", CORE], mine[:, columns:], near[:, columns:], 1)
+    pair = jnp.concatenate([mine[:, :columns] + near[:, :columns], router], axis=1)
     totals_gate = pair, swap(pair, "shard", CHIP)
-    scale_gate = scale_of(totals_gate, columns)
     gate = narrow(fresh_gate, totals_gate, 0, GATE[:1], False)
     *rest, whole = narrow(fresh_gate, totals_gate, GATE[0], GATE[1:], True)
     near, far = from_all([*gate, *rest], whole)
@@ -271,14 +279,13 @@
     fresh_up, sums_up = mean_of(mix_share, w_up, avg_up, 56)
     pair = sums_up + swap(sums_up, "shard", CORE)
     totals_up = pair, swap(pair, "shard", CHIP)
-    scale_up = scale_of(totals_up, columns)
-    *up, whole = narrow(fresh_up, totals_up, 0, UP, True)
+    *up, whole, scale_up, scale_gate = narrow(fresh_up, totals_up + totals_gate, 0, UP, True, scales=2)
     near, far = from_all(up, whole)
     serve_up = place(sum(far[:2], near), rows, shape)
     serve_up = place(sum(far[2:], []), rows, shape, serve_up)
 
     other = totals_gate[1][:, columns:].astype(jnp.bfloat16)
-    serve_router = router_of(lows, part, other)
+    serve_router = router_of(lows, router.astype(jnp.bfloat16), other)
     return (serve_gate, serve_up, scale_gate, scale_up, serve_router)
 
 

time: 102 us -> 96.9 us (0.950)
  waiting for transfers between devices: 43.4 us -> 35.2 us
  starting transfers between devices: 44 us -> 47.7 us
    ppermute x3 -> x10, starting transfers between devices: 8.2 us -> 36.5 us  [sent(): return lax.ppermute(x, ('expert', 'shard'), pairs)]
    ppermute x27 -> x20, starting transfers between devices: 35.8 us -> 11.2 us  [swap(): return lax.ppermute(x, axis, [(i, i ^ mask) for i in range(n)])]
    ppermute x27 -> x20, waiting for transfers between devices: 39.3 us -> 29.6 us  [swap(): return lax.ppermute(x, axis, [(i, i ^ mask) for i in range(n)])]
    ppermute x3 -> x10, waiting for transfers between devices: 4.09 us -> 5.61 us  [sent(): return lax.ppermute(x, ('expert', 'shard'), pairs)]
    sqrt x2 -> x0, other arithmetic: 1.21 us -> none  [scale_of(): return jnp.sqrt(pair[:, :columns] + other[:, :columns])]
  transfers between devices with their start and end apart: 30 -> 30, of which waited for: 10 -> 12; matrix products, arithmetic and copies ran while one was open for 2% -> 1% of each run, Pallas kernels for 6% -> 7%
where the time goes in v3:
time: 96.9 us; the launch traced here: 96.5 us
  starting transfers between devices  47.7 us (49%)
  waiting for transfers between devices  35.2 us (36%)
  Pallas kernels  11.2 us (12%)
  between operations  1.6 us (2%)
    ppermute x10, starting transfers between devices, sent(): return lax.ppermute(x, ('expert', 'shard'), pairs)  36.5 us
    ppermute x20, waiting for transfers between devices, swap(): return lax.ppermute(x, axis, [(i, i ^ mask) for i in range(n)])  29.6 us
    ppermute x20, starting transfers between devices, swap(): return lax.ppermute(x, axis, [(i, i ^ mask) for i in range(n)])  11.2 us
    ppermute x10, waiting for transfers between devices, sent(): return lax.ppermute(x, ('expert', 'shard'), pairs)  5.61 us
    pallas_call x3, Pallas kernels, place(): call(functools.partial(place_body, places), jax.ShapeDtypeStruct(shape, b...  4.79 us
    pallas_call x2, Pallas kernels, mean_of(): call(functools.partial(mean_body, n), (pltpu.VMEM((rows, columns), jnp.fl...  4.73 us
  transfers between devices with their start and end apart: 30, of which 12 were waited for; matrix products, arithmetic and copies ran while one was open for 1% of the time, Pallas kernels for 7%

profile of v3, /device:TPU:1, one launch (start us, length us, event | category | flops | bytes accessed | tf_op | source)
XLA Modules:
  0.0 96.5 jit_solution(17983385630682718829)
XLA Ops:
  1.3 2.4 %shard_map.110 = (f32[512,1024]{1,0:T(8,128)S(1)}, f32[1,1536]{1,0:T(1,128)S(1)}) custom-call(f32[1]{0:T(128)S(6)} %copy.14.share_ref, f32[1,512,1024]{2,1,0:T(8,128)} %w_ref.2, f32[1,512,1024]{2,1,0:T(8,128)} %avg_ref.2, f32[1,512]{1,0:T(1,128)} %bitcast.17, f32[1,512]{1,0:T(1,128)} %bitcast.18), custom_call_target="tpu_custom_call" | custom-call | flops 4194304 | bytes 4194304 | tf_op jit(solution)/shard_map/pallas_call | solution.py:81
  3.7 3.3 %collective-permute-start = (f32[1,1536]{1,0:T(1,128)S(1)}, f32[1,1536]{1,0:T(1,128)S(1)}, u32[]{:S(2)}, u32[]{:S(2)}) collective-permute-start(f32[1,1536]{1,0:T(1,128)S(1)} %get-tuple-element.26), channel_id=1, source_target_pairs={{0,1},{1,0},{2,3},{3,2},{4,5},{5,4},{6,7},{7,6},{8,9},{9,8},{10,11... | collective-permute-start | bytes 18440 | tf_op jit(solution)/shard_map/ppermute | solution.py:23
  7.0 0.8 collective-permute-done
  7.8 0.1 collective-permute-start.1
  7.9 2.5 %collective-permute-done.1.refs_1_.refs_3_ = f32[1,2048]{1,0:T(1,128)S(1)} collective-permute-done((f32[1,2048]{1,0:T(1,128)S(1)}, f32[1,2048]{1,0:T(1,128)S(1)}, u32[]{:S(2)}, u32[]{:S(2)}) %collective-permute-start.1) | collective-permute-done | bytes 8224 | tf_op jit(solution)/shard_map/ppermute | solution.py:23
  10.4 6.2 %collective-permute-start.20 = (bf16[1,2,1,1024]{3,2,1,0:T(2,128)(2,1)S(1)}, bf16[1,2,1,1024]{3,2,1,0:T(2,128)(2,1)S(1)}, u32[]{:S(2)}, u32[]{:S(2)}) collective-permute-start(bf16[1,2,1,1024]{3,2,1,0:T(2,128)(2,1)S(1)} %pad_maximum_fusion.7.refs_0_), channel_id=1, source_target_pairs={{1,193},{3,67},{5,197},{7,71},{9,201},{11,75},{13,205},{15,79},{17... | collective-permute-start | bytes 12296 | tf_op jit(solution)/shard_map/ppermute | solution.py:231
  16.7 0.8 collective-permute-done.20.refs_1_
  17.4 5.7 %collective-permute-start.21 = (bf16[1,2,1,1024]{3,2,1,0:T(2,128)(2,1)S(1)}, bf16[1,2,1,1024]{3,2,1,0:T(2,128)(2,1)S(1)}, u32[]{:S(2)}, u32[]{:S(2)}) collective-permute-start(bf16[1,2,1,1024]{3,2,1,0:T(2,128)(2,1)S(1)} %collective-permute-done.20.refs_1_), channel_id=1, source_target_pairs={{1,193},{3,67},{5,197},{7,71},{9,201},{11,75},{13,205},{15,79},{17... | collective-permute-start | bytes 12296 | tf_op jit(solution)/shard_map/ppermute | solution.py:231
  23.2 2.4 %shard_map.115 = (f32[512,1024]{1,0:T(8,128)S(1)}, f32[1,1024]{1,0:T(1,128)S(1)}) custom-call(f32[1]{0:T(128)S(6)} %copy.14.share_ref, f32[1,512,1024]{2,1,0:T(8,128)} %w_ref.3, f32[1,512,1024]{2,1,0:T(8,128)} %avg_ref.3), custom_call_target="tpu_custom_call" | custom-call | flops 4194304 | bytes 4194304 | tf_op jit(solution)/shard_map/pallas_call | solution.py:81
  25.5 0.1 collective-permute-start.9
  25.6 4.0 %collective-permute-start.22 = (bf16[1,2,1,1024]{3,2,1,0:T(2,128)(2,1)S(1)}, bf16[1,2,1,1024]{3,2,1,0:T(2,128)(2,1)S(1)}, u32[]{:S(2)}, u32[]{:S(2)}) collective-permute-start(bf16[1,2,1,1024]{3,2,1,0:T(2,128)(2,1)S(1)} %collective-permute-done.21.refs_2_), channel_id=1, source_target_pairs={{1,193},{3,67},{5,197},{7,71},{9,201},{11,75},{13,205},{15,79},{17... | collective-permute-start | bytes 12296 | tf_op jit(solution)/shard_map/ppermute | solution.py:231
  29.7 1.2 %collective-permute-done.22.refs_3_ = bf16[1,2,1,1024]{3,2,1,0:T(2,128)(2,1)S(1)} collective-permute-done((bf16[1,2,1,1024]{3,2,1,0:T(2,128)(2,1)S(1)}, bf16[1,2,1,1024]{3,2,1,0:T(2,128)(2,1)S(1)}, u32[]{:S(2)}, u32[]{:S(2)}) %collective-permute-start.22) | collective-permute-done | bytes 4128 | tf_op jit(solution)/shard_map/ppermute | solution.py:231
  31.0 3.1 %collective-permute-start.23 = (bf16[4,2,1,1024]{3,2,1,0:T(2,128)(2,1)S(1)}, bf16[4,2,1,1024]{3,2,1,0:T(2,128)(2,1)S(1)}, u32[]{:S(2)}, u32[]{:S(2)}) collective-permute-start(bf16[4,2,1,1024]{3,2,1,0:T(2,128)(2,1)S(1)} %shard_map.119), channel_id=1, source_target_pairs={{1,5},{3,7},{5,1},{7,3},{9,13},{11,15},{13,9},{15,11},{17,21},{19,... | collective-permute-start | bytes 49160 | tf_op jit(solution)/shard_map/ppermute | solution.py:231
  34.1 4.4 %collective-permute-start.24 = (bf16[4,2,1,1024]{3,2,1,0:T(2,128)(2,1)S(1)}, bf16[4,2,1,1024]{3,2,1,0:T(2,128)(2,1)S(1)}, u32[]{:S(2)}, u32[]{:S(2)}) collective-permute-start(bf16[4,2,1,1024]{3,2,1,0:T(2,128)(2,1)S(1)} %shard_map.119), channel_id=1, source_target_pairs={{1,9},{3,11},{5,13},{7,15},{9,1},{11,3},{13,5},{15,7},{17,25},{19,... | collective-permute-start | bytes 49160 | tf_op jit(solution)/shard_map/ppermute | solution.py:231
  38.5 2.1 %collective-permute-start.25 = (bf16[4,2,1,1024]{3,2,1,0:T(2,128)(2,1)S(1)}, bf16[4,2,1,1024]{3,2,1,0:T(2,128)(2,1)S(1)}, u32[]{:S(2)}, u32[]{:S(2)}) collective-permute-start(bf16[4,2,1,1024]{3,2,1,0:T(2,128)(2,1)S(1)} %shard_map.119), channel_id=1, source_target_pairs={{1,13},{3,15},{5,9},{7,11},{9,5},{11,7},{13,1},{15,3},{17,29},{19,... | collective-permute-start | bytes 49160 | tf_op jit(solution)/shard_map/ppermute | solution.py:231
  40.6 0.6 collective-permute-start.10
  41.2 3.1 %collective-permute-done.25 = bf16[4,2,1,1024]{3,2,1,0:T(2,128)(2,1)S(1)} collective-permute-done((bf16[4,2,1,1024]{3,2,1,0:T(2,128)(2,1)S(1)}, bf16[4,2,1,1024]{3,2,1,0:T(2,128)(2,1)S(1)}, u32[]{:S(2)}, u32[]{:S(2)}) %collective-permute-start.25) | collective-permute-done | bytes 16416 | tf_op jit(solution)/shard_map/ppermute | solution.py:231
  44.3 0.1 broadcast_select_fusion.5
  44.5 0.2 broadcast_select_fusion.7
  44.7 3.2 %collective-permute-start.26 = (bf16[4,2,4,1024]{3,2,1,0:T(4,128)(2,1)S(1)}, bf16[4,2,4,1024]{3,2,1,0:T(4,128)(2,1)S(1)}, u32[]{:S(2)}, u32[]{:S(2)}) collective-permute-start(bf16[4,2,4,1024]{3,2,1,0:T(4,128)(2,1)S(1)} %pad_maximum_fusion.3), channel_id=1, source_target_pairs={{1,17},{3,19},{5,21},{7,23},{9,25},{11,27},{13,29},{15,31},{17,1},... | collective-permute-start | bytes 196616 | tf_op jit(solution)/shard_map/ppermute | solution.py:231
  47.9 4.5 %collective-permute-start.27 = (bf16[4,2,4,1024]{3,2,1,0:T(4,128)(2,1)S(1)}, bf16[4,2,4,1024]{3,2,1,0:T(4,128)(2,1)S(1)}, u32[]{:S(2)}, u32[]{:S(2)}) collective-permute-start(bf16[4,2,4,1024]{3,2,1,0:T(4,128)(2,1)S(1)} %pad_maximum_fusion.3), channel_id=1, source_target_pairs={{1,33},{3,35},{5,37},{7,39},{9,41},{11,43},{13,45},{15,47},{17,49}... | collective-permute-start | bytes 196616 | tf_op jit(solution)/shard_map/ppermute | solution.py:231
  52.5 1.9 %collective-permute-start.28 = (bf16[4,2,4,1024]{3,2,1,0:T(4,128)(2,1)S(1)}, bf16[4,2,4,1024]{3,2,1,0:T(4,128)(2,1)S(1)}, u32[]{:S(2)}, u32[]{:S(2)}) collective-permute-start(bf16[4,2,4,1024]{3,2,1,0:T(4,128)(2,1)S(1)} %pad_maximum_fusion.3), channel_id=1, source_target_pairs={{1,49},{3,51},{5,53},{7,55},{9,57},{11,59},{13,61},{15,63},{17,33}... | collective-permute-start | bytes 196616 | tf_op jit(solution)/shard_map/ppermute | solution.py:231
  54.5 0.7 shard_map.116
  55.2 0.5 collective-permute-start.18
  55.7 1.0 %collective-permute-start.11 = (bf16[1,64,1024]{2,1,0:T(8,128)(2,1)S(1)}, bf16[1,64,1024]{2,1,0:T(8,128)(2,1)S(1)}, u32[]{:S(2)}, u32[]{:S(2)}) collective-permute-start(bf16[1,64,1024]{2,1,0:T(8,128)(2,1)S(1)} %get-tuple-element.33), channel_id=1, source_target_pairs={{0,2},{1,3},{2,0},{3,1},{4,6},{5,7},{6,4},{7,5},{8,10},{9,11},{10,... | collective-permute-start | bytes 393224 | tf_op jit(solution)/shard_map/ppermute | solution.py:23
  56.7 0.6 collective-permute-start.13
  57.3 1.0 %collective-permute-start.3 = (bf16[1,64,1024]{2,1,0:T(8,128)(2,1)S(1)}, bf16[1,64,1024]{2,1,0:T(8,128)(2,1)S(1)}, u32[]{:S(2)}, u32[]{:S(2)}) collective-permute-start(bf16[1,64,1024]{2,1,0:T(8,128)(2,1)S(1)} %shard_map.113), channel_id=1, source_target_pairs={{0,2},{1,3},{2,0},{3,1},{4,6},{5,7},{6,4},{7,5},{8,10},{9,11},{10,... | collective-permute-start | bytes 393224 | tf_op jit(solution)/shard_map/ppermute | solution.py:23
  58.2 0.5 collective-permute-done.28
  58.7 0.2 broadcast_select_fusion.11
  58.9 0.2 broadcast_select_fusion.1
  59.1 1.3 %collective-permute-start.29 = (bf16[4,2,16,1024]{3,2,1,0:T(8,128)(2,1)S(1)}, bf16[4,2,16,1024]{3,2,1,0:T(8,128)(2,1)S(1)}, u32[]{:S(2)}, u32[]{:S(2)}) collective-permute-start(bf16[4,2,16,1024]{3,2,1,0:T(8,128)(2,1)S(1)} %pad_maximum_fusion.own_ref), channel_id=1, source_target_pairs={{1,0},{3,2},{5,4},{7,6},{9,8},{11,10},{13,12},{15,14},{17,16},{19,... | collective-permute-start | bytes 786440 | tf_op jit(solution)/shard_map/ppermute | solution.py:231
  60.4 1.4 %collective-permute-done.11.refs_0_ = bf16[1,64,1024]{2,1,0:T(8,128)(2,1)S(1)} collective-permute-done((bf16[1,64,1024]{2,1,0:T(8,128)(2,1)S(1)}, bf16[1,64,1024]{2,1,0:T(8,128)(2,1)S(1)}, u32[]{:S(2)}, u32[]{:S(2)}) %collective-permute-start.11) | collective-permute-done | bytes 131104 | tf_op jit(solution)/shard_map/ppermute | solution.py:23
  61.8 0.5 collective-permute-start.16
  62.3 0.9 collective-permute-done.13.refs_2_
  63.2 1.4 %collective-permute-done.3.refs_2_ = bf16[1,64,1024]{2,1,0:T(8,128)(2,1)S(1)} collective-permute-done((bf16[1,64,1024]{2,1,0:T(8,128)(2,1)S(1)}, bf16[1,64,1024]{2,1,0:T(8,128)(2,1)S(1)}, u32[]{:S(2)}, u32[]{:S(2)}) %collective-permute-start.3) | collective-permute-done | bytes 131104 | tf_op jit(solution)/shard_map/ppermute | solution.py:23
  64.6 0.1 shard_map.112
  64.8 0.6 collective-permute-start.5
  65.4 1.0 %collective-permute-start.7 = (bf16[1,256,1024]{2,1,0:T(8,128)(2,1)S(1)}, bf16[1,256,1024]{2,1,0:T(8,128)(2,1)S(1)}, u32[]{:S(2)}, u32[]{:S(2)}) collective-permute-start(bf16[1,256,1024]{2,1,0:T(8,128)(2,1)S(1)} %get-tuple-element.30), channel_id=1, source_target_pairs={{0,2},{1,3},{2,0},{3,1},{4,6},{5,7},{6,4},{7,5},{8,10},{9,11},{10,... | collective-permute-start | bytes 1572872 | tf_op jit(solution)/shard_map/ppermute | solution.py:23
  66.3 1.1 %collective-permute-start.2 = (bf16[1,512,1024]{2,1,0:T(8,128)(2,1)S(1)}, bf16[1,512,1024]{2,1,0:T(8,128)(2,1)S(1)}, u32[]{:S(2)}, u32[]{:S(2)}) collective-permute-start(bf16[1,512,1024]{2,1,0:T(8,128)(2,1)S(1)} %get-tuple-element.28.refs_0_), channel_id=1, source_target_pairs={{0,1},{1,0},{2,3},{3,2},{4,5},{5,4},{6,7},{7,6},{8,9},{9,8},{10,11... | collective-permute-start | bytes 3145736 | tf_op jit(solution)/shard_map/ppermute | solution.py:23
  67.4 5.1 %collective-permute-done.16.refs_2_ = bf16[1,256,1024]{2,1,0:T(8,128)(2,1)S(1)} collective-permute-done((bf16[1,256,1024]{2,1,0:T(8,128)(2,1)S(1)}, bf16[1,256,1024]{2,1,0:T(8,128)(2,1)S(1)}, u32[]{:S(2)}, u32[]{:S(2)}) %collective-permute-start.16) | collective-permute-done | bytes 524320 | tf_op jit(solution)/shard_map/ppermute | solution.py:23
  72.5 8.4 %collective-permute-done.5.refs_4_ = bf16[1,192,1024]{2,1,0:T(8,128)(2,1)S(1)} collective-permute-done((bf16[1,192,1024]{2,1,0:T(8,128)(2,1)S(1)}, bf16[1,192,1024]{2,1,0:T(8,128)(2,1)S(1)}, u32[]{:S(2)}, u32[]{:S(2)}) %collective-permute-start.5) | collective-permute-done | bytes 393248 | tf_op jit(solution)/shard_map/ppermute | solution.py:23
  80.9 9.0 %collective-permute-done.7.refs_6_ = bf16[1,256,1024]{2,1,0:T(8,128)(2,1)S(1)} collective-permute-done((bf16[1,256,1024]{2,1,0:T(8,128)(2,1)S(1)}, bf16[1,256,1024]{2,1,0:T(8,128)(2,1)S(1)}, u32[]{:S(2)}, u32[]{:S(2)}) %collective-permute-start.7) | collective-permute-done | bytes 524320 | tf_op jit(solution)/shard_map/ppermute | solution.py:23
  89.9 0.5 collective-permute-start.6
  90.5 0.4 collective-permute-start.4
  90.9 0.7 shard_map.120
  91.7 1.9 %shard_map.117.refs_4_ = bf16[1,2048,1024]{2,1,0:T(8,128)(2,1)} custom-call(bf16[1,512,1024]{2,1,0:T(8,128)(2,1)S(1)} %get-tuple-element.35.refs_0_, bf16[1,512,1024]{2,1,0:T(8,128)(2,1)S(1)} %collective-permute-done.15.refs_1_, bf16[1,256,1024]{2,1,0:T(8,128)(2,1)S(1)} %collective-permute-done.16.refs_2_, ...), custom_call_target="tpu_custom_call" | custom-call | flops 1048576 | bytes 4194304 | tf_op jit(solution)/shard_map/pallas_call | solution.py:160
  93.5 0.8 shard_map.118
  94.4 2.1 %shard_map.114 = bf16[1,2048,1024]{2,1,0:T(8,128)(2,1)} custom-call(bf16[1,512,1024]{2,1,0:T(8,128)(2,1)S(1)} %get-tuple-element.28.refs_0_, bf16[1,512,1024]{2,1,0:T(8,128)(2,1)S(1)} %collective-permute-done.2.refs_1_, bf16[1,64,1024]{2,1,0:T(8,128)(2,1)S(1)} %collective-permute-done.3.refs_2_, bf16[1,64,1024]{2,1,0:T(8,128)(2,1)S(1)} %collective-permute-done.4.refs_3_, ...), custom_call_target="tpu_custom_call" | custom-call | flops 1048576 | bytes 4194304 | tf_op jit(solution)/shard_map/pallas_call | solution.py:160
  (38 shorter events, 0.5 us)
Async XLA Ops:
  3.7 4.1 %collective-permute-start = (f32[1,1536]{1,0:T(1,128)S(1)}, f32[1,1536]{1,0:T(1,128)S(1)}, u32[]{:S(2)}, u32[]{:S(2)}) collective-permute-start(f32[1,1536]{1,0:T(1,128)S(1)} %get-tuple-element.26), channel_id=1, source_target_pairs={{0,1},{1,0},{2,3},{3,2},{4,5},{5,4},{6,7},{7,6},{8,9},{9,8},{10,11... | collective-permute-start | bytes 18440 | tf_op jit(solution)/shard_map/ppermute | solution.py:23
  7.8 2.6 %collective-permute-start.1 = (f32[1,2048]{1,0:T(1,128)S(1)}, f32[1,2048]{1,0:T(1,128)S(1)}, u32[]{:S(2)}, u32[]{:S(2)}) collective-permute-start(f32[1,2048]{1,0:T(1,128)S(1)} %pad_maximum_fusion.6.refs_0_.refs_2_), channel_id=1, source_target_pairs={{0,2},{1,3},{2,0},{3,1},{4,6},{5,7},{6,4},{7,5},{8,10},{9,11},{10,... | collective-permute-start | bytes 24584 | tf_op jit(solution)/shard_map/ppermute | solution.py:23
  10.4 7.0 %collective-permute-start.20 = (bf16[1,2,1,1024]{3,2,1,0:T(2,128)(2,1)S(1)}, bf16[1,2,1,1024]{3,2,1,0:T(2,128)(2,1)S(1)}, u32[]{:S(2)}, u32[]{:S(2)}) collective-permute-start(bf16[1,2,1,1024]{3,2,1,0:T(2,128)(2,1)S(1)} %pad_maximum_fusion.7.refs_0_), channel_id=1, source_target_pairs={{1,193},{3,67},{5,197},{7,71},{9,201},{11,75},{13,205},{15,79},{17... | collective-permute-start | bytes 12296 | tf_op jit(solution)/shard_map/ppermute | solution.py:231
  17.4 8.2 %collective-permute-start.21 = (bf16[1,2,1,1024]{3,2,1,0:T(2,128)(2,1)S(1)}, bf16[1,2,1,1024]{3,2,1,0:T(2,128)(2,1)S(1)}, u32[]{:S(2)}, u32[]{:S(2)}) collective-permute-start(bf16[1,2,1,1024]{3,2,1,0:T(2,128)(2,1)S(1)} %collective-permute-done.20.refs_1_), channel_id=1, source_target_pairs={{1,193},{3,67},{5,197},{7,71},{9,201},{11,75},{13,205},{15,79},{17... | collective-permute-start | bytes 12296 | tf_op jit(solution)/shard_map/ppermute | solution.py:231
  25.5 15.1 %collective-permute-start.9 = (f32[1,1024]{1,0:T(1,128)S(1)}, f32[1,1024]{1,0:T(1,128)S(1)}, u32[]{:S(2)}, u32[]{:S(2)}) collective-permute-start(f32[1,1024]{1,0:T(1,128)S(1)} %get-tuple-element.32), channel_id=1, source_target_pairs={{0,1},{1,0},{2,3},{3,2},{4,5},{5,4},{6,7},{7,6},{8,9},{9,8},{10,11... | collective-permute-start | bytes 12296 | tf_op jit(solution)/shard_map/ppermute | solution.py:23
  25.6 5.3 %collective-permute-start.22 = (bf16[1,2,1,1024]{3,2,1,0:T(2,128)(2,1)S(1)}, bf16[1,2,1,1024]{3,2,1,0:T(2,128)(2,1)S(1)}, u32[]{:S(2)}, u32[]{:S(2)}) collective-permute-start(bf16[1,2,1,1024]{3,2,1,0:T(2,128)(2,1)S(1)} %collective-permute-done.21.refs_2_), channel_id=1, source_target_pairs={{1,193},{3,67},{5,197},{7,71},{9,201},{11,75},{13,205},{15,79},{17... | collective-permute-start | bytes 12296 | tf_op jit(solution)/shard_map/ppermute | solution.py:231
  31.0 10.2 %collective-permute-start.23 = (bf16[4,2,1,1024]{3,2,1,0:T(2,128)(2,1)S(1)}, bf16[4,2,1,1024]{3,2,1,0:T(2,128)(2,1)S(1)}, u32[]{:S(2)}, u32[]{:S(2)}) collective-permute-start(bf16[4,2,1,1024]{3,2,1,0:T(2,128)(2,1)S(1)} %shard_map.119), channel_id=1, source_target_pairs={{1,5},{3,7},{5,1},{7,3},{9,13},{11,15},{13,9},{15,11},{17,21},{19,... | collective-permute-start | bytes 49160 | tf_op jit(solution)/shard_map/ppermute | solution.py:231
  34.1 7.1 %collective-permute-start.24 = (bf16[4,2,1,1024]{3,2,1,0:T(2,128)(2,1)S(1)}, bf16[4,2,1,1024]{3,2,1,0:T(2,128)(2,1)S(1)}, u32[]{:S(2)}, u32[]{:S(2)}) collective-permute-start(bf16[4,2,1,1024]{3,2,1,0:T(2,128)(2,1)S(1)} %shard_map.119), channel_id=1, source_target_pairs={{1,9},{3,11},{5,13},{7,15},{9,1},{11,3},{13,5},{15,7},{17,25},{19,... | collective-permute-start | bytes 49160 | tf_op jit(solution)/shard_map/ppermute | solution.py:231
  38.5 5.9 %collective-permute-start.25 = (bf16[4,2,1,1024]{3,2,1,0:T(2,128)(2,1)S(1)}, bf16[4,2,1,1024]{3,2,1,0:T(2,128)(2,1)S(1)}, u32[]{:S(2)}, u32[]{:S(2)}) collective-permute-start(bf16[4,2,1,1024]{3,2,1,0:T(2,128)(2,1)S(1)} %shard_map.119), channel_id=1, source_target_pairs={{1,13},{3,15},{5,9},{7,11},{9,5},{11,7},{13,1},{15,3},{17,29},{19,... | collective-permute-start | bytes 49160 | tf_op jit(solution)/shard_map/ppermute | solution.py:231
  40.6 13.8 %collective-permute-start.10 = (f32[1,1024]{1,0:T(1,128)S(1)}, f32[1,1024]{1,0:T(1,128)S(1)}, u32[]{:S(2)}, u32[]{:S(2)}) collective-permute-start(f32[1,1024]{1,0:T(1,128)S(1)} %add.7.refs_0_), channel_id=1, source_target_pairs={{0,2},{1,3},{2,0},{3,1},{4,6},{5,7},{6,4},{7,5},{8,10},{9,11},{10,... | collective-permute-start | bytes 12296 | tf_op jit(solution)/shard_map/ppermute | solution.py:23
  44.7 11.9 %collective-permute-start.26 = (bf16[4,2,4,1024]{3,2,1,0:T(4,128)(2,1)S(1)}, bf16[4,2,4,1024]{3,2,1,0:T(4,128)(2,1)S(1)}, u32[]{:S(2)}, u32[]{:S(2)}) collective-permute-start(bf16[4,2,4,1024]{3,2,1,0:T(4,128)(2,1)S(1)} %pad_maximum_fusion.3), channel_id=1, source_target_pairs={{1,17},{3,19},{5,21},{7,23},{9,25},{11,27},{13,29},{15,31},{17,1},... | collective-permute-start | bytes 196616 | tf_op jit(solution)/shard_map/ppermute | solution.py:231
  47.9 9.3 %collective-permute-start.27 = (bf16[4,2,4,1024]{3,2,1,0:T(4,128)(2,1)S(1)}, bf16[4,2,4,1024]{3,2,1,0:T(4,128)(2,1)S(1)}, u32[]{:S(2)}, u32[]{:S(2)}) collective-permute-start(bf16[4,2,4,1024]{3,2,1,0:T(4,128)(2,1)S(1)} %pad_maximum_fusion.3), channel_id=1, source_target_pairs={{1,33},{3,35},{5,37},{7,39},{9,41},{11,43},{13,45},{15,47},{17,49}... | collective-permute-start | bytes 196616 | tf_op jit(solution)/shard_map/ppermute | solution.py:231
  52.5 6.2 %collective-permute-start.28 = (bf16[4,2,4,1024]{3,2,1,0:T(4,128)(2,1)S(1)}, bf16[4,2,4,1024]{3,2,1,0:T(4,128)(2,1)S(1)}, u32[]{:S(2)}, u32[]{:S(2)}) collective-permute-start(bf16[4,2,4,1024]{3,2,1,0:T(4,128)(2,1)S(1)} %pad_maximum_fusion.3), channel_id=1, source_target_pairs={{1,49},{3,51},{5,53},{7,55},{9,57},{11,59},{13,61},{15,63},{17,33}... | collective-permute-start | bytes 196616 | tf_op jit(solution)/shard_map/ppermute | solution.py:231
  55.2 9.6 %collective-permute-start.18 = (bf16[1,128,1024]{2,1,0:T(8,128)(2,1)S(1)}, bf16[1,128,1024]{2,1,0:T(8,128)(2,1)S(1)}, u32[]{:S(2)}, u32[]{:S(2)}) collective-permute-start(bf16[1,128,1024]{2,1,0:T(8,128)(2,1)S(1)} %get-tuple-element.37), channel_id=1, source_target_pairs={{0,2},{1,3},{2,0},{3,1},{4,6},{5,7},{6,4},{7,5},{8,10},{9,11},{10,... | collective-permute-start | bytes 786440 | tf_op jit(solution)/shard_map/ppermute | solution.py:23
  55.7 6.1 %collective-permute-start.11 = (bf16[1,64,1024]{2,1,0:T(8,128)(2,1)S(1)}, bf16[1,64,1024]{2,1,0:T(8,128)(2,1)S(1)}, u32[]{:S(2)}, u32[]{:S(2)}) collective-permute-start(bf16[1,64,1024]{2,1,0:T(8,128)(2,1)S(1)} %get-tuple-element.33), channel_id=1, source_target_pairs={{0,2},{1,3},{2,0},{3,1},{4,6},{5,7},{6,4},{7,5},{8,10},{9,11},{10,... | collective-permute-start | bytes 393224 | tf_op jit(solution)/shard_map/ppermute | solution.py:23
  56.7 6.5 %collective-permute-start.13 = (bf16[1,64,1024]{2,1,0:T(8,128)(2,1)S(1)}, bf16[1,64,1024]{2,1,0:T(8,128)(2,1)S(1)}, u32[]{:S(2)}, u32[]{:S(2)}) collective-permute-start(bf16[1,64,1024]{2,1,0:T(8,128)(2,1)S(1)} %get-tuple-element.34), channel_id=1, source_target_pairs={{0,2},{1,3},{2,0},{3,1},{4,6},{5,7},{6,4},{7,5},{8,10},{9,11},{10,... | collective-permute-start | bytes 393224 | tf_op jit(solution)/shard_map/ppermute | solution.py:23
  57.3 7.3 %collective-permute-start.3 = (bf16[1,64,1024]{2,1,0:T(8,128)(2,1)S(1)}, bf16[1,64,1024]{2,1,0:T(8,128)(2,1)S(1)}, u32[]{:S(2)}, u32[]{:S(2)}) collective-permute-start(bf16[1,64,1024]{2,1,0:T(8,128)(2,1)S(1)} %shard_map.113), channel_id=1, source_target_pairs={{0,2},{1,3},{2,0},{3,1},{4,6},{5,7},{6,4},{7,5},{8,10},{9,11},{10,... | collective-permute-start | bytes 393224 | tf_op jit(solution)/shard_map/ppermute | solution.py:23
  59.1 7.3 %collective-permute-start.29 = (bf16[4,2,16,1024]{3,2,1,0:T(8,128)(2,1)S(1)}, bf16[4,2,16,1024]{3,2,1,0:T(8,128)(2,1)S(1)}, u32[]{:S(2)}, u32[]{:S(2)}) collective-permute-start(bf16[4,2,16,1024]{3,2,1,0:T(8,128)(2,1)S(1)} %pad_maximum_fusion.own_ref), channel_id=1, source_target_pairs={{1,0},{3,2},{5,4},{7,6},{9,8},{11,10},{13,12},{15,14},{17,16},{19,... | collective-permute-start | bytes 786440 | tf_op jit(solution)/shard_map/ppermute | solution.py:231
  61.8 10.7 %collective-permute-start.16 = (bf16[1,256,1024]{2,1,0:T(8,128)(2,1)S(1)}, bf16[1,256,1024]{2,1,0:T(8,128)(2,1)S(1)}, u32[]{:S(2)}, u32[]{:S(2)}) collective-permute-start(bf16[1,256,1024]{2,1,0:T(8,128)(2,1)S(1)} %get-tuple-element.36), channel_id=1, source_target_pairs={{0,2},{1,3},{2,0},{3,1},{4,6},{5,7},{6,4},{7,5},{8,10},{9,11},{10,... | collective-permute-start | bytes 1572872 | tf_op jit(solution)/shard_map/ppermute | solution.py:23
  63.2 2.2 %collective-permute-start.12 = (bf16[1,64,1024]{2,1,0:T(8,128)(2,1)S(1)}, bf16[1,64,1024]{2,1,0:T(8,128)(2,1)S(1)}, u32[]{:S(2)}, u32[]{:S(2)}) collective-permute-start(bf16[1,64,1024]{2,1,0:T(8,128)(2,1)S(1)} %collective-permute-done.11.refs_0_), channel_id=1, source_target_pairs={{0,1},{1,0},{2,3},{3,2},{4,5},{5,4},{6,7},{7,6},{8,9},{9,8},{10,11... | collective-permute-start | bytes 393224 | tf_op jit(solution)/shard_map/ppermute | solution.py:23
  64.6 25.9 %collective-permute-start.15 = (bf16[1,512,1024]{2,1,0:T(8,128)(2,1)S(1)}, bf16[1,512,1024]{2,1,0:T(8,128)(2,1)S(1)}, u32[]{:S(2)}, u32[]{:S(2)}) collective-permute-start(bf16[1,512,1024]{2,1,0:T(8,128)(2,1)S(1)} %get-tuple-element.35.refs_0_), channel_id=1, source_target_pairs={{0,1},{1,0},{2,3},{3,2},{4,5},{5,4},{6,7},{7,6},{8,9},{9,8},{10,11... | collective-permute-start | bytes 3145736 | tf_op jit(solution)/shard_map/ppermute | solution.py:23
  64.8 16.1 %collective-permute-start.5 = (bf16[1,192,1024]{2,1,0:T(8,128)(2,1)S(1)}, bf16[1,192,1024]{2,1,0:T(8,128)(2,1)S(1)}, u32[]{:S(2)}, u32[]{:S(2)}) collective-permute-start(bf16[1,192,1024]{2,1,0:T(8,128)(2,1)S(1)} %get-tuple-element.29), channel_id=1, source_target_pairs={{0,2},{1,3},{2,0},{3,1},{4,6},{5,7},{6,4},{7,5},{8,10},{9,11},{10,... | collective-permute-start | bytes 1179656 | tf_op jit(solution)/shard_map/ppermute | solution.py:23
  65.4 24.5 %collective-permute-start.7 = (bf16[1,256,1024]{2,1,0:T(8,128)(2,1)S(1)}, bf16[1,256,1024]{2,1,0:T(8,128)(2,1)S(1)}, u32[]{:S(2)}, u32[]{:S(2)}) collective-permute-start(bf16[1,256,1024]{2,1,0:T(8,128)(2,1)S(1)} %get-tuple-element.30), channel_id=1, source_target_pairs={{0,2},{1,3},{2,0},{3,1},{4,6},{5,7},{6,4},{7,5},{8,10},{9,11},{10,... | collective-permute-start | bytes 1572872 | tf_op jit(solution)/shard_map/ppermute | solution.py:23
  66.3 28.1 %collective-permute-start.2 = (bf16[1,512,1024]{2,1,0:T(8,128)(2,1)S(1)}, bf16[1,512,1024]{2,1,0:T(8,128)(2,1)S(1)}, u32[]{:S(2)}, u32[]{:S(2)}) collective-permute-start(bf16[1,512,1024]{2,1,0:T(8,128)(2,1)S(1)} %get-tuple-element.28.refs_0_), channel_id=1, source_target_pairs={{0,1},{1,0},{2,3},{3,2},{4,5},{5,4},{6,7},{7,6},{8,9},{9,8},{10,11... | collective-permute-start | bytes 3145736 | tf_op jit(solution)/shard_map/ppermute | solution.py:23
  72.5 17.9 %collective-permute-start.17 = (bf16[1,256,1024]{2,1,0:T(8,128)(2,1)S(1)}, bf16[1,256,1024]{2,1,0:T(8,128)(2,1)S(1)}, u32[]{:S(2)}, u32[]{:S(2)}) collective-permute-start(bf16[1,256,1024]{2,1,0:T(8,128)(2,1)S(1)} %collective-permute-done.16.refs_2_), channel_id=1, source_target_pairs={{0,1},{1,0},{2,3},{3,2},{4,5},{5,4},{6,7},{7,6},{8,9},{9,8},{10,11... | collective-permute-start | bytes 1572872 | tf_op jit(solution)/shard_map/ppermute | solution.py:23
  80.9 9.0 %collective-permute-start.19 = (bf16[1,128,1024]{2,1,0:T(8,128)(2,1)S(1)}, bf16[1,128,1024]{2,1,0:T(8,128)(2,1)S(1)}, u32[]{:S(2)}, u32[]{:S(2)}) collective-permute-start(bf16[1,128,1024]{2,1,0:T(8,128)(2,1)S(1)} %collective-permute-done.18.refs_4_), channel_id=1, source_target_pairs={{0,1},{1,0},{2,3},{3,2},{4,5},{5,4},{6,7},{7,6},{8,9},{9,8},{10,11... | collective-permute-start | bytes 786440 | tf_op jit(solution)/shard_map/ppermute | solution.py:23
  89.9 4.5 %collective-permute-start.8 = (bf16[1,256,1024]{2,1,0:T(8,128)(2,1)S(1)}, bf16[1,256,1024]{2,1,0:T(8,128)(2,1)S(1)}, u32[]{:S(2)}, u32[]{:S(2)}) collective-permute-start(bf16[1,256,1024]{2,1,0:T(8,128)(2,1)S(1)} %collective-permute-done.7.refs_6_), channel_id=1, source_target_pairs={{0,1},{1,0},{2,3},{3,2},{4,5},{5,4},{6,7},{7,6},{8,9},{9,8},{10,11... | collective-permute-start | bytes 1572872 | tf_op jit(solution)/shard_map/ppermute | solution.py:23
  89.9 4.5 %collective-permute-start.6 = (bf16[1,192,1024]{2,1,0:T(8,128)(2,1)S(1)}, bf16[1,192,1024]{2,1,0:T(8,128)(2,1)S(1)}, u32[]{:S(2)}, u32[]{:S(2)}) collective-permute-start(bf16[1,192,1024]{2,1,0:T(8,128)(2,1)S(1)} %collective-permute-done.5.refs_4_), channel_id=1, source_target_pairs={{0,1},{1,0},{2,3},{3,2},{4,5},{5,4},{6,7},{7,6},{8,9},{9,8},{10,11... | collective-permute-start | bytes 1179656 | tf_op jit(solution)/shard_map/ppermute | solution.py:23
  90.4 3.1 %collective-permute-start.14 = (bf16[1,64,1024]{2,1,0:T(8,128)(2,1)S(1)}, bf16[1,64,1024]{2,1,0:T(8,128)(2,1)S(1)}, u32[]{:S(2)}, u32[]{:S(2)}) collective-permute-start(bf16[1,64,1024]{2,1,0:T(8,128)(2,1)S(1)} %collective-permute-done.13.refs_2_), channel_id=1, source_target_pairs={{0,1},{1,0},{2,3},{3,2},{4,5},{5,4},{6,7},{7,6},{8,9},{9,8},{10,11... | collective-permute-start | bytes 393224 | tf_op jit(solution)/shard_map/ppermute | solution.py:23
  90.5 3.9 %collective-permute-start.4 = (bf16[1,64,1024]{2,1,0:T(8,128)(2,1)S(1)}, bf16[1,64,1024]{2,1,0:T(8,128)(2,1)S(1)}, u32[]{:S(2)}, u32[]{:S(2)}) collective-permute-start(bf16[1,64,1024]{2,1,0:T(8,128)(2,1)S(1)} %collective-permute-done.3.refs_2_), channel_id=1, source_target_pairs={{0,1},{1,0},{2,3},{3,2},{4,5},{5,4},{6,7},{7,6},{8,9},{9,8},{10,11... | collective-permute-start | bytes 393224 | tf_op jit(solution)/shard_map/ppermute | solution.py:23

commit v4 on v3

--- a/solution.py
+++ b/solution.py
@@ -225,14 +225,14 @@
     experts, shards = lax.axis_size("expert"), lax.axis_size("shard")
     pairs = []
     for e in range(experts):
-        for s in range(CORE, shards, 2):
-            f, t = to(e, s)
-            pairs.append((e * shards + s, f % experts * shards + t))
+        for s in range(shards):
+            target = to(e, s) % experts if s & CORE else e
+            pairs.append((e * shards + s, target * shards + s))
     return lax.ppermute(x, ("expert", "shard"), pairs)
 
 
 def turned(x):
-    return sent(x, lambda e, s: (e + (16 if s & CHIP else -16), s))
+    return sent(x, lambda e, s: e + (16 if s & CHIP else -16))
 
 
 def planes_body(*refs):
@@ -251,10 +251,10 @@
         planes_body, jax.ShapeDtypeStruct((4, *x.shape[1:]), x.dtype), [VMEM] * 4, 1, 1 << 10, out_specs=VMEM
     )(*pieces)
     for unit in (1, 4):
-        a, b, c = (sent(x, lambda e, s, k=k: (e ^ unit * k, s)) for k in (1, 2, 3))
+        a, b, c = (sent(x, lambda e, s, k=k: e ^ unit * k) for k in (1, 2, 3))
         low = lows["expert", unit]
         x = in_order(lows["expert", 2 * unit], in_order(low, x, a, 2), in_order(low, b, c, 2), 2)
-    other = sent(x, lambda e, s: (e, s ^ CORE))
+    other = swap(x, "shard", CORE)
     z, chips, plane, rows = x.shape
     return call(
         router_body, jax.ShapeDtypeStruct((z * plane, chips * rows), x.dtype), [VMEM, VMEM], 2, 1 << 20, out_specs=VMEM

time: 96.9 us -> 102 us (1.053)
  waiting for transfers between devices: 35.2 us -> 42 us
  starting transfers between devices: 47.7 us -> 46.5 us
    ppermute x20 -> x21, waiting for transfers between devices: 29.6 us -> 36.4 us  [swap(): return lax.ppermute(x, axis, [(i, i ^ mask) for i in range(n)])]
    ppermute x10 -> x9, starting transfers between devices: 36.5 us -> 35.2 us  [sent(): return lax.ppermute(x, ('expert', 'shard'), pairs)]
    ppermute x20 -> x21, starting transfers between devices: 11.2 us -> 11.3 us  [swap(): return lax.ppermute(x, axis, [(i, i ^ mask) for i in range(n)])]
    ppermute x10 -> x9, waiting for transfers between devices: 5.61 us -> 5.61 us  [sent(): return lax.ppermute(x, ('expert', 'shard'), pairs)]
where the time goes in v4:
time: 102 us
  starting transfers between devices  46.5 us (46%)
  waiting for transfers between devices  42 us (41%)
  Pallas kernels  11.2 us (11%)
  between operations  1.6 us (2%)
    ppermute x21, waiting for transfers between devices, swap(): return lax.ppermute(x, axis, [(i, i ^ mask) for i in range(n)])  36.4 us
    ppermute x9, starting transfers between devices, sent(): return lax.ppermute(x, ('expert', 'shard'), pairs)  35.2 us
    ppermute x21, starting transfers between devices, swap(): return lax.ppermute(x, axis, [(i, i ^ mask) for i in range(n)])  11.3 us
    ppermute x9, waiting for transfers between devices, sent(): return lax.ppermute(x, ('expert', 'shard'), pairs)  5.61 us
    pallas_call x3, Pallas kernels, place(): call(functools.partial(place_body, places), jax.ShapeDtypeStruct(shape, b...  4.79 us
    pallas_call x2, Pallas kernels, mean_of(): call(functools.partial(mean_body, n), (pltpu.VMEM((rows, columns), jnp.fl...  4.73 us
  transfers between devices with their start and end apart: 30, of which 12 were waited for; matrix products, arithmetic and copies ran while one was open for 1% of the time, Pallas kernels for 7%

profile of v4, /device:TPU:1, one launch (start us, length us, event | category | flops | bytes accessed | tf_op | source)
XLA Modules:
  0.0 102.1 jit_solution(5385819385439715308)
XLA Ops:
  1.3 2.4 %shard_map.110 = (f32[512,1024]{1,0:T(8,128)S(1)}, f32[1,1536]{1,0:T(1,128)S(1)}) custom-call(f32[1]{0:T(128)S(6)} %copy.14.share_ref, f32[1,512,1024]{2,1,0:T(8,128)} %w_ref.2, f32[1,512,1024]{2,1,0:T(8,128)} %avg_ref.2, f32[1,512]{1,0:T(1,128)} %bitcast.17, f32[1,512]{1,0:T(1,128)} %bitcast.18), custom_call_target="tpu_custom_call" | custom-call | flops 4194304 | bytes 4194304 | tf_op jit(solution)/shard_map/pallas_call | solution.py:81
  3.7 3.3 %collective-permute-start = (f32[1,1536]{1,0:T(1,128)S(1)}, f32[1,1536]{1,0:T(1,128)S(1)}, u32[]{:S(2)}, u32[]{:S(2)}) collective-permute-start(f32[1,1536]{1,0:T(1,128)S(1)} %get-tuple-element.26), channel_id=1, source_target_pairs={{0,1},{1,0},{2,3},{3,2},{4,5},{5,4},{6,7},{7,6},{8,9},{9,8},{10,11... | collective-permute-start | bytes 18440 | tf_op jit(solution)/shard_map/ppermute | solution.py:23
  7.0 0.8 collective-permute-done
  7.8 0.1 collective-permute-start.1
  7.9 2.5 %collective-permute-done.1.refs_1_.refs_3_ = f32[1,2048]{1,0:T(1,128)S(1)} collective-permute-done((f32[1,2048]{1,0:T(1,128)S(1)}, f32[1,2048]{1,0:T(1,128)S(1)}, u32[]{:S(2)}, u32[]{:S(2)}) %collective-permute-start.1) | collective-permute-done | bytes 8224 | tf_op jit(solution)/shard_map/ppermute | solution.py:23
  10.4 6.2 %collective-permute-start.20 = (bf16[1,2,1,1024]{3,2,1,0:T(2,128)(2,1)S(1)}, bf16[1,2,1,1024]{3,2,1,0:T(2,128)(2,1)S(1)}, u32[]{:S(2)}, u32[]{:S(2)}) collective-permute-start(bf16[1,2,1,1024]{3,2,1,0:T(2,128)(2,1)S(1)} %pad_maximum_fusion.7.refs_0_), channel_id=1, source_target_pairs={{0,0},{1,193},{2,2},{3,67},{4,4},{5,197},{6,6},{7,71},{8,8},{9,201... | collective-permute-start | bytes 12296 | tf_op jit(solution)/shard_map/ppermute | solution.py:231
  16.7 0.8 collective-permute-done.20.refs_1_
  17.4 5.7 %collective-permute-start.21 = (bf16[1,2,1,1024]{3,2,1,0:T(2,128)(2,1)S(1)}, bf16[1,2,1,1024]{3,2,1,0:T(2,128)(2,1)S(1)}, u32[]{:S(2)}, u32[]{:S(2)}) collective-permute-start(bf16[1,2,1,1024]{3,2,1,0:T(2,128)(2,1)S(1)} %collective-permute-done.20.refs_1_), channel_id=1, source_target_pairs={{0,0},{1,193},{2,2},{3,67},{4,4},{5,197},{6,6},{7,71},{8,8},{9,201... | collective-permute-start | bytes 12296 | tf_op jit(solution)/shard_map/ppermute | solution.py:231
  23.2 2.4 %shard_map.115 = (f32[512,1024]{1,0:T(8,128)S(1)}, f32[1,1024]{1,0:T(1,128)S(1)}) custom-call(f32[1]{0:T(128)S(6)} %copy.14.share_ref, f32[1,512,1024]{2,1,0:T(8,128)} %w_ref.3, f32[1,512,1024]{2,1,0:T(8,128)} %avg_ref.3), custom_call_target="tpu_custom_call" | custom-call | flops 4194304 | bytes 4194304 | tf_op jit(solution)/shard_map/pallas_call | solution.py:81
  25.5 0.1 collective-permute-start.9
  25.6 4.0 %collective-permute-start.22 = (bf16[1,2,1,1024]{3,2,1,0:T(2,128)(2,1)S(1)}, bf16[1,2,1,1024]{3,2,1,0:T(2,128)(2,1)S(1)}, u32[]{:S(2)}, u32[]{:S(2)}) collective-permute-start(bf16[1,2,1,1024]{3,2,1,0:T(2,128)(2,1)S(1)} %collective-permute-done.21.refs_2_), channel_id=1, source_target_pairs={{0,0},{1,193},{2,2},{3,67},{4,4},{5,197},{6,6},{7,71},{8,8},{9,201... | collective-permute-start | bytes 12296 | tf_op jit(solution)/shard_map/ppermute | solution.py:231
  29.7 1.2 %collective-permute-done.22.refs_3_ = bf16[1,2,1,1024]{3,2,1,0:T(2,128)(2,1)S(1)} collective-permute-done((bf16[1,2,1,1024]{3,2,1,0:T(2,128)(2,1)S(1)}, bf16[1,2,1,1024]{3,2,1,0:T(2,128)(2,1)S(1)}, u32[]{:S(2)}, u32[]{:S(2)}) %collective-permute-start.22) | collective-permute-done | bytes 4128 | tf_op jit(solution)/shard_map/ppermute | solution.py:231
  31.0 3.1 %collective-permute-start.23 = (bf16[4,2,1,1024]{3,2,1,0:T(2,128)(2,1)S(1)}, bf16[4,2,1,1024]{3,2,1,0:T(2,128)(2,1)S(1)}, u32[]{:S(2)}, u32[]{:S(2)}) collective-permute-start(bf16[4,2,1,1024]{3,2,1,0:T(2,128)(2,1)S(1)} %shard_map.119), channel_id=1, source_target_pairs={{0,0},{1,5},{2,2},{3,7},{4,4},{5,1},{6,6},{7,3},{8,8},{9,13},{10,1... | collective-permute-start | bytes 49160 | tf_op jit(solution)/shard_map/ppermute | solution.py:231
  34.1 4.4 %collective-permute-start.24 = (bf16[4,2,1,1024]{3,2,1,0:T(2,128)(2,1)S(1)}, bf16[4,2,1,1024]{3,2,1,0:T(2,128)(2,1)S(1)}, u32[]{:S(2)}, u32[]{:S(2)}) collective-permute-start(bf16[4,2,1,1024]{3,2,1,0:T(2,128)(2,1)S(1)} %shard_map.119), channel_id=1, source_target_pairs={{0,0},{1,9},{2,2},{3,11},{4,4},{5,13},{6,6},{7,15},{8,8},{9,1},{10... | collective-permute-start | bytes 49160 | tf_op jit(solution)/shard_map/ppermute | solution.py:231
  38.5 2.1 %collective-permute-start.25 = (bf16[4,2,1,1024]{3,2,1,0:T(2,128)(2,1)S(1)}, bf16[4,2,1,1024]{3,2,1,0:T(2,128)(2,1)S(1)}, u32[]{:S(2)}, u32[]{:S(2)}) collective-permute-start(bf16[4,2,1,1024]{3,2,1,0:T(2,128)(2,1)S(1)} %shard_map.119), channel_id=1, source_target_pairs={{0,0},{1,13},{2,2},{3,15},{4,4},{5,9},{6,6},{7,11},{8,8},{9,5},{10... | collective-permute-start | bytes 49160 | tf_op jit(solution)/shard_map/ppermute | solution.py:231
  40.6 0.6 collective-permute-start.10
  41.2 3.1 %collective-permute-done.25 = bf16[4,2,1,1024]{3,2,1,0:T(2,128)(2,1)S(1)} collective-permute-done((bf16[4,2,1,1024]{3,2,1,0:T(2,128)(2,1)S(1)}, bf16[4,2,1,1024]{3,2,1,0:T(2,128)(2,1)S(1)}, u32[]{:S(2)}, u32[]{:S(2)}) %collective-permute-start.25) | collective-permute-done | bytes 16416 | tf_op jit(solution)/shard_map/ppermute | solution.py:231
  44.3 0.1 broadcast_select_fusion.5
  44.5 0.2 broadcast_select_fusion.7
  44.7 3.2 %collective-permute-start.26 = (bf16[4,2,4,1024]{3,2,1,0:T(4,128)(2,1)S(1)}, bf16[4,2,4,1024]{3,2,1,0:T(4,128)(2,1)S(1)}, u32[]{:S(2)}, u32[]{:S(2)}) collective-permute-start(bf16[4,2,4,1024]{3,2,1,0:T(4,128)(2,1)S(1)} %pad_maximum_fusion.3), channel_id=1, source_target_pairs={{0,0},{1,17},{2,2},{3,19},{4,4},{5,21},{6,6},{7,23},{8,8},{9,25},{... | collective-permute-start | bytes 196616 | tf_op jit(solution)/shard_map/ppermute | solution.py:231
  47.9 4.5 %collective-permute-start.27 = (bf16[4,2,4,1024]{3,2,1,0:T(4,128)(2,1)S(1)}, bf16[4,2,4,1024]{3,2,1,0:T(4,128)(2,1)S(1)}, u32[]{:S(2)}, u32[]{:S(2)}) collective-permute-start(bf16[4,2,4,1024]{3,2,1,0:T(4,128)(2,1)S(1)} %pad_maximum_fusion.3), channel_id=1, source_target_pairs={{0,0},{1,33},{2,2},{3,35},{4,4},{5,37},{6,6},{7,39},{8,8},{9,41},{... | collective-permute-start | bytes 196616 | tf_op jit(solution)/shard_map/ppermute | solution.py:231
  52.5 1.9 %collective-permute-start.28 = (bf16[4,2,4,1024]{3,2,1,0:T(4,128)(2,1)S(1)}, bf16[4,2,4,1024]{3,2,1,0:T(4,128)(2,1)S(1)}, u32[]{:S(2)}, u32[]{:S(2)}) collective-permute-start(bf16[4,2,4,1024]{3,2,1,0:T(4,128)(2,1)S(1)} %pad_maximum_fusion.3), channel_id=1, source_target_pairs={{0,0},{1,49},{2,2},{3,51},{4,4},{5,53},{6,6},{7,55},{8,8},{9,57},{... | collective-permute-start | bytes 196616 | tf_op jit(solution)/shard_map/ppermute | solution.py:231
  54.5 0.7 shard_map.116
  55.2 0.5 collective-permute-start.18
  55.7 1.0 collective-permute-start.11
  56.7 0.6 collective-permute-start.13
  57.3 1.0 collective-permute-start.3
  58.2 0.5 collective-permute-done.28
  58.7 0.2 broadcast_select_fusion.11
  58.9 0.2 broadcast_select_fusion.1
  59.1 0.1 collective-permute-start.29
  59.2 2.6 %collective-permute-done.11.refs_0_ = bf16[1,64,1024]{2,1,0:T(8,128)(2,1)S(1)} collective-permute-done((bf16[1,64,1024]{2,1,0:T(8,128)(2,1)S(1)}, bf16[1,64,1024]{2,1,0:T(8,128)(2,1)S(1)}, u32[]{:S(2)}, u32[]{:S(2)}) %collective-permute-start.11) | collective-permute-done | bytes 131104 | tf_op jit(solution)/shard_map/ppermute | solution.py:23
  61.8 0.5 collective-permute-start.16
  62.3 1.9 %collective-permute-done.13.refs_2_ = bf16[1,64,1024]{2,1,0:T(8,128)(2,1)S(1)} collective-permute-done((bf16[1,64,1024]{2,1,0:T(8,128)(2,1)S(1)}, bf16[1,64,1024]{2,1,0:T(8,128)(2,1)S(1)}, u32[]{:S(2)}, u32[]{:S(2)}) %collective-permute-start.13) | collective-permute-done | bytes 131104 | tf_op jit(solution)/shard_map/ppermute | solution.py:23
  64.2 2.8 %collective-permute-done.3.refs_2_ = bf16[1,64,1024]{2,1,0:T(8,128)(2,1)S(1)} collective-permute-done((bf16[1,64,1024]{2,1,0:T(8,128)(2,1)S(1)}, bf16[1,64,1024]{2,1,0:T(8,128)(2,1)S(1)}, u32[]{:S(2)}, u32[]{:S(2)}) %collective-permute-start.3) | collective-permute-done | bytes 131104 | tf_op jit(solution)/shard_map/ppermute | solution.py:23
  67.0 0.1 shard_map.112
  67.1 0.6 collective-permute-start.5
  67.7 1.0 collective-permute-start.7
  68.7 1.1 %collective-permute-start.2 = (bf16[1,512,1024]{2,1,0:T(8,128)(2,1)S(1)}, bf16[1,512,1024]{2,1,0:T(8,128)(2,1)S(1)}, u32[]{:S(2)}, u32[]{:S(2)}) collective-permute-start(bf16[1,512,1024]{2,1,0:T(8,128)(2,1)S(1)} %get-tuple-element.28.refs_0_), channel_id=1, source_target_pairs={{0,1},{1,0},{2,3},{3,2},{4,5},{5,4},{6,7},{7,6},{8,9},{9,8},{10,11... | collective-permute-start | bytes 3145736 | tf_op jit(solution)/shard_map/ppermute | solution.py:23
  69.8 8.4 %collective-permute-done.16.refs_2_ = bf16[1,256,1024]{2,1,0:T(8,128)(2,1)S(1)} collective-permute-done((bf16[1,256,1024]{2,1,0:T(8,128)(2,1)S(1)}, bf16[1,256,1024]{2,1,0:T(8,128)(2,1)S(1)}, u32[]{:S(2)}, u32[]{:S(2)}) %collective-permute-start.16) | collective-permute-done | bytes 524320 | tf_op jit(solution)/shard_map/ppermute | solution.py:23
  78.2 8.4 %collective-permute-done.5.refs_4_ = bf16[1,192,1024]{2,1,0:T(8,128)(2,1)S(1)} collective-permute-done((bf16[1,192,1024]{2,1,0:T(8,128)(2,1)S(1)}, bf16[1,192,1024]{2,1,0:T(8,128)(2,1)S(1)}, u32[]{:S(2)}, u32[]{:S(2)}) %collective-permute-start.5) | collective-permute-done | bytes 393248 | tf_op jit(solution)/shard_map/ppermute | solution.py:23
  86.6 8.9 %collective-permute-done.7.refs_6_ = bf16[1,256,1024]{2,1,0:T(8,128)(2,1)S(1)} collective-permute-done((bf16[1,256,1024]{2,1,0:T(8,128)(2,1)S(1)}, bf16[1,256,1024]{2,1,0:T(8,128)(2,1)S(1)}, u32[]{:S(2)}, u32[]{:S(2)}) %collective-permute-start.7) | collective-permute-done | bytes 524320 | tf_op jit(solution)/shard_map/ppermute | solution.py:23
  95.5 0.5 collective-permute-start.6
  96.1 0.4 collective-permute-start.4
  96.5 0.7 shard_map.120
  97.3 1.9 %shard_map.117.refs_4_ = bf16[1,2048,1024]{2,1,0:T(8,128)(2,1)} custom-call(bf16[1,512,1024]{2,1,0:T(8,128)(2,1)S(1)} %get-tuple-element.35.refs_0_, bf16[1,512,1024]{2,1,0:T(8,128)(2,1)S(1)} %collective-permute-done.15.refs_1_, bf16[1,256,1024]{2,1,0:T(8,128)(2,1)S(1)} %collective-permute-done.16.refs_2_, ...), custom_call_target="tpu_custom_call" | custom-call | flops 1048576 | bytes 4194304 | tf_op jit(solution)/shard_map/pallas_call | solution.py:160
  99.2 0.8 shard_map.118
  100.0 2.1 %shard_map.114 = bf16[1,2048,1024]{2,1,0:T(8,128)(2,1)} custom-call(bf16[1,512,1024]{2,1,0:T(8,128)(2,1)S(1)} %get-tuple-element.28.refs_0_, bf16[1,512,1024]{2,1,0:T(8,128)(2,1)S(1)} %collective-permute-done.2.refs_1_, bf16[1,64,1024]{2,1,0:T(8,128)(2,1)S(1)} %collective-permute-done.3.refs_2_, bf16[1,64,1024]{2,1,0:T(8,128)(2,1)S(1)} %collective-permute-done.4.refs_3_, ...), custom_call_target="tpu_custom_call" | custom-call | flops 1048576 | bytes 4194304 | tf_op jit(solution)/shard_map/pallas_call | solution.py:160
  (38 shorter events, 0.5 us)
Async XLA Ops:
  3.7 4.1 %collective-permute-start = (f32[1,1536]{1,0:T(1,128)S(1)}, f32[1,1536]{1,0:T(1,128)S(1)}, u32[]{:S(2)}, u32[]{:S(2)}) collective-permute-start(f32[1,1536]{1,0:T(1,128)S(1)} %get-tuple-element.26), channel_id=1, source_target_pairs={{0,1},{1,0},{2,3},{3,2},{4,5},{5,4},{6,7},{7,6},{8,9},{9,8},{10,11... | collective-permute-start | bytes 18440 | tf_op jit(solution)/shard_map/ppermute | solution.py:23
  7.8 2.6 %collective-permute-start.1 = (f32[1,2048]{1,0:T(1,128)S(1)}, f32[1,2048]{1,0:T(1,128)S(1)}, u32[]{:S(2)}, u32[]{:S(2)}) collective-permute-start(f32[1,2048]{1,0:T(1,128)S(1)} %pad_maximum_fusion.6.refs_0_.refs_2_), channel_id=1, source_target_pairs={{0,2},{1,3},{2,0},{3,1},{4,6},{5,7},{6,4},{7,5},{8,10},{9,11},{10,... | collective-permute-start | bytes 24584 | tf_op jit(solution)/shard_map/ppermute | solution.py:23
  10.4 7.0 %collective-permute-start.20 = (bf16[1,2,1,1024]{3,2,1,0:T(2,128)(2,1)S(1)}, bf16[1,2,1,1024]{3,2,1,0:T(2,128)(2,1)S(1)}, u32[]{:S(2)}, u32[]{:S(2)}) collective-permute-start(bf16[1,2,1,1024]{3,2,1,0:T(2,128)(2,1)S(1)} %pad_maximum_fusion.7.refs_0_), channel_id=1, source_target_pairs={{0,0},{1,193},{2,2},{3,67},{4,4},{5,197},{6,6},{7,71},{8,8},{9,201... | collective-permute-start | bytes 12296 | tf_op jit(solution)/shard_map/ppermute | solution.py:231
  17.4 8.2 %collective-permute-start.21 = (bf16[1,2,1,1024]{3,2,1,0:T(2,128)(2,1)S(1)}, bf16[1,2,1,1024]{3,2,1,0:T(2,128)(2,1)S(1)}, u32[]{:S(2)}, u32[]{:S(2)}) collective-permute-start(bf16[1,2,1,1024]{3,2,1,0:T(2,128)(2,1)S(1)} %collective-permute-done.20.refs_1_), channel_id=1, source_target_pairs={{0,0},{1,193},{2,2},{3,67},{4,4},{5,197},{6,6},{7,71},{8,8},{9,201... | collective-permute-start | bytes 12296 | tf_op jit(solution)/shard_map/ppermute | solution.py:231
  25.5 15.1 %collective-permute-start.9 = (f32[1,1024]{1,0:T(1,128)S(1)}, f32[1,1024]{1,0:T(1,128)S(1)}, u32[]{:S(2)}, u32[]{:S(2)}) collective-permute-start(f32[1,1024]{1,0:T(1,128)S(1)} %get-tuple-element.32), channel_id=1, source_target_pairs={{0,1},{1,0},{2,3},{3,2},{4,5},{5,4},{6,7},{7,6},{8,9},{9,8},{10,11... | collective-permute-start | bytes 12296 | tf_op jit(solution)/shard_map/ppermute | solution.py:23
  25.6 5.3 %collective-permute-start.22 = (bf16[1,2,1,1024]{3,2,1,0:T(2,128)(2,1)S(1)}, bf16[1,2,1,1024]{3,2,1,0:T(2,128)(2,1)S(1)}, u32[]{:S(2)}, u32[]{:S(2)}) collective-permute-start(bf16[1,2,1,1024]{3,2,1,0:T(2,128)(2,1)S(1)} %collective-permute-done.21.refs_2_), channel_id=1, source_target_pairs={{0,0},{1,193},{2,2},{3,67},{4,4},{5,197},{6,6},{7,71},{8,8},{9,201... | collective-permute-start | bytes 12296 | tf_op jit(solution)/shard_map/ppermute | solution.py:231
  31.0 10.2 %collective-permute-start.23 = (bf16[4,2,1,1024]{3,2,1,0:T(2,128)(2,1)S(1)}, bf16[4,2,1,1024]{3,2,1,0:T(2,128)(2,1)S(1)}, u32[]{:S(2)}, u32[]{:S(2)}) collective-permute-start(bf16[4,2,1,1024]{3,2,1,0:T(2,128)(2,1)S(1)} %shard_map.119), channel_id=1, source_target_pairs={{0,0},{1,5},{2,2},{3,7},{4,4},{5,1},{6,6},{7,3},{8,8},{9,13},{10,1... | collective-permute-start | bytes 49160 | tf_op jit(solution)/shard_map/ppermute | solution.py:231
  34.1 7.1 %collective-permute-start.24 = (bf16[4,2,1,1024]{3,2,1,0:T(2,128)(2,1)S(1)}, bf16[4,2,1,1024]{3,2,1,0:T(2,128)(2,1)S(1)}, u32[]{:S(2)}, u32[]{:S(2)}) collective-permute-start(bf16[4,2,1,1024]{3,2,1,0:T(2,128)(2,1)S(1)} %shard_map.119), channel_id=1, source_target_pairs={{0,0},{1,9},{2,2},{3,11},{4,4},{5,13},{6,6},{7,15},{8,8},{9,1},{10... | collective-permute-start | bytes 49160 | tf_op jit(solution)/shard_map/ppermute | solution.py:231
  38.5 5.9 %collective-permute-start.25 = (bf16[4,2,1,1024]{3,2,1,0:T(2,128)(2,1)S(1)}, bf16[4,2,1,1024]{3,2,1,0:T(2,128)(2,1)S(1)}, u32[]{:S(2)}, u32[]{:S(2)}) collective-permute-start(bf16[4,2,1,1024]{3,2,1,0:T(2,128)(2,1)S(1)} %shard_map.119), channel_id=1, source_target_pairs={{0,0},{1,13},{2,2},{3,15},{4,4},{5,9},{6,6},{7,11},{8,8},{9,5},{10... | collective-permute-start | bytes 49160 | tf_op jit(solution)/shard_map/ppermute | solution.py:231
  40.6 13.8 %collective-permute-start.10 = (f32[1,1024]{1,0:T(1,128)S(1)}, f32[1,1024]{1,0:T(1,128)S(1)}, u32[]{:S(2)}, u32[]{:S(2)}) collective-permute-start(f32[1,1024]{1,0:T(1,128)S(1)} %add.7.refs_0_), channel_id=1, source_target_pairs={{0,2},{1,3},{2,0},{3,1},{4,6},{5,7},{6,4},{7,5},{8,10},{9,11},{10,... | collective-permute-start | bytes 12296 | tf_op jit(solution)/shard_map/ppermute | solution.py:23
  44.7 11.9 %collective-permute-start.26 = (bf16[4,2,4,1024]{3,2,1,0:T(4,128)(2,1)S(1)}, bf16[4,2,4,1024]{3,2,1,0:T(4,128)(2,1)S(1)}, u32[]{:S(2)}, u32[]{:S(2)}) collective-permute-start(bf16[4,2,4,1024]{3,2,1,0:T(4,128)(2,1)S(1)} %pad_maximum_fusion.3), channel_id=1, source_target_pairs={{0,0},{1,17},{2,2},{3,19},{4,4},{5,21},{6,6},{7,23},{8,8},{9,25},{... | collective-permute-start | bytes 196616 | tf_op jit(solution)/shard_map/ppermute | solution.py:231
  47.9 9.3 %collective-permute-start.27 = (bf16[4,2,4,1024]{3,2,1,0:T(4,128)(2,1)S(1)}, bf16[4,2,4,1024]{3,2,1,0:T(4,128)(2,1)S(1)}, u32[]{:S(2)}, u32[]{:S(2)}) collective-permute-start(bf16[4,2,4,1024]{3,2,1,0:T(4,128)(2,1)S(1)} %pad_maximum_fusion.3), channel_id=1, source_target_pairs={{0,0},{1,33},{2,2},{3,35},{4,4},{5,37},{6,6},{7,39},{8,8},{9,41},{... | collective-permute-start | bytes 196616 | tf_op jit(solution)/shard_map/ppermute | solution.py:231
  52.5 6.2 %collective-permute-start.28 = (bf16[4,2,4,1024]{3,2,1,0:T(4,128)(2,1)S(1)}, bf16[4,2,4,1024]{3,2,1,0:T(4,128)(2,1)S(1)}, u32[]{:S(2)}, u32[]{:S(2)}) collective-permute-start(bf16[4,2,4,1024]{3,2,1,0:T(4,128)(2,1)S(1)} %pad_maximum_fusion.3), channel_id=1, source_target_pairs={{0,0},{1,49},{2,2},{3,51},{4,4},{5,53},{6,6},{7,55},{8,8},{9,57},{... | collective-permute-start | bytes 196616 | tf_op jit(solution)/shard_map/ppermute | solution.py:231
  55.2 12.0 %collective-permute-start.18 = (bf16[1,128,1024]{2,1,0:T(8,128)(2,1)S(1)}, bf16[1,128,1024]{2,1,0:T(8,128)(2,1)S(1)}, u32[]{:S(2)}, u32[]{:S(2)}) collective-permute-start(bf16[1,128,1024]{2,1,0:T(8,128)(2,1)S(1)} %get-tuple-element.37), channel_id=1, source_target_pairs={{0,2},{1,3},{2,0},{3,1},{4,6},{5,7},{6,4},{7,5},{8,10},{9,11},{10,... | collective-permute-start | bytes 786440 | tf_op jit(solution)/shard_map/ppermute | solution.py:23
  55.7 6.1 %collective-permute-start.11 = (bf16[1,64,1024]{2,1,0:T(8,128)(2,1)S(1)}, bf16[1,64,1024]{2,1,0:T(8,128)(2,1)S(1)}, u32[]{:S(2)}, u32[]{:S(2)}) collective-permute-start(bf16[1,64,1024]{2,1,0:T(8,128)(2,1)S(1)} %get-tuple-element.33), channel_id=1, source_target_pairs={{0,2},{1,3},{2,0},{3,1},{4,6},{5,7},{6,4},{7,5},{8,10},{9,11},{10,... | collective-permute-start | bytes 393224 | tf_op jit(solution)/shard_map/ppermute | solution.py:23
  56.7 7.5 %collective-permute-start.13 = (bf16[1,64,1024]{2,1,0:T(8,128)(2,1)S(1)}, bf16[1,64,1024]{2,1,0:T(8,128)(2,1)S(1)}, u32[]{:S(2)}, u32[]{:S(2)}) collective-permute-start(bf16[1,64,1024]{2,1,0:T(8,128)(2,1)S(1)} %get-tuple-element.34), channel_id=1, source_target_pairs={{0,2},{1,3},{2,0},{3,1},{4,6},{5,7},{6,4},{7,5},{8,10},{9,11},{10,... | collective-permute-start | bytes 393224 | tf_op jit(solution)/shard_map/ppermute | solution.py:23
  57.3 9.7 %collective-permute-start.3 = (bf16[1,64,1024]{2,1,0:T(8,128)(2,1)S(1)}, bf16[1,64,1024]{2,1,0:T(8,128)(2,1)S(1)}, u32[]{:S(2)}, u32[]{:S(2)}) collective-permute-start(bf16[1,64,1024]{2,1,0:T(8,128)(2,1)S(1)} %shard_map.113), channel_id=1, source_target_pairs={{0,2},{1,3},{2,0},{3,1},{4,6},{5,7},{6,4},{7,5},{8,10},{9,11},{10,... | collective-permute-start | bytes 393224 | tf_op jit(solution)/shard_map/ppermute | solution.py:23
  59.1 9.6 %collective-permute-start.29 = (bf16[4,2,16,1024]{3,2,1,0:T(8,128)(2,1)S(1)}, bf16[4,2,16,1024]{3,2,1,0:T(8,128)(2,1)S(1)}, u32[]{:S(2)}, u32[]{:S(2)}) collective-permute-start(bf16[4,2,16,1024]{3,2,1,0:T(8,128)(2,1)S(1)} %pad_maximum_fusion.own_ref), channel_id=1, source_target_pairs={{0,1},{1,0},{2,3},{3,2},{4,5},{5,4},{6,7},{7,6},{8,9},{9,8},{10,11... | collective-permute-start | bytes 786440 | tf_op jit(solution)/shard_map/ppermute | solution.py:23
  61.8 16.4 %collective-permute-start.16 = (bf16[1,256,1024]{2,1,0:T(8,128)(2,1)S(1)}, bf16[1,256,1024]{2,1,0:T(8,128)(2,1)S(1)}, u32[]{:S(2)}, u32[]{:S(2)}) collective-permute-start(bf16[1,256,1024]{2,1,0:T(8,128)(2,1)S(1)} %get-tuple-element.36), channel_id=1, source_target_pairs={{0,2},{1,3},{2,0},{3,1},{4,6},{5,7},{6,4},{7,5},{8,10},{9,11},{10,... | collective-permute-start | bytes 1572872 | tf_op jit(solution)/shard_map/ppermute | solution.py:23
  64.2 3.6 %collective-permute-start.12 = (bf16[1,64,1024]{2,1,0:T(8,128)(2,1)S(1)}, bf16[1,64,1024]{2,1,0:T(8,128)(2,1)S(1)}, u32[]{:S(2)}, u32[]{:S(2)}) collective-permute-start(bf16[1,64,1024]{2,1,0:T(8,128)(2,1)S(1)} %collective-permute-done.11.refs_0_), channel_id=1, source_target_pairs={{0,1},{1,0},{2,3},{3,2},{4,5},{5,4},{6,7},{7,6},{8,9},{9,8},{10,11... | collective-permute-start | bytes 393224 | tf_op jit(solution)/shard_map/ppermute | solution.py:23
  67.0 29.1 %collective-permute-start.15 = (bf16[1,512,1024]{2,1,0:T(8,128)(2,1)S(1)}, bf16[1,512,1024]{2,1,0:T(8,128)(2,1)S(1)}, u32[]{:S(2)}, u32[]{:S(2)}) collective-permute-start(bf16[1,512,1024]{2,1,0:T(8,128)(2,1)S(1)} %get-tuple-element.35.refs_0_), channel_id=1, source_target_pairs={{0,1},{1,0},{2,3},{3,2},{4,5},{5,4},{6,7},{7,6},{8,9},{9,8},{10,11... | collective-permute-start | bytes 3145736 | tf_op jit(solution)/shard_map/ppermute | solution.py:23
  67.1 19.5 %collective-permute-start.5 = (bf16[1,192,1024]{2,1,0:T(8,128)(2,1)S(1)}, bf16[1,192,1024]{2,1,0:T(8,128)(2,1)S(1)}, u32[]{:S(2)}, u32[]{:S(2)}) collective-permute-start(bf16[1,192,1024]{2,1,0:T(8,128)(2,1)S(1)} %get-tuple-element.29), channel_id=1, source_target_pairs={{0,2},{1,3},{2,0},{3,1},{4,6},{5,7},{6,4},{7,5},{8,10},{9,11},{10,... | collective-permute-start | bytes 1179656 | tf_op jit(solution)/shard_map/ppermute | solution.py:23
  67.7 27.8 %collective-permute-start.7 = (bf16[1,256,1024]{2,1,0:T(8,128)(2,1)S(1)}, bf16[1,256,1024]{2,1,0:T(8,128)(2,1)S(1)}, u32[]{:S(2)}, u32[]{:S(2)}) collective-permute-start(bf16[1,256,1024]{2,1,0:T(8,128)(2,1)S(1)} %get-tuple-element.30), channel_id=1, source_target_pairs={{0,2},{1,3},{2,0},{3,1},{4,6},{5,7},{6,4},{7,5},{8,10},{9,11},{10,... | collective-permute-start | bytes 1572872 | tf_op jit(solution)/shard_map/ppermute | solution.py:23
  68.7 31.3 %collective-permute-start.2 = (bf16[1,512,1024]{2,1,0:T(8,128)(2,1)S(1)}, bf16[1,512,1024]{2,1,0:T(8,128)(2,1)S(1)}, u32[]{:S(2)}, u32[]{:S(2)}) collective-permute-start(bf16[1,512,1024]{2,1,0:T(8,128)(2,1)S(1)} %get-tuple-element.28.refs_0_), channel_id=1, source_target_pairs={{0,1},{1,0},{2,3},{3,2},{4,5},{5,4},{6,7},{7,6},{8,9},{9,8},{10,11... | collective-permute-start | bytes 3145736 | tf_op jit(solution)/shard_map/ppermute | solution.py:23
  78.2 17.8 %collective-permute-start.17 = (bf16[1,256,1024]{2,1,0:T(8,128)(2,1)S(1)}, bf16[1,256,1024]{2,1,0:T(8,128)(2,1)S(1)}, u32[]{:S(2)}, u32[]{:S(2)}) collective-permute-start(bf16[1,256,1024]{2,1,0:T(8,128)(2,1)S(1)} %collective-permute-done.16.refs_2_), channel_id=1, source_target_pairs={{0,1},{1,0},{2,3},{3,2},{4,5},{5,4},{6,7},{7,6},{8,9},{9,8},{10,11... | collective-permute-start | bytes 1572872 | tf_op jit(solution)/shard_map/ppermute | solution.py:23
  86.6 8.9 %collective-permute-start.19 = (bf16[1,128,1024]{2,1,0:T(8,128)(2,1)S(1)}, bf16[1,128,1024]{2,1,0:T(8,128)(2,1)S(1)}, u32[]{:S(2)}, u32[]{:S(2)}) collective-permute-start(bf16[1,128,1024]{2,1,0:T(8,128)(2,1)S(1)} %collective-permute-done.18.refs_4_), channel_id=1, source_target_pairs={{0,1},{1,0},{2,3},{3,2},{4,5},{5,4},{6,7},{7,6},{8,9},{9,8},{10,11... | collective-permute-start | bytes 786440 | tf_op jit(solution)/shard_map/ppermute | solution.py:23
  95.5 4.5 %collective-permute-start.8 = (bf16[1,256,1024]{2,1,0:T(8,128)(2,1)S(1)}, bf16[1,256,1024]{2,1,0:T(8,128)(2,1)S(1)}, u32[]{:S(2)}, u32[]{:S(2)}) collective-permute-start(bf16[1,256,1024]{2,1,0:T(8,128)(2,1)S(1)} %collective-permute-done.7.refs_6_), channel_id=1, source_target_pairs={{0,1},{1,0},{2,3},{3,2},{4,5},{5,4},{6,7},{7,6},{8,9},{9,8},{10,11... | collective-permute-start | bytes 1572872 | tf_op jit(solution)/shard_map/ppermute | solution.py:23
  95.5 4.5 %collective-permute-start.6 = (bf16[1,192,1024]{2,1,0:T(8,128)(2,1)S(1)}, bf16[1,192,1024]{2,1,0:T(8,128)(2,1)S(1)}, u32[]{:S(2)}, u32[]{:S(2)}) collective-permute-start(bf16[1,192,1024]{2,1,0:T(8,128)(2,1)S(1)} %collective-permute-done.5.refs_4_), channel_id=1, source_target_pairs={{0,1},{1,0},{2,3},{3,2},{4,5},{5,4},{6,7},{7,6},{8,9},{9,8},{10,11... | collective-permute-start | bytes 1179656 | tf_op jit(solution)/shard_map/ppermute | solution.py:23
  96.0 3.1 %collective-permute-start.14 = (bf16[1,64,1024]{2,1,0:T(8,128)(2,1)S(1)}, bf16[1,64,1024]{2,1,0:T(8,128)(2,1)S(1)}, u32[]{:S(2)}, u32[]{:S(2)}) collective-permute-start(bf16[1,64,1024]{2,1,0:T(8,128)(2,1)S(1)} %collective-permute-done.13.refs_2_), channel_id=1, source_target_pairs={{0,1},{1,0},{2,3},{3,2},{4,5},{5,4},{6,7},{7,6},{8,9},{9,8},{10,11... | collective-permute-start | bytes 393224 | tf_op jit(solution)/shard_map/ppermute | solution.py:23
  96.1 3.9 %collective-permute-start.4 = (bf16[1,64,1024]{2,1,0:T(8,128)(2,1)S(1)}, bf16[1,64,1024]{2,1,0:T(8,128)(2,1)S(1)}, u32[]{:S(2)}, u32[]{:S(2)}) collective-permute-start(bf16[1,64,1024]{2,1,0:T(8,128)(2,1)S(1)} %collective-permute-done.3.refs_2_), channel_id=1, source_target_pairs={{0,1},{1,0},{2,3},{3,2},{4,5},{5,4},{6,7},{7,6},{8,9},{9,8},{10,11... | collective-permute-start | bytes 393224 | tf_op jit(solution)/shard_map/ppermute | solution.py:23

commit v5 on v2

--- a/solution.py
+++ b/solution.py
@@ -10,7 +10,8 @@
 
 CORE, CHIP = 1, 2
 GATE = (64, 192, 256)
-UP = (256, 128, 64, 64)
+UP = (256, 128, 112, 16)
+DIRECT = 3
 LOADS = 8
 MIB = 1 << 20
 VMEM = pl.BlockSpec(memory_space=pltpu.VMEM)
@@ -82,9 +83,15 @@
     )(share, w, avg)
 
 
-def narrow_body(first, blocks, whole, fresh_ref, pair_ref, other_ref, *outs):
+def narrow_body(first, blocks, whole, scales, fresh_ref, *refs):
     columns = fresh_ref.shape[1]
-    inverse = 1.0 / jnp.sqrt(pair_ref[:, :columns] + other_ref[:, :columns])
+    totals, outs = refs[: 2 * max(scales, 1)], refs[2 * max(scales, 1) :]
+    scale = [jnp.sqrt(a[:, :columns] + b[:, :columns]) for a, b in zip(totals[::2], totals[1::2])]
+    inverse = 1.0 / scale[0]
+    if scales:
+        for value, out in zip(scale, outs[-scales:]):
+            out[...] = value
+        outs = outs[:-scales]
 
     def rows_of(at):
         return (fresh_ref[pl.ds(at, 16)] * inverse).astype(jnp.bfloat16)
@@ -102,14 +109,15 @@
         at += rows
 
 
-def narrow(fresh, totals, first, blocks, whole):
+def narrow(fresh, totals, first, blocks, whole, scales=0):
     rows, columns = fresh.shape
     sizes = [*blocks, rows] if whole else blocks
-    outs = tuple(pltpu.VMEM((1, n, columns), jnp.bfloat16) for n in sizes)
+    outs = [pltpu.VMEM((1, n, columns), jnp.bfloat16) for n in sizes]
+    outs += [jax.ShapeDtypeStruct((1, columns), jnp.float32)] * scales
     return call(
-        functools.partial(narrow_body, first, blocks, whole),
-        outs,
-        [VMEM, VMEM, VMEM],
+        functools.partial(narrow_body, first, blocks, whole, scales),
+        tuple(outs),
+        [VMEM] * (1 + len(totals)),
         2,
         2 << 20,
         out_specs=(VMEM,) * len(outs),
@@ -154,9 +162,10 @@
     return out
 
 
-def from_all(blocks, whole):
+def from_all(blocks, whole, direct):
     chips = [swap(b, "shard", CHIP) for b in blocks]
-    boths = [swap(b, "shard", CORE) for b in chips]
+    boths = [swap(b, "shard", CORE) for b in chips[:direct]]
+    boths += [swap(b, "shard", CORE | CHIP) for b in blocks[direct:]]
     at = starts([b.shape[1] for b in blocks])
     near = [(whole, 0, 0), (swap(whole, "shard", CORE), CORE, 0)]
     far = [[(c, CHIP, n), (b, CORE | CHIP, n)] for c, b, n in zip(chips, boths, at)]
@@ -224,12 +233,7 @@
         pieces.append(turned(pieces[-1]))
     x = pieces[0]
     x = call(
-        planes_body,
-        jax.ShapeDtypeStruct((4, *x.shape[1:]), x.dtype),
-        [VMEM] * 4,
-        1,
-        1 << 10,
-        out_specs=VMEM,
+        planes_body, jax.ShapeDtypeStruct((4, *x.shape[1:]), x.dtype), [VMEM] * 4, 1, 1 << 10, out_specs=VMEM
     )(*pieces)
     for unit in (1, 4):
         a, b, c = (swap(x, "expert", unit * k) for k in (1, 2, 3))
@@ -247,11 +251,6 @@
     )(x, other).T
 
 
-def scale_of(totals, columns):
-    pair, other = totals
-    return jnp.sqrt(pair[:, :columns] + other[:, :columns])
-
-
 def per_device(w_gate, avg_gate, w_up, avg_up, mix_share, router_weight, router_gain):
     rows, columns = w_gate.shape[1:]
     shape = (1, lax.axis_size("shard") * rows, columns)
@@ -262,19 +261,18 @@
     pair = sums_gate + swap(sums_gate, "shard", CORE)
     pair = jnp.concatenate([pair, part.astype(jnp.float32)], axis=1)
     totals_gate = pair, swap(pair, "shard", CHIP)
-    scale_gate = scale_of(totals_gate, columns)
     gate = narrow(fresh_gate, totals_gate, 0, GATE[:1], False)
     *rest, whole = narrow(fresh_gate, totals_gate, GATE[0], GATE[1:], True)
-    near, far = from_all([*gate, *rest], whole)
+    near, far = from_all([*gate, *rest], whole, len(GATE))
     serve_gate = place(sum(far, near), rows, shape)
 
     fresh_up, sums_up = mean_of(mix_share, w_up, avg_up, 56)
     pair = sums_up + swap(sums_up, "shard", CORE)
     totals_up = pair, swap(pair, "shard", CHIP)
-    scale_up = scale_of(totals_up, columns)
-    *up, whole = narrow(fresh_up, totals_up, 0, UP, True)
-    near, far = from_all(up, whole)
-    serve_up = place(sum(far[:2], near), rows, shape)
+    *up, whole, scale_up, scale_gate = narrow(fresh_up, totals_up + totals_gate, 0, UP, True, scales=2)
+    near, far = from_all(up, whole, DIRECT)
+    serve_up = place(near, rows, shape)
+    serve_up = place(sum(far[:2], []), rows, shape, serve_up)
     serve_up = place(sum(far[2:], []), rows, shape, serve_up)
 
     other = totals_gate[1][:, columns:].astype(jnp.bfloat16)

time: 102 us -> 101 us (level)
  other arithmetic: 1.71 us -> 0.5 us
  Pallas kernels: 10.5 us -> 11.7 us
    sqrt x2 -> x0, other arithmetic: 1.21 us -> none  [scale_of(): return jnp.sqrt(pair[:, :columns] + other[:, :columns])]
    pallas_call x3 -> x4, Pallas kernels: 4.79 us -> 5.42 us  [place(): call(functools.partial(place_body, places), jax.ShapeDtypeStruct(shape, b...]
  transfers between devices with their start and end apart: 30 -> 30, of which waited for: 10 -> 11; matrix products, arithmetic and copies ran while one was open for 2% -> 0% of each run, Pallas kernels for 6% -> 7%
where the time goes in v5:
time: 101 us
  starting transfers between devices  43.6 us (43%)
  waiting for transfers between devices  43 us (43%)
  Pallas kernels  11.7 us (12%)
  between operations  1.72 us (2%)
    ppermute x27, waiting for transfers between devices, swap(): return lax.ppermute(x, axis, [(i, i ^ mask) for i in range(n)])  38.9 us
    ppermute x27, starting transfers between devices, swap(): return lax.ppermute(x, axis, [(i, i ^ mask) for i in range(n)])  35.4 us
    ppermute x3, starting transfers between devices, turned(): return lax.ppermute(x, ('expert', 'shard'), pairs)  8.2 us
    pallas_call x4, Pallas kernels, place(): call(functools.partial(place_body, places), jax.ShapeDtypeStruct(shape, b...  5.42 us
    pallas_call x2, Pallas kernels, mean_of(): call(mean_body, (pltpu.VMEM((rows, columns), jnp.float32), pltpu.VMEM((1,...  4.67 us
    ppermute x3, waiting for transfers between devices, turned(): return lax.ppermute(x, ('expert', 'shard'), pairs)  4.09 us
  transfers between devices with their start and end apart: 30, of which 11 were waited for; matrix products, arithmetic and copies ran while one was open for 0% of the time, Pallas kernels for 7%

profile of v5, /device:TPU:1, one launch (start us, length us, event | category | flops | bytes accessed | tf_op | source)
XLA Modules:
  0.0 100.6 jit_solution(3010090099782340847)
XLA Ops:
  1.3 2.3 %shard_map.110 = (f32[512,1024]{1,0:T(8,128)S(1)}, f32[1,1024]{1,0:T(1,128)S(1)}) custom-call(f32[1]{0:T(128)S(6)} %copy.17.share_ref, f32[1,512,1024]{2,1,0:T(8,128)} %w_ref.2, f32[1,512,1024]{2,1,0:T(8,128)} %avg_ref.2), custom_call_target="tpu_custom_call" | custom-call | flops 4194304 | bytes 4194304 | tf_op jit(solution)/shard_map/pallas_call | solution.py:71
  3.6 3.3 %collective-permute-start = (f32[1,1024]{1,0:T(1,128)S(1)}, f32[1,1024]{1,0:T(1,128)S(1)}, u32[]{:S(2)}, u32[]{:S(2)}) collective-permute-start(f32[1,1024]{1,0:T(1,128)S(1)} %get-tuple-element.25), channel_id=1, source_target_pairs={{0,1},{1,0},{2,3},{3,2},{4,5},{5,4},{6,7},{7,6},{8,9},{9,8},{10,11... | collective-permute-start | bytes 12296 | tf_op jit(solution)/shard_map/ppermute | solution.py:24
  7.0 0.8 collective-permute-done
  7.8 0.1 collective-permute-start.1
  7.9 2.4 %collective-permute-done.1.refs_1_.refs_3_ = f32[1,1536]{1,0:T(1,128)S(1)} collective-permute-done((f32[1,1536]{1,0:T(1,128)S(1)}, f32[1,1536]{1,0:T(1,128)S(1)}, u32[]{:S(2)}, u32[]{:S(2)}) %collective-permute-start.1) | collective-permute-done | bytes 6176 | tf_op jit(solution)/shard_map/ppermute | solution.py:24
  10.4 4.4 %collective-permute-start.20 = (bf16[1,2,1,512]{3,2,1,0:T(2,128)(2,1)S(1)}, bf16[1,2,1,512]{3,2,1,0:T(2,128)(2,1)S(1)}, u32[]{:S(2)}, u32[]{:S(2)}) collective-permute-start(bf16[1,2,1,512]{3,2,1,0:T(2,128)(2,1)S(1)} %constant_dynamic-update-slice_fusion.refs_0_), channel_id=1, source_target_pairs={{0,192},{1,193},{2,66},{3,67},{4,196},{5,197},{6,70},{7,71},{8,200... | collective-permute-start | bytes 6152 | tf_op jit(solution)/shard_map/ppermute | solution.py:220
  14.8 0.8 collective-permute-done.20.refs_1_
  15.5 3.8 %collective-permute-start.21 = (bf16[1,2,1,512]{3,2,1,0:T(2,128)(2,1)S(1)}, bf16[1,2,1,512]{3,2,1,0:T(2,128)(2,1)S(1)}, u32[]{:S(2)}, u32[]{:S(2)}) collective-permute-start(bf16[1,2,1,512]{3,2,1,0:T(2,128)(2,1)S(1)} %collective-permute-done.20.refs_1_), channel_id=1, source_target_pairs={{0,192},{1,193},{2,66},{3,67},{4,196},{5,197},{6,70},{7,71},{8,200... | collective-permute-start | bytes 6152 | tf_op jit(solution)/shard_map/ppermute | solution.py:220
  19.4 2.3 %shard_map.114 = (f32[512,1024]{1,0:T(8,128)S(1)}, f32[1,1024]{1,0:T(1,128)S(1)}) custom-call(f32[1]{0:T(128)S(6)} %copy.17.share_ref, f32[1,512,1024]{2,1,0:T(8,128)} %w_ref.3, f32[1,512,1024]{2,1,0:T(8,128)} %avg_ref.3), custom_call_target="tpu_custom_call" | custom-call | flops 4194304 | bytes 4194304 | tf_op jit(solution)/shard_map/pallas_call | solution.py:71
  21.7 3.0 %collective-permute-start.9 = (f32[1,1024]{1,0:T(1,128)S(1)}, f32[1,1024]{1,0:T(1,128)S(1)}, u32[]{:S(2)}, u32[]{:S(2)}) collective-permute-start(f32[1,1024]{1,0:T(1,128)S(1)} %get-tuple-element.30), channel_id=1, source_target_pairs={{0,1},{1,0},{2,3},{3,2},{4,5},{5,4},{6,7},{7,6},{8,9},{9,8},{10,11... | collective-permute-start | bytes 12296 | tf_op jit(solution)/shard_map/ppermute | solution.py:24
  24.7 3.3 %collective-permute-done.22.refs_3_ = bf16[1,2,1,512]{3,2,1,0:T(2,128)(2,1)S(1)} collective-permute-done((bf16[1,2,1,512]{3,2,1,0:T(2,128)(2,1)S(1)}, bf16[1,2,1,512]{3,2,1,0:T(2,128)(2,1)S(1)}, u32[]{:S(2)}, u32[]{:S(2)}) %collective-permute-start.22) | collective-permute-done | bytes 2080 | tf_op jit(solution)/shard_map/ppermute | solution.py:220
  28.1 1.3 %collective-permute-start.23 = (bf16[4,2,1,512]{3,2,1,0:T(2,128)(2,1)S(1)}, bf16[4,2,1,512]{3,2,1,0:T(2,128)(2,1)S(1)}, u32[]{:S(2)}, u32[]{:S(2)}) collective-permute-start(bf16[4,2,1,512]{3,2,1,0:T(2,128)(2,1)S(1)} %shard_map.120), channel_id=1, source_target_pairs={{0,4},{4,0},{8,12},{12,8},{16,20},{20,16},{24,28},{28,24},{32,36},... | collective-permute-start | bytes 24584 | tf_op jit(solution)/shard_map/ppermute | solution.py:24
  29.4 2.5 %collective-permute-start.24 = (bf16[4,2,1,512]{3,2,1,0:T(2,128)(2,1)S(1)}, bf16[4,2,1,512]{3,2,1,0:T(2,128)(2,1)S(1)}, u32[]{:S(2)}, u32[]{:S(2)}) collective-permute-start(bf16[4,2,1,512]{3,2,1,0:T(2,128)(2,1)S(1)} %shard_map.120), channel_id=1, source_target_pairs={{0,8},{4,12},{8,0},{12,4},{16,24},{20,28},{24,16},{28,20},{32,40},... | collective-permute-start | bytes 24584 | tf_op jit(solution)/shard_map/ppermute | solution.py:24
  31.8 0.2 collective-permute-start.25
  32.1 0.1 collective-permute-start.10
  32.2 1.3 %collective-permute-done.24 = bf16[4,2,1,512]{3,2,1,0:T(2,128)(2,1)S(1)} collective-permute-done((bf16[4,2,1,512]{3,2,1,0:T(2,128)(2,1)S(1)}, bf16[4,2,1,512]{3,2,1,0:T(2,128)(2,1)S(1)}, u32[]{:S(2)}, u32[]{:S(2)}) %collective-permute-start.24) | collective-permute-done | bytes 8224 | tf_op jit(solution)/shard_map/ppermute | solution.py:24
  33.5 2.3 %collective-permute-done.25 = bf16[4,2,1,512]{3,2,1,0:T(2,128)(2,1)S(1)} collective-permute-done((bf16[4,2,1,512]{3,2,1,0:T(2,128)(2,1)S(1)}, bf16[4,2,1,512]{3,2,1,0:T(2,128)(2,1)S(1)}, u32[]{:S(2)}, u32[]{:S(2)}) %collective-permute-start.25) | collective-permute-done | bytes 8224 | tf_op jit(solution)/shard_map/ppermute | solution.py:24
  35.8 0.1 broadcast_select_fusion.7
  36.0 1.4 %collective-permute-start.26 = (bf16[4,2,4,512]{3,2,1,0:T(4,128)(2,1)S(1)}, bf16[4,2,4,512]{3,2,1,0:T(4,128)(2,1)S(1)}, u32[]{:S(2)}, u32[]{:S(2)}) collective-permute-start(bf16[4,2,4,512]{3,2,1,0:T(4,128)(2,1)S(1)} %pad_maximum_fusion.3), channel_id=1, source_target_pairs={{0,16},{4,20},{8,24},{12,28},{16,0},{20,4},{24,8},{28,12},{32,48},... | collective-permute-start | bytes 98312 | tf_op jit(solution)/shard_map/ppermute | solution.py:24
  37.4 2.6 %collective-permute-start.27 = (bf16[4,2,4,512]{3,2,1,0:T(4,128)(2,1)S(1)}, bf16[4,2,4,512]{3,2,1,0:T(4,128)(2,1)S(1)}, u32[]{:S(2)}, u32[]{:S(2)}) collective-permute-start(bf16[4,2,4,512]{3,2,1,0:T(4,128)(2,1)S(1)} %pad_maximum_fusion.3), channel_id=1, source_target_pairs={{0,32},{4,36},{8,40},{12,44},{16,48},{20,52},{24,56},{28,60},{32,0... | collective-permute-start | bytes 98312 | tf_op jit(solution)/shard_map/ppermute | solution.py:24
  40.0 0.7 shard_map.115
  40.7 5.2 %collective-permute-start.14 = (bf16[1,16,1024]{2,1,0:T(8,128)(2,1)S(1)}, bf16[1,16,1024]{2,1,0:T(8,128)(2,1)S(1)}, u32[]{:S(2)}, u32[]{:S(2)}) collective-permute-start(bf16[1,16,1024]{2,1,0:T(8,128)(2,1)S(1)} %get-tuple-element.32), channel_id=1, source_target_pairs={{0,3},{1,2},{2,1},{3,0},{4,7},{5,6},{6,5},{7,4},{8,11},{9,10},{10,... | collective-permute-start | bytes 98312 | tf_op jit(solution)/shard_map/ppermute | solution.py:24
  46.0 0.1 collective-permute-start.19
  46.1 1.1 %collective-permute-start.17 = (bf16[1,128,1024]{2,1,0:T(8,128)(2,1)S(1)}, bf16[1,128,1024]{2,1,0:T(8,128)(2,1)S(1)}, u32[]{:S(2)}, u32[]{:S(2)}) collective-permute-start(bf16[1,128,1024]{2,1,0:T(8,128)(2,1)S(1)} %get-tuple-element.34), channel_id=1, source_target_pairs={{0,2},{1,3},{2,0},{3,1},{4,6},{5,7},{6,4},{7,5},{8,10},{9,11},{10,... | collective-permute-start | bytes 786440 | tf_op jit(solution)/shard_map/ppermute | solution.py:24
  47.2 0.5 collective-permute-start.3
  47.7 0.1 broadcast_select_fusion.11
  47.9 1.1 %collective-permute-start.11 = (bf16[1,112,1024]{2,1,0:T(8,128)(2,1)S(1)}, bf16[1,112,1024]{2,1,0:T(8,128)(2,1)S(1)}, u32[]{:S(2)}, u32[]{:S(2)}) collective-permute-start(bf16[1,112,1024]{2,1,0:T(8,128)(2,1)S(1)} %get-tuple-element.31), channel_id=1, source_target_pairs={{0,2},{1,3},{2,0},{3,1},{4,6},{5,7},{6,4},{7,5},{8,10},{9,11},{10,... | collective-permute-start | bytes 688136 | tf_op jit(solution)/shard_map/ppermute | solution.py:24
  49.0 1.9 %collective-permute-start.29 = (bf16[4,2,16,512]{3,2,1,0:T(8,128)(2,1)S(1)}, bf16[4,2,16,512]{3,2,1,0:T(8,128)(2,1)S(1)}, u32[]{:S(2)}, u32[]{:S(2)}) collective-permute-start(bf16[4,2,16,512]{3,2,1,0:T(8,128)(2,1)S(1)} %pad_maximum_fusion.own_ref), channel_id=1, source_target_pairs={{0,1},{1,0},{2,3},{3,2},{4,5},{5,4},{6,7},{7,6},{8,9},{9,8},{10,11... | collective-permute-start | bytes 393224 | tf_op jit(solution)/shard_map/ppermute | solution.py:24
  50.9 5.6 %collective-permute-done.3.refs_2_ = bf16[1,64,1024]{2,1,0:T(8,128)(2,1)S(1)} collective-permute-done((bf16[1,64,1024]{2,1,0:T(8,128)(2,1)S(1)}, bf16[1,64,1024]{2,1,0:T(8,128)(2,1)S(1)}, u32[]{:S(2)}, u32[]{:S(2)}) %collective-permute-start.3) | collective-permute-done | bytes 131104 | tf_op jit(solution)/shard_map/ppermute | solution.py:24
  56.5 1.0 collective-permute-start.15
  57.5 0.1 shard_map.111
  57.7 0.6 collective-permute-start.5
  58.2 3.2 %collective-permute-done.11.refs_0_ = bf16[1,112,1024]{2,1,0:T(8,128)(2,1)S(1)} collective-permute-done((bf16[1,112,1024]{2,1,0:T(8,128)(2,1)S(1)}, bf16[1,112,1024]{2,1,0:T(8,128)(2,1)S(1)}, u32[]{:S(2)}, u32[]{:S(2)}) %collective-permute-start.11) | collective-permute-done | bytes 229408 | tf_op jit(solution)/shard_map/ppermute | solution.py:24
  61.4 1.0 collective-permute-start.7
  62.4 2.4 %collective-permute-start.2 = (bf16[1,512,1024]{2,1,0:T(8,128)(2,1)S(1)}, bf16[1,512,1024]{2,1,0:T(8,128)(2,1)S(1)}, u32[]{:S(2)}, u32[]{:S(2)}) collective-permute-start(bf16[1,512,1024]{2,1,0:T(8,128)(2,1)S(1)} %get-tuple-element.26.refs_0_), channel_id=1, source_target_pairs={{0,1},{1,0},{2,3},{3,2},{4,5},{5,4},{6,7},{7,6},{8,9},{9,8},{10,11... | collective-permute-start | bytes 3145736 | tf_op jit(solution)/shard_map/ppermute | solution.py:24
  64.8 7.8 %collective-permute-done.15.refs_0_ = bf16[1,256,1024]{2,1,0:T(8,128)(2,1)S(1)} collective-permute-done((bf16[1,256,1024]{2,1,0:T(8,128)(2,1)S(1)}, bf16[1,256,1024]{2,1,0:T(8,128)(2,1)S(1)}, u32[]{:S(2)}, u32[]{:S(2)}) %collective-permute-start.15) | collective-permute-done | bytes 524320 | tf_op jit(solution)/shard_map/ppermute | solution.py:24
  72.6 2.1 %collective-permute-start.16 = (bf16[1,256,1024]{2,1,0:T(8,128)(2,1)S(1)}, bf16[1,256,1024]{2,1,0:T(8,128)(2,1)S(1)}, u32[]{:S(2)}, u32[]{:S(2)}) collective-permute-start(bf16[1,256,1024]{2,1,0:T(8,128)(2,1)S(1)} %collective-permute-done.15.refs_0_), channel_id=1, source_target_pairs={{0,1},{1,0},{2,3},{3,2},{4,5},{5,4},{6,7},{7,6},{8,9},{9,8},{10,11... | collective-permute-start | bytes 1572872 | tf_op jit(solution)/shard_map/ppermute | solution.py:24
  74.8 6.3 %collective-permute-done.5.refs_4_ = bf16[1,192,1024]{2,1,0:T(8,128)(2,1)S(1)} collective-permute-done((bf16[1,192,1024]{2,1,0:T(8,128)(2,1)S(1)}, bf16[1,192,1024]{2,1,0:T(8,128)(2,1)S(1)}, u32[]{:S(2)}, u32[]{:S(2)}) %collective-permute-start.5) | collective-permute-done | bytes 393248 | tf_op jit(solution)/shard_map/ppermute | solution.py:24
  81.1 2.1 %collective-permute-start.18 = (bf16[1,128,1024]{2,1,0:T(8,128)(2,1)S(1)}, bf16[1,128,1024]{2,1,0:T(8,128)(2,1)S(1)}, u32[]{:S(2)}, u32[]{:S(2)}) collective-permute-start(bf16[1,128,1024]{2,1,0:T(8,128)(2,1)S(1)} %collective-permute-done.17.refs_2_), channel_id=1, source_target_pairs={{0,1},{1,0},{2,3},{3,2},{4,5},{5,4},{6,7},{7,6},{8,9},{9,8},{10,11... | collective-permute-start | bytes 786440 | tf_op jit(solution)/shard_map/ppermute | solution.py:24
  83.2 9.1 %collective-permute-done.7.refs_6_ = bf16[1,256,1024]{2,1,0:T(8,128)(2,1)S(1)} collective-permute-done((bf16[1,256,1024]{2,1,0:T(8,128)(2,1)S(1)}, bf16[1,256,1024]{2,1,0:T(8,128)(2,1)S(1)}, u32[]{:S(2)}, u32[]{:S(2)}) %collective-permute-start.7) | collective-permute-done | bytes 524320 | tf_op jit(solution)/shard_map/ppermute | solution.py:24
  92.3 1.3 %collective-permute-start.8 = (bf16[1,256,1024]{2,1,0:T(8,128)(2,1)S(1)}, bf16[1,256,1024]{2,1,0:T(8,128)(2,1)S(1)}, u32[]{:S(2)}, u32[]{:S(2)}) collective-permute-start(bf16[1,256,1024]{2,1,0:T(8,128)(2,1)S(1)} %collective-permute-done.7.refs_6_), channel_id=1, source_target_pairs={{0,1},{1,0},{2,3},{3,2},{4,5},{5,4},{6,7},{7,6},{8,9},{9,8},{10,11... | collective-permute-start | bytes 1572872 | tf_op jit(solution)/shard_map/ppermute | solution.py:24
  93.6 0.5 collective-permute-start.12
  94.1 0.1 collective-permute-start.4
  94.2 0.7 shard_map.121
  94.9 1.3 %shard_map.116.refs_4_ = bf16[1,2048,1024]{2,1,0:T(8,128)(2,1)} custom-call(bf16[1,512,1024]{2,1,0:T(8,128)(2,1)S(1)} %get-tuple-element.35.refs_0_, bf16[1,512,1024]{2,1,0:T(8,128)(2,1)S(1)} %collective-permute-done.19.refs_1_), custom_call_target="tpu_custom_call" | custom-call | flops 1048576 | bytes 4194304 | tf_op jit(solution)/shard_map/pallas_call | solution.py:145
  96.2 1.2 %shard_map.117.refs_4_ = bf16[1,2048,1024]{2,1,0:T(8,128)(2,1)} custom-call(bf16[1,256,1024]{2,1,0:T(8,128)(2,1)S(1)} %collective-permute-done.15.refs_0_, bf16[1,256,1024]{2,1,0:T(8,128)(2,1)S(1)} %collective-permute-done.16.refs_1_, bf16[1,128,1024]{2,1,0:T(8,128)(2,1)S(1)} %collective-permute-done.17.refs_2_, ...), custom_call_target="tpu_custom_call", output_to_operand_aliasing={{}: (4, {})} | custom-call | flops 1048576 | bytes 4194304 | tf_op jit(solution)/shard_map/pallas_call | solution.py:145
  97.4 0.8 shard_map.118
  98.3 2.1 %shard_map.113 = bf16[1,2048,1024]{2,1,0:T(8,128)(2,1)} custom-call(bf16[1,512,1024]{2,1,0:T(8,128)(2,1)S(1)} %get-tuple-element.26.refs_0_, bf16[1,512,1024]{2,1,0:T(8,128)(2,1)S(1)} %collective-permute-done.2.refs_1_, bf16[1,64,1024]{2,1,0:T(8,128)(2,1)S(1)} %collective-permute-done.3.refs_2_, bf16[1,64,1024]{2,1,0:T(8,128)(2,1)S(1)} %collective-permute-done.4.refs_3_, ...), custom_call_target="tpu_custom_call" | custom-call | flops 1048576 | bytes 4194304 | tf_op jit(solution)/shard_map/pallas_call | solution.py:145
  (46 shorter events, 0.5 us)
Async XLA Ops:
  1.3 5.7 %copy-start = (f32[512,1]{0,1:T(1,128)S(1)}, f32[512,1]{0,1:T(1,128)}, u32[]{:S(2)}) copy-start(f32[512,1]{0,1:T(1,128)} %param.12) | copy-start | bytes 6148
  1.3 5.7 %copy-start.1 = (f32[512]{0:T(512)S(1)}, f32[512]{0:T(512)}, u32[]{:S(2)}) copy-start(f32[512]{0:T(512)} %param.13) | copy-start | bytes 6148
  3.6 4.1 %collective-permute-start = (f32[1,1024]{1,0:T(1,128)S(1)}, f32[1,1024]{1,0:T(1,128)S(1)}, u32[]{:S(2)}, u32[]{:S(2)}) collective-permute-start(f32[1,1024]{1,0:T(1,128)S(1)} %get-tuple-element.25), channel_id=1, source_target_pairs={{0,1},{1,0},{2,3},{3,2},{4,5},{5,4},{6,7},{7,6},{8,9},{9,8},{10,11... | collective-permute-start | bytes 12296 | tf_op jit(solution)/shard_map/ppermute | solution.py:24
  7.8 2.6 %collective-permute-start.1 = (f32[1,1536]{1,0:T(1,128)S(1)}, f32[1,1536]{1,0:T(1,128)S(1)}, u32[]{:S(2)}, u32[]{:S(2)}) collective-permute-start(f32[1,1536]{1,0:T(1,128)S(1)} %pad_maximum_fusion.6.refs_0_.refs_2_), channel_id=1, source_target_pairs={{0,2},{1,3},{2,0},{3,1},{4,6},{5,7},{6,4},{7,5},{8,10},{9,11},{10,... | collective-permute-start | bytes 18440 | tf_op jit(solution)/shard_map/ppermute | solution.py:24
  10.4 5.1 %collective-permute-start.20 = (bf16[1,2,1,512]{3,2,1,0:T(2,128)(2,1)S(1)}, bf16[1,2,1,512]{3,2,1,0:T(2,128)(2,1)S(1)}, u32[]{:S(2)}, u32[]{:S(2)}) collective-permute-start(bf16[1,2,1,512]{3,2,1,0:T(2,128)(2,1)S(1)} %constant_dynamic-update-slice_fusion.refs_0_), channel_id=1, source_target_pairs={{0,192},{1,193},{2,66},{3,67},{4,196},{5,197},{6,70},{7,71},{8,200... | collective-permute-start | bytes 6152 | tf_op jit(solution)/shard_map/ppermute | solution.py:220
  15.5 9.2 %collective-permute-start.21 = (bf16[1,2,1,512]{3,2,1,0:T(2,128)(2,1)S(1)}, bf16[1,2,1,512]{3,2,1,0:T(2,128)(2,1)S(1)}, u32[]{:S(2)}, u32[]{:S(2)}) collective-permute-start(bf16[1,2,1,512]{3,2,1,0:T(2,128)(2,1)S(1)} %collective-permute-done.20.refs_1_), channel_id=1, source_target_pairs={{0,192},{1,193},{2,66},{3,67},{4,196},{5,197},{6,70},{7,71},{8,200... | collective-permute-start | bytes 6152 | tf_op jit(solution)/shard_map/ppermute | solution.py:220
  21.7 10.4 %collective-permute-start.9 = (f32[1,1024]{1,0:T(1,128)S(1)}, f32[1,1024]{1,0:T(1,128)S(1)}, u32[]{:S(2)}, u32[]{:S(2)}) collective-permute-start(f32[1,1024]{1,0:T(1,128)S(1)} %get-tuple-element.30), channel_id=1, source_target_pairs={{0,1},{1,0},{2,3},{3,2},{4,5},{5,4},{6,7},{7,6},{8,9},{9,8},{10,11... | collective-permute-start | bytes 12296 | tf_op jit(solution)/shard_map/ppermute | solution.py:24
  24.7 3.4 %collective-permute-start.22 = (bf16[1,2,1,512]{3,2,1,0:T(2,128)(2,1)S(1)}, bf16[1,2,1,512]{3,2,1,0:T(2,128)(2,1)S(1)}, u32[]{:S(2)}, u32[]{:S(2)}) collective-permute-start(bf16[1,2,1,512]{3,2,1,0:T(2,128)(2,1)S(1)} %collective-permute-done.21.refs_2_), channel_id=1, source_target_pairs={{0,192},{1,193},{2,66},{3,67},{4,196},{5,197},{6,70},{7,71},{8,200... | collective-permute-start | bytes 6152 | tf_op jit(solution)/shard_map/ppermute | solution.py:220
  28.1 4.1 %collective-permute-start.23 = (bf16[4,2,1,512]{3,2,1,0:T(2,128)(2,1)S(1)}, bf16[4,2,1,512]{3,2,1,0:T(2,128)(2,1)S(1)}, u32[]{:S(2)}, u32[]{:S(2)}) collective-permute-start(bf16[4,2,1,512]{3,2,1,0:T(2,128)(2,1)S(1)} %shard_map.120), channel_id=1, source_target_pairs={{0,4},{4,0},{8,12},{12,8},{16,20},{20,16},{24,28},{28,24},{32,36},... | collective-permute-start | bytes 24584 | tf_op jit(solution)/shard_map/ppermute | solution.py:24
  29.4 4.1 %collective-permute-start.24 = (bf16[4,2,1,512]{3,2,1,0:T(2,128)(2,1)S(1)}, bf16[4,2,1,512]{3,2,1,0:T(2,128)(2,1)S(1)}, u32[]{:S(2)}, u32[]{:S(2)}) collective-permute-start(bf16[4,2,1,512]{3,2,1,0:T(2,128)(2,1)S(1)} %shard_map.120), channel_id=1, source_target_pairs={{0,8},{4,12},{8,0},{12,4},{16,24},{20,28},{24,16},{28,20},{32,40},... | collective-permute-start | bytes 24584 | tf_op jit(solution)/shard_map/ppermute | solution.py:24
  31.8 3.9 %collective-permute-start.25 = (bf16[4,2,1,512]{3,2,1,0:T(2,128)(2,1)S(1)}, bf16[4,2,1,512]{3,2,1,0:T(2,128)(2,1)S(1)}, u32[]{:S(2)}, u32[]{:S(2)}) collective-permute-start(bf16[4,2,1,512]{3,2,1,0:T(2,128)(2,1)S(1)} %shard_map.120), channel_id=1, source_target_pairs={{0,12},{4,8},{8,4},{12,0},{16,28},{20,24},{24,20},{28,16},{32,44},... | collective-permute-start | bytes 24584 | tf_op jit(solution)/shard_map/ppermute | solution.py:24
  32.1 8.0 %collective-permute-start.10 = (f32[1,1024]{1,0:T(1,128)S(1)}, f32[1,1024]{1,0:T(1,128)S(1)}, u32[]{:S(2)}, u32[]{:S(2)}) collective-permute-start(f32[1,1024]{1,0:T(1,128)S(1)} %add.7.refs_0_), channel_id=1, source_target_pairs={{0,2},{1,3},{2,0},{3,1},{4,6},{5,7},{6,4},{7,5},{8,10},{9,11},{10,... | collective-permute-start | bytes 12296 | tf_op jit(solution)/shard_map/ppermute | solution.py:24
  36.0 10.0 %collective-permute-start.26 = (bf16[4,2,4,512]{3,2,1,0:T(4,128)(2,1)S(1)}, bf16[4,2,4,512]{3,2,1,0:T(4,128)(2,1)S(1)}, u32[]{:S(2)}, u32[]{:S(2)}) collective-permute-start(bf16[4,2,4,512]{3,2,1,0:T(4,128)(2,1)S(1)} %pad_maximum_fusion.3), channel_id=1, source_target_pairs={{0,16},{4,20},{8,24},{12,28},{16,0},{20,4},{24,8},{28,12},{32,48},... | collective-permute-start | bytes 98312 | tf_op jit(solution)/shard_map/ppermute | solution.py:24
  37.4 8.8 %collective-permute-start.27 = (bf16[4,2,4,512]{3,2,1,0:T(4,128)(2,1)S(1)}, bf16[4,2,4,512]{3,2,1,0:T(4,128)(2,1)S(1)}, u32[]{:S(2)}, u32[]{:S(2)}) collective-permute-start(bf16[4,2,4,512]{3,2,1,0:T(4,128)(2,1)S(1)} %pad_maximum_fusion.3), channel_id=1, source_target_pairs={{0,32},{4,36},{8,40},{12,44},{16,48},{20,52},{24,56},{28,60},{32,0... | collective-permute-start | bytes 98312 | tf_op jit(solution)/shard_map/ppermute | solution.py:24
  40.0 7.2 %collective-permute-start.28 = (bf16[4,2,4,512]{3,2,1,0:T(4,128)(2,1)S(1)}, bf16[4,2,4,512]{3,2,1,0:T(4,128)(2,1)S(1)}, u32[]{:S(2)}, u32[]{:S(2)}) collective-permute-start(bf16[4,2,4,512]{3,2,1,0:T(4,128)(2,1)S(1)} %pad_maximum_fusion.3), channel_id=1, source_target_pairs={{0,48},{4,52},{8,56},{12,60},{16,32},{20,36},{24,40},{28,44},{32,1... | collective-permute-start | bytes 98312 | tf_op jit(solution)/shard_map/ppermute | solution.py:24
  40.7 7.1 %collective-permute-start.13 = (bf16[1,16,1024]{2,1,0:T(8,128)(2,1)S(1)}, bf16[1,16,1024]{2,1,0:T(8,128)(2,1)S(1)}, u32[]{:S(2)}, u32[]{:S(2)}) collective-permute-start(bf16[1,16,1024]{2,1,0:T(8,128)(2,1)S(1)} %get-tuple-element.32), channel_id=1, source_target_pairs={{0,2},{1,3},{2,0},{3,1},{4,6},{5,7},{6,4},{7,5},{8,10},{9,11},{10,... | collective-permute-start | bytes 98312 | tf_op jit(solution)/shard_map/ppermute | solution.py:24
  40.7 8.2 %collective-permute-start.14 = (bf16[1,16,1024]{2,1,0:T(8,128)(2,1)S(1)}, bf16[1,16,1024]{2,1,0:T(8,128)(2,1)S(1)}, u32[]{:S(2)}, u32[]{:S(2)}) collective-permute-start(bf16[1,16,1024]{2,1,0:T(8,128)(2,1)S(1)} %get-tuple-element.32), channel_id=1, source_target_pairs={{0,3},{1,2},{2,1},{3,0},{4,7},{5,6},{6,5},{7,4},{8,11},{9,10},{10,... | collective-permute-start | bytes 98312 | tf_op jit(solution)/shard_map/ppermute | solution.py:24
  46.0 47.6 %collective-permute-start.19 = (bf16[1,512,1024]{2,1,0:T(8,128)(2,1)S(1)}, bf16[1,512,1024]{2,1,0:T(8,128)(2,1)S(1)}, u32[]{:S(2)}, u32[]{:S(2)}) collective-permute-start(bf16[1,512,1024]{2,1,0:T(8,128)(2,1)S(1)} %get-tuple-element.35.refs_0_), channel_id=1, source_target_pairs={{0,1},{1,0},{2,3},{3,2},{4,5},{5,4},{6,7},{7,6},{8,9},{9,8},{10,11... | collective-permute-start | bytes 3145736 | tf_op jit(solution)/shard_map/ppermute | solution.py:24
  46.1 16.3 %collective-permute-start.17 = (bf16[1,128,1024]{2,1,0:T(8,128)(2,1)S(1)}, bf16[1,128,1024]{2,1,0:T(8,128)(2,1)S(1)}, u32[]{:S(2)}, u32[]{:S(2)}) collective-permute-start(bf16[1,128,1024]{2,1,0:T(8,128)(2,1)S(1)} %get-tuple-element.34), channel_id=1, source_target_pairs={{0,2},{1,3},{2,0},{3,1},{4,6},{5,7},{6,4},{7,5},{8,10},{9,11},{10,... | collective-permute-start | bytes 786440 | tf_op jit(solution)/shard_map/ppermute | solution.py:24
  47.2 9.3 %collective-permute-start.3 = (bf16[1,64,1024]{2,1,0:T(8,128)(2,1)S(1)}, bf16[1,64,1024]{2,1,0:T(8,128)(2,1)S(1)}, u32[]{:S(2)}, u32[]{:S(2)}) collective-permute-start(bf16[1,64,1024]{2,1,0:T(8,128)(2,1)S(1)} %shard_map.112), channel_id=1, source_target_pairs={{0,2},{1,3},{2,0},{3,1},{4,6},{5,7},{6,4},{7,5},{8,10},{9,11},{10,... | collective-permute-start | bytes 393224 | tf_op jit(solution)/shard_map/ppermute | solution.py:24
  47.9 13.5 %collective-permute-start.11 = (bf16[1,112,1024]{2,1,0:T(8,128)(2,1)S(1)}, bf16[1,112,1024]{2,1,0:T(8,128)(2,1)S(1)}, u32[]{:S(2)}, u32[]{:S(2)}) collective-permute-start(bf16[1,112,1024]{2,1,0:T(8,128)(2,1)S(1)} %get-tuple-element.31), channel_id=1, source_target_pairs={{0,2},{1,3},{2,0},{3,1},{4,6},{5,7},{6,4},{7,5},{8,10},{9,11},{10,... | collective-permute-start | bytes 688136 | tf_op jit(solution)/shard_map/ppermute | solution.py:24
  49.0 8.7 %collective-permute-start.29 = (bf16[4,2,16,512]{3,2,1,0:T(8,128)(2,1)S(1)}, bf16[4,2,16,512]{3,2,1,0:T(8,128)(2,1)S(1)}, u32[]{:S(2)}, u32[]{:S(2)}) collective-permute-start(bf16[4,2,16,512]{3,2,1,0:T(8,128)(2,1)S(1)} %pad_maximum_fusion.own_ref), channel_id=1, source_target_pairs={{0,1},{1,0},{2,3},{3,2},{4,5},{5,4},{6,7},{7,6},{8,9},{9,8},{10,11... | collective-permute-start | bytes 393224 | tf_op jit(solution)/shard_map/ppermute | solution.py:24
  56.5 16.2 %collective-permute-start.15 = (bf16[1,256,1024]{2,1,0:T(8,128)(2,1)S(1)}, bf16[1,256,1024]{2,1,0:T(8,128)(2,1)S(1)}, u32[]{:S(2)}, u32[]{:S(2)}) collective-permute-start(bf16[1,256,1024]{2,1,0:T(8,128)(2,1)S(1)} %get-tuple-element.33), channel_id=1, source_target_pairs={{0,2},{1,3},{2,0},{3,1},{4,6},{5,7},{6,4},{7,5},{8,10},{9,11},{10,... | collective-permute-start | bytes 1572872 | tf_op jit(solution)/shard_map/ppermute | solution.py:24
  57.7 23.4 %collective-permute-start.5 = (bf16[1,192,1024]{2,1,0:T(8,128)(2,1)S(1)}, bf16[1,192,1024]{2,1,0:T(8,128)(2,1)S(1)}, u32[]{:S(2)}, u32[]{:S(2)}) collective-permute-start(bf16[1,192,1024]{2,1,0:T(8,128)(2,1)S(1)} %get-tuple-element.27), channel_id=1, source_target_pairs={{0,2},{1,3},{2,0},{3,1},{4,6},{5,7},{6,4},{7,5},{8,10},{9,11},{10,... | collective-permute-start | bytes 1179656 | tf_op jit(solution)/shard_map/ppermute | solution.py:24
  61.4 30.9 %collective-permute-start.7 = (bf16[1,256,1024]{2,1,0:T(8,128)(2,1)S(1)}, bf16[1,256,1024]{2,1,0:T(8,128)(2,1)S(1)}, u32[]{:S(2)}, u32[]{:S(2)}) collective-permute-start(bf16[1,256,1024]{2,1,0:T(8,128)(2,1)S(1)} %get-tuple-element.28), channel_id=1, source_target_pairs={{0,2},{1,3},{2,0},{3,1},{4,6},{5,7},{6,4},{7,5},{8,10},{9,11},{10,... | collective-permute-start | bytes 1572872 | tf_op jit(solution)/shard_map/ppermute | solution.py:24
  62.4 35.9 %collective-permute-start.2 = (bf16[1,512,1024]{2,1,0:T(8,128)(2,1)S(1)}, bf16[1,512,1024]{2,1,0:T(8,128)(2,1)S(1)}, u32[]{:S(2)}, u32[]{:S(2)}) collective-permute-start(bf16[1,512,1024]{2,1,0:T(8,128)(2,1)S(1)} %get-tuple-element.26.refs_0_), channel_id=1, source_target_pairs={{0,1},{1,0},{2,3},{3,2},{4,5},{5,4},{6,7},{7,6},{8,9},{9,8},{10,11... | collective-permute-start | bytes 3145736 | tf_op jit(solution)/shard_map/ppermute | solution.py:24
  72.6 21.4 %collective-permute-start.16 = (bf16[1,256,1024]{2,1,0:T(8,128)(2,1)S(1)}, bf16[1,256,1024]{2,1,0:T(8,128)(2,1)S(1)}, u32[]{:S(2)}, u32[]{:S(2)}) collective-permute-start(bf16[1,256,1024]{2,1,0:T(8,128)(2,1)S(1)} %collective-permute-done.15.refs_0_), channel_id=1, source_target_pairs={{0,1},{1,0},{2,3},{3,2},{4,5},{5,4},{6,7},{7,6},{8,9},{9,8},{10,11... | collective-permute-start | bytes 1572872 | tf_op jit(solution)/shard_map/ppermute | solution.py:24
  81.1 12.5 %collective-permute-start.18 = (bf16[1,128,1024]{2,1,0:T(8,128)(2,1)S(1)}, bf16[1,128,1024]{2,1,0:T(8,128)(2,1)S(1)}, u32[]{:S(2)}, u32[]{:S(2)}) collective-permute-start(bf16[1,128,1024]{2,1,0:T(8,128)(2,1)S(1)} %collective-permute-done.17.refs_2_), channel_id=1, source_target_pairs={{0,1},{1,0},{2,3},{3,2},{4,5},{5,4},{6,7},{7,6},{8,9},{9,8},{10,11... | collective-permute-start | bytes 786440 | tf_op jit(solution)/shard_map/ppermute | solution.py:24
  92.3 6.0 %collective-permute-start.8 = (bf16[1,256,1024]{2,1,0:T(8,128)(2,1)S(1)}, bf16[1,256,1024]{2,1,0:T(8,128)(2,1)S(1)}, u32[]{:S(2)}, u32[]{:S(2)}) collective-permute-start(bf16[1,256,1024]{2,1,0:T(8,128)(2,1)S(1)} %collective-permute-done.7.refs_6_), channel_id=1, source_target_pairs={{0,1},{1,0},{2,3},{3,2},{4,5},{5,4},{6,7},{7,6},{8,9},{9,8},{10,11... | collective-permute-start | bytes 1572872 | tf_op jit(solution)/shard_map/ppermute | solution.py:24
  93.6 4.7 %collective-permute-start.6 = (bf16[1,192,1024]{2,1,0:T(8,128)(2,1)S(1)}, bf16[1,192,1024]{2,1,0:T(8,128)(2,1)S(1)}, u32[]{:S(2)}, u32[]{:S(2)}) collective-permute-start(bf16[1,192,1024]{2,1,0:T(8,128)(2,1)S(1)} %collective-permute-done.5.refs_4_), channel_id=1, source_target_pairs={{0,1},{1,0},{2,3},{3,2},{4,5},{5,4},{6,7},{7,6},{8,9},{9,8},{10,11... | collective-permute-start | bytes 1179656 | tf_op jit(solution)/shard_map/ppermute | solution.py:24
  93.6 3.9 %collective-permute-start.12 = (bf16[1,112,1024]{2,1,0:T(8,128)(2,1)S(1)}, bf16[1,112,1024]{2,1,0:T(8,128)(2,1)S(1)}, u32[]{:S(2)}, u32[]{:S(2)}) collective-permute-start(bf16[1,112,1024]{2,1,0:T(8,128)(2,1)S(1)} %collective-permute-done.11.refs_0_), channel_id=1, source_target_pairs={{0,1},{1,0},{2,3},{3,2},{4,5},{5,4},{6,7},{7,6},{8,9},{9,8},{10,11... | collective-permute-start | bytes 688136 | tf_op jit(solution)/shard_map/ppermute | solution.py:24
  94.1 4.2 %collective-permute-start.4 = (bf16[1,64,1024]{2,1,0:T(8,128)(2,1)S(1)}, bf16[1,64,1024]{2,1,0:T(8,128)(2,1)S(1)}, u32[]{:S(2)}, u32[]{:S(2)}) collective-permute-start(bf16[1,64,1024]{2,1,0:T(8,128)(2,1)S(1)} %collective-permute-done.3.refs_2_), channel_id=1, source_target_pairs={{0,1},{1,0},{2,3},{3,2},{4,5},{5,4},{6,7},{7,6},{8,9},{9,8},{10,11... | collective-permute-start | bytes 393224 | tf_op jit(solution)/shard_map/ppermute | solution.py:24

commit v6 on v5

--- a/solution.py
+++ b/solution.py
@@ -9,9 +9,8 @@
 
 
 CORE, CHIP = 1, 2
-GATE = (64, 192, 256)
-UP = (256, 128, 112, 16)
-DIRECT = 3
+GATE = (112, 144, 256)
+UP = (256, 128, 64, 64)
 LOADS = 8
 MIB = 1 << 20
 VMEM = pl.BlockSpec(memory_space=pltpu.VMEM)
@@ -35,15 +34,15 @@
     )
 
 
-def mean_body(share_ref, w_ref, avg_ref, fresh_ref, sums_ref, w_buf, avg_buf, sem):
+def mean_body(first, share_ref, w_ref, avg_ref, fresh_ref, sums_ref, w_buf, avg_buf, sem):
     rows = w_buf.shape[0]
     step = rows // LOADS
 
     def copies(k):
-        at = pl.ds(k * step, step)
+        at, source = pl.ds(k * step, step), pl.ds(first + k * step, step)
         return (
-            pltpu.make_async_copy(w_ref.at[0, at], w_buf.at[at], sem.at[0, k]),
-            pltpu.make_async_copy(avg_ref.at[0, at], avg_buf.at[at], sem.at[1, k]),
+            pltpu.make_async_copy(w_ref.at[0, source], w_buf.at[at], sem.at[0, k]),
+            pltpu.make_async_copy(avg_ref.at[0, source], avg_buf.at[at], sem.at[1, k]),
         )
 
     for k in range(LOADS):
@@ -66,10 +65,11 @@
     sums_ref[...] = jnp.sum(total, axis=0, keepdims=True)
 
 
-def mean_of(share, w, avg, mib):
-    _, rows, columns = w.shape
+def mean_of(share, w, avg, mib, first=0, rows=None):
+    columns = w.shape[2]
+    rows = rows or w.shape[1]
     return call(
-        mean_body,
+        functools.partial(mean_body, first),
         (pltpu.VMEM((rows, columns), jnp.float32), pltpu.VMEM((1, columns), jnp.float32)),
         [SMEM, HBM, HBM],
         mib,
@@ -83,8 +83,9 @@
     )(share, w, avg)
 
 
-def narrow_body(first, blocks, whole, scales, fresh_ref, *refs):
-    columns = fresh_ref.shape[1]
+def narrow_body(first, blocks, whole, scales, parts, *refs):
+    fresh, refs = refs[:parts], refs[parts:]
+    part_rows, columns = fresh[0].shape
     totals, outs = refs[: 2 * max(scales, 1)], refs[2 * max(scales, 1) :]
     scale = [jnp.sqrt(a[:, :columns] + b[:, :columns]) for a, b in zip(totals[::2], totals[1::2])]
     inverse = 1.0 / scale[0]
@@ -94,7 +95,7 @@
         outs = outs[:-scales]
 
     def rows_of(at):
-        return (fresh_ref[pl.ds(at, 16)] * inverse).astype(jnp.bfloat16)
+        return (fresh[at // part_rows][pl.ds(at % part_rows, 16)] * inverse).astype(jnp.bfloat16)
 
     if whole:
         for at in range(0, first, 16):
@@ -110,18 +111,18 @@
 
 
 def narrow(fresh, totals, first, blocks, whole, scales=0):
-    rows, columns = fresh.shape
+    rows, columns = sum(f.shape[0] for f in fresh), fresh[0].shape[1]
     sizes = [*blocks, rows] if whole else blocks
     outs = [pltpu.VMEM((1, n, columns), jnp.bfloat16) for n in sizes]
     outs += [jax.ShapeDtypeStruct((1, columns), jnp.float32)] * scales
     return call(
-        functools.partial(narrow_body, first, blocks, whole, scales),
+        functools.partial(narrow_body, first, blocks, whole, scales, len(fresh)),
         tuple(outs),
-        [VMEM] * (1 + len(totals)),
+        [VMEM] * (len(fresh) + len(totals)),
         2,
         2 << 20,
         out_specs=(VMEM,) * len(outs),
-    )(fresh, *totals)
+    )(*fresh, *totals)
 
 
 def place_body(places, *refs):
@@ -162,10 +163,9 @@
     return out
 
 
-def from_all(blocks, whole, direct):
+def from_all(blocks, whole):
     chips = [swap(b, "shard", CHIP) for b in blocks]
-    boths = [swap(b, "shard", CORE) for b in chips[:direct]]
-    boths += [swap(b, "shard", CORE | CHIP) for b in blocks[direct:]]
+    boths = [swap(b, "shard", CORE) for b in chips]
     at = starts([b.shape[1] for b in blocks])
     near = [(whole, 0, 0), (swap(whole, "shard", CORE), CORE, 0)]
     far = [[(c, CHIP, n), (b, CORE | CHIP, n)] for c, b, n in zip(chips, boths, at)]
@@ -233,7 +233,12 @@
         pieces.append(turned(pieces[-1]))
     x = pieces[0]
     x = call(
-        planes_body, jax.ShapeDtypeStruct((4, *x.shape[1:]), x.dtype), [VMEM] * 4, 1, 1 << 10, out_specs=VMEM
+        planes_body,
+        jax.ShapeDtypeStruct((4, *x.shape[1:]), x.dtype),
+        [VMEM] * 4,
+        1,
+        1 << 10,
+        out_specs=VMEM,
     )(*pieces)
     for unit in (1, 4):
         a, b, c = (swap(x, "expert", unit * k) for k in (1, 2, 3))
@@ -261,16 +266,21 @@
     pair = sums_gate + swap(sums_gate, "shard", CORE)
     pair = jnp.concatenate([pair, part.astype(jnp.float32)], axis=1)
     totals_gate = pair, swap(pair, "shard", CHIP)
-    gate = narrow(fresh_gate, totals_gate, 0, GATE[:1], False)
-    *rest, whole = narrow(fresh_gate, totals_gate, GATE[0], GATE[1:], True)
-    near, far = from_all([*gate, *rest], whole, len(GATE))
+    gate = narrow([fresh_gate], totals_gate, 0, GATE[:1], False)
+    *rest, whole = narrow([fresh_gate], totals_gate, GATE[0], GATE[1:], True)
+    near, far = from_all([*gate, *rest], whole)
     serve_gate = place(sum(far, near), rows, shape)
 
-    fresh_up, sums_up = mean_of(mix_share, w_up, avg_up, 56)
+    half = rows // 2
+    fresh_0, sums_0 = mean_of(mix_share, w_up, avg_up, 58, 0, half)
+    fresh_1, sums_1 = mean_of(mix_share, w_up, avg_up, 56, half, half)
+    fresh_up, sums_up = [fresh_0, fresh_1], sums_0 + sums_1
     pair = sums_up + swap(sums_up, "shard", CORE)
     totals_up = pair, swap(pair, "shard", CHIP)
-    *up, whole, scale_up, scale_gate = narrow(fresh_up, totals_up + totals_gate, 0, UP, True, scales=2)
-    near, far = from_all(up, whole, DIRECT)
+    *up, whole, scale_up, scale_gate = narrow(
+        fresh_up, totals_up + totals_gate, 0, UP, True, scales=2
+    )
+    near, far = from_all(up, whole)
     serve_up = place(near, rows, shape)
     serve_up = place(sum(far[:2], []), rows, shape, serve_up)
     serve_up = place(sum(far[2:], []), rows, shape, serve_up)

time: 101 us -> 102 us (level)
  waiting for transfers between devices: 43 us -> 51.6 us
  starting transfers between devices: 43.6 us -> 35.2 us
  Pallas kernels: 11.7 us -> 13 us
    ppermute x27, waiting for transfers between devices: 38.9 us -> 47.5 us  [swap(): return lax.ppermute(x, axis, [(i, i ^ mask) for i in range(n)])]
    ppermute x27, starting transfers between devices: 35.4 us -> 27 us  [swap(): return lax.ppermute(x, axis, [(i, i ^ mask) for i in range(n)])]
    pallas_call x5 -> x6, Pallas kernels: 5.56 us -> 6.79 us  [the longest x3 5.89 us: mean_of(): call(functools.partial(mean_body, first), (pltpu.VMEM((rows, columns), jn...]
  transfers between devices with their start and end apart: 30 -> 30, of which waited for: 11 -> 13; matrix products, arithmetic and copies ran while one was open for 0% -> 0% of each run, Pallas kernels for 7% -> 8%
where the time goes in v6:
time: 102 us
  waiting for transfers between devices  51.6 us (51%)
  starting transfers between devices  35.2 us (35%)
  Pallas kernels  13 us (13%)
  between operations  1.7 us (2%)
    ppermute x27, waiting for transfers between devices, swap(): return lax.ppermute(x, axis, [(i, i ^ mask) for i in range(n)])  47.5 us
    ppermute x27, starting transfers between devices, swap(): return lax.ppermute(x, axis, [(i, i ^ mask) for i in range(n)])  27 us
    ppermute x3, starting transfers between devices, turned(): return lax.ppermute(x, ('expert', 'shard'), pairs)  8.2 us
    pallas_call x3, Pallas kernels, mean_of(): call(functools.partial(mean_body, first), (pltpu.VMEM((rows, columns), jn...  5.89 us
    pallas_call x4, Pallas kernels, place(): call(functools.partial(place_body, places), jax.ShapeDtypeStruct(shape, b...  5.42 us
    ppermute x3, waiting for transfers between devices, turned(): return lax.ppermute(x, ('expert', 'shard'), pairs)  4.09 us
  transfers between devices with their start and end apart: 30, of which 13 were waited for; matrix products, arithmetic and copies ran while one was open for 0% of the time, Pallas kernels for 8%

profile of v6, /device:TPU:1, one launch (start us, length us, event | category | flops | bytes accessed | tf_op | source)
XLA Modules:
  0.0 102.1 jit_solution(10930954046119010124)
XLA Ops:
  1.3 2.3 %shard_map.110 = (f32[512,1024]{1,0:T(8,128)S(1)}, f32[1,1024]{1,0:T(1,128)S(1)}) custom-call(f32[1]{0:T(128)S(6)} %copy.17.share_ref, f32[1,512,1024]{2,1,0:T(8,128)} %w_ref.3, f32[1,512,1024]{2,1,0:T(8,128)} %avg_ref.3), custom_call_target="tpu_custom_call" | custom-call | flops 4194304 | bytes 4194304 | tf_op jit(solution)/shard_map/pallas_call | solution.py:71
  3.6 3.3 %collective-permute-start = (f32[1,1024]{1,0:T(1,128)S(1)}, f32[1,1024]{1,0:T(1,128)S(1)}, u32[]{:S(2)}, u32[]{:S(2)}) collective-permute-start(f32[1,1024]{1,0:T(1,128)S(1)} %get-tuple-element.27), channel_id=1, source_target_pairs={{0,1},{1,0},{2,3},{3,2},{4,5},{5,4},{6,7},{7,6},{8,9},{9,8},{10,11... | collective-permute-start | bytes 12296 | tf_op jit(solution)/shard_map/ppermute | solution.py:23
  7.0 0.8 collective-permute-done
  7.8 0.1 collective-permute-start.1
  7.9 2.4 %collective-permute-done.1.refs_2_.refs_5_ = f32[1,1536]{1,0:T(1,128)S(1)} collective-permute-done((f32[1,1536]{1,0:T(1,128)S(1)}, f32[1,1536]{1,0:T(1,128)S(1)}, u32[]{:S(2)}, u32[]{:S(2)}) %collective-permute-start.1) | collective-permute-done | bytes 6176 | tf_op jit(solution)/shard_map/ppermute | solution.py:23
  10.4 4.4 %collective-permute-start.20 = (bf16[1,2,1,512]{3,2,1,0:T(2,128)(2,1)S(1)}, bf16[1,2,1,512]{3,2,1,0:T(2,128)(2,1)S(1)}, u32[]{:S(2)}, u32[]{:S(2)}) collective-permute-start(bf16[1,2,1,512]{3,2,1,0:T(2,128)(2,1)S(1)} %constant_dynamic-update-slice_fusion.refs_0_), channel_id=1, source_target_pairs={{0,192},{1,193},{2,66},{3,67},{4,196},{5,197},{6,70},{7,71},{8,200... | collective-permute-start | bytes 6152 | tf_op jit(solution)/shard_map/ppermute | solution.py:220
  14.8 0.8 collective-permute-done.20.refs_1_
  15.5 3.8 %collective-permute-start.21 = (bf16[1,2,1,512]{3,2,1,0:T(2,128)(2,1)S(1)}, bf16[1,2,1,512]{3,2,1,0:T(2,128)(2,1)S(1)}, u32[]{:S(2)}, u32[]{:S(2)}) collective-permute-start(bf16[1,2,1,512]{3,2,1,0:T(2,128)(2,1)S(1)} %collective-permute-done.20.refs_1_), channel_id=1, source_target_pairs={{0,192},{1,193},{2,66},{3,67},{4,196},{5,197},{6,70},{7,71},{8,200... | collective-permute-start | bytes 6152 | tf_op jit(solution)/shard_map/ppermute | solution.py:220
  19.4 1.8 %shard_map.114 = (f32[256,1024]{1,0:T(8,128)S(1)}, f32[1,1024]{1,0:T(1,128)S(1)}) custom-call(f32[1]{0:T(128)S(6)} %copy.17.share_ref, f32[1,512,1024]{2,1,0:T(8,128)} %w_ref.5, f32[1,512,1024]{2,1,0:T(8,128)} %avg_ref.5), custom_call_target="tpu_custom_call" | custom-call | flops 4194304 | bytes 4194304 | tf_op jit(solution)/shard_map/pallas_call | solution.py:71
  21.1 1.8 %shard_map.115 = (f32[256,1024]{1,0:T(8,128)S(1)}, f32[1,1024]{1,0:T(1,128)S(1)}) custom-call(f32[1]{0:T(128)S(6)} %copy.17.share_ref, f32[1,512,1024]{2,1,0:T(8,128)} %w_ref.5, f32[1,512,1024]{2,1,0:T(8,128)} %avg_ref.5), custom_call_target="tpu_custom_call" | custom-call | flops 4194304 | bytes 4194304 | tf_op jit(solution)/shard_map/pallas_call | solution.py:71
  22.9 3.0 %collective-permute-start.9 = (f32[1,1024]{1,0:T(1,128)S(1)}, f32[1,1024]{1,0:T(1,128)S(1)}, u32[]{:S(2)}, u32[]{:S(2)}) collective-permute-start(f32[1,1024]{1,0:T(1,128)S(1)} %add.10), channel_id=1, source_target_pairs={{0,1},{1,0},{2,3},{3,2},{4,5},{5,4},{6,7},{7,6},{8,9},{9,8},{10,11... | collective-permute-start | bytes 12296 | tf_op jit(solution)/shard_map/ppermute | solution.py:23
  26.0 3.3 %collective-permute-done.22.refs_3_ = bf16[1,2,1,512]{3,2,1,0:T(2,128)(2,1)S(1)} collective-permute-done((bf16[1,2,1,512]{3,2,1,0:T(2,128)(2,1)S(1)}, bf16[1,2,1,512]{3,2,1,0:T(2,128)(2,1)S(1)}, u32[]{:S(2)}, u32[]{:S(2)}) %collective-permute-start.22) | collective-permute-done | bytes 2080 | tf_op jit(solution)/shard_map/ppermute | solution.py:220
  29.3 1.3 %collective-permute-start.23 = (bf16[4,2,1,512]{3,2,1,0:T(2,128)(2,1)S(1)}, bf16[4,2,1,512]{3,2,1,0:T(2,128)(2,1)S(1)}, u32[]{:S(2)}, u32[]{:S(2)}) collective-permute-start(bf16[4,2,1,512]{3,2,1,0:T(2,128)(2,1)S(1)} %shard_map.121), channel_id=1, source_target_pairs={{0,4},{4,0},{8,12},{12,8},{16,20},{20,16},{24,28},{28,24},{32,36},... | collective-permute-start | bytes 24584 | tf_op jit(solution)/shard_map/ppermute | solution.py:23
  30.6 2.5 %collective-permute-start.24 = (bf16[4,2,1,512]{3,2,1,0:T(2,128)(2,1)S(1)}, bf16[4,2,1,512]{3,2,1,0:T(2,128)(2,1)S(1)}, u32[]{:S(2)}, u32[]{:S(2)}) collective-permute-start(bf16[4,2,1,512]{3,2,1,0:T(2,128)(2,1)S(1)} %shard_map.121), channel_id=1, source_target_pairs={{0,8},{4,12},{8,0},{12,4},{16,24},{20,28},{24,16},{28,20},{32,40},... | collective-permute-start | bytes 24584 | tf_op jit(solution)/shard_map/ppermute | solution.py:23
  33.1 0.2 collective-permute-start.25
  33.3 0.1 collective-permute-start.10
  33.4 1.3 %collective-permute-done.24 = bf16[4,2,1,512]{3,2,1,0:T(2,128)(2,1)S(1)} collective-permute-done((bf16[4,2,1,512]{3,2,1,0:T(2,128)(2,1)S(1)}, bf16[4,2,1,512]{3,2,1,0:T(2,128)(2,1)S(1)}, u32[]{:S(2)}, u32[]{:S(2)}) %collective-permute-start.24) | collective-permute-done | bytes 8224 | tf_op jit(solution)/shard_map/ppermute | solution.py:23
  34.7 2.3 %collective-permute-done.25 = bf16[4,2,1,512]{3,2,1,0:T(2,128)(2,1)S(1)} collective-permute-done((bf16[4,2,1,512]{3,2,1,0:T(2,128)(2,1)S(1)}, bf16[4,2,1,512]{3,2,1,0:T(2,128)(2,1)S(1)}, u32[]{:S(2)}, u32[]{:S(2)}) %collective-permute-start.25) | collective-permute-done | bytes 8224 | tf_op jit(solution)/shard_map/ppermute | solution.py:23
  37.1 0.1 broadcast_select_fusion.7
  37.2 1.4 %collective-permute-start.26 = (bf16[4,2,4,512]{3,2,1,0:T(4,128)(2,1)S(1)}, bf16[4,2,4,512]{3,2,1,0:T(4,128)(2,1)S(1)}, u32[]{:S(2)}, u32[]{:S(2)}) collective-permute-start(bf16[4,2,4,512]{3,2,1,0:T(4,128)(2,1)S(1)} %pad_maximum_fusion.3), channel_id=1, source_target_pairs={{0,16},{4,20},{8,24},{12,28},{16,0},{20,4},{24,8},{28,12},{32,48},... | collective-permute-start | bytes 98312 | tf_op jit(solution)/shard_map/ppermute | solution.py:23
  38.6 2.6 %collective-permute-start.27 = (bf16[4,2,4,512]{3,2,1,0:T(4,128)(2,1)S(1)}, bf16[4,2,4,512]{3,2,1,0:T(4,128)(2,1)S(1)}, u32[]{:S(2)}, u32[]{:S(2)}) collective-permute-start(bf16[4,2,4,512]{3,2,1,0:T(4,128)(2,1)S(1)} %pad_maximum_fusion.3), channel_id=1, source_target_pairs={{0,32},{4,36},{8,40},{12,44},{16,48},{20,52},{24,56},{28,60},{32,0... | collective-permute-start | bytes 98312 | tf_op jit(solution)/shard_map/ppermute | solution.py:23
  41.3 0.7 shard_map.116
  42.0 3.6 %collective-permute-start.19 = (bf16[1,512,1024]{2,1,0:T(8,128)(2,1)S(1)}, bf16[1,512,1024]{2,1,0:T(8,128)(2,1)S(1)}, u32[]{:S(2)}, u32[]{:S(2)}) collective-permute-start(bf16[1,512,1024]{2,1,0:T(8,128)(2,1)S(1)} %get-tuple-element.39.refs_0_), channel_id=1, source_target_pairs={{0,1},{1,0},{2,3},{3,2},{4,5},{5,4},{6,7},{7,6},{8,9},{9,8},{10,11... | collective-permute-start | bytes 3145736 | tf_op jit(solution)/shard_map/ppermute | solution.py:23
  45.6 1.5 %collective-permute-start.17 = (bf16[1,128,1024]{2,1,0:T(8,128)(2,1)S(1)}, bf16[1,128,1024]{2,1,0:T(8,128)(2,1)S(1)}, u32[]{:S(2)}, u32[]{:S(2)}) collective-permute-start(bf16[1,128,1024]{2,1,0:T(8,128)(2,1)S(1)} %get-tuple-element.38), channel_id=1, source_target_pairs={{0,2},{1,3},{2,0},{3,1},{4,6},{5,7},{6,4},{7,5},{8,10},{9,11},{10,... | collective-permute-start | bytes 786440 | tf_op jit(solution)/shard_map/ppermute | solution.py:23
  47.2 0.1 collective-permute-start.11
  47.3 1.4 %collective-permute-start.13 = (bf16[1,64,1024]{2,1,0:T(8,128)(2,1)S(1)}, bf16[1,64,1024]{2,1,0:T(8,128)(2,1)S(1)}, u32[]{:S(2)}, u32[]{:S(2)}) collective-permute-start(bf16[1,64,1024]{2,1,0:T(8,128)(2,1)S(1)} %get-tuple-element.36), channel_id=1, source_target_pairs={{0,2},{1,3},{2,0},{3,1},{4,6},{5,7},{6,4},{7,5},{8,10},{9,11},{10,... | collective-permute-start | bytes 393224 | tf_op jit(solution)/shard_map/ppermute | solution.py:23
  48.7 0.1 broadcast_select_fusion.11
  48.8 18.6 %collective-permute-done.11.refs_0_ = bf16[1,64,1024]{2,1,0:T(8,128)(2,1)S(1)} collective-permute-done((bf16[1,64,1024]{2,1,0:T(8,128)(2,1)S(1)}, bf16[1,64,1024]{2,1,0:T(8,128)(2,1)S(1)}, u32[]{:S(2)}, u32[]{:S(2)}) %collective-permute-start.11) | collective-permute-done | bytes 131104 | tf_op jit(solution)/shard_map/ppermute | solution.py:23
  67.5 0.2 collective-permute-start.3
  67.7 2.6 %collective-permute-done.13.refs_2_ = bf16[1,64,1024]{2,1,0:T(8,128)(2,1)S(1)} collective-permute-done((bf16[1,64,1024]{2,1,0:T(8,128)(2,1)S(1)}, bf16[1,64,1024]{2,1,0:T(8,128)(2,1)S(1)}, u32[]{:S(2)}, u32[]{:S(2)}) %collective-permute-start.13) | collective-permute-done | bytes 131104 | tf_op jit(solution)/shard_map/ppermute | solution.py:23
  70.3 1.3 %collective-permute-start.29 = (bf16[4,2,16,512]{3,2,1,0:T(8,128)(2,1)S(1)}, bf16[4,2,16,512]{3,2,1,0:T(8,128)(2,1)S(1)}, u32[]{:S(2)}, u32[]{:S(2)}) collective-permute-start(bf16[4,2,16,512]{3,2,1,0:T(8,128)(2,1)S(1)} %pad_maximum_fusion.own_ref), channel_id=1, source_target_pairs={{0,1},{1,0},{2,3},{3,2},{4,5},{5,4},{6,7},{7,6},{8,9},{9,8},{10,11... | collective-permute-start | bytes 393224 | tf_op jit(solution)/shard_map/ppermute | solution.py:23
  71.6 0.1 shard_map.111
  71.8 0.8 collective-permute-done.29.other_ref
  72.6 1.9 %collective-permute-done.3.refs_2_ = bf16[1,112,1024]{2,1,0:T(8,128)(2,1)S(1)} collective-permute-done((bf16[1,112,1024]{2,1,0:T(8,128)(2,1)S(1)}, bf16[1,112,1024]{2,1,0:T(8,128)(2,1)S(1)}, u32[]{:S(2)}, u32[]{:S(2)}) %collective-permute-start.3) | collective-permute-done | bytes 229408 | tf_op jit(solution)/shard_map/ppermute | solution.py:23
  74.5 2.0 %collective-permute-start.2 = (bf16[1,512,1024]{2,1,0:T(8,128)(2,1)S(1)}, bf16[1,512,1024]{2,1,0:T(8,128)(2,1)S(1)}, u32[]{:S(2)}, u32[]{:S(2)}) collective-permute-start(bf16[1,512,1024]{2,1,0:T(8,128)(2,1)S(1)} %get-tuple-element.28.refs_0_), channel_id=1, source_target_pairs={{0,1},{1,0},{2,3},{3,2},{4,5},{5,4},{6,7},{7,6},{8,9},{9,8},{10,11... | collective-permute-start | bytes 3145736 | tf_op jit(solution)/shard_map/ppermute | solution.py:23
  76.4 2.5 %collective-permute-done.12.refs_1_ = bf16[1,64,1024]{2,1,0:T(8,128)(2,1)S(1)} collective-permute-done((bf16[1,64,1024]{2,1,0:T(8,128)(2,1)S(1)}, bf16[1,64,1024]{2,1,0:T(8,128)(2,1)S(1)}, u32[]{:S(2)}, u32[]{:S(2)}) %collective-permute-start.12) | collective-permute-done | bytes 131104 | tf_op jit(solution)/shard_map/ppermute | solution.py:23
  78.9 0.7 collective-permute-start.16
  79.6 13.2 %collective-permute-done.5.refs_4_ = bf16[1,144,1024]{2,1,0:T(8,128)(2,1)S(1)} collective-permute-done((bf16[1,144,1024]{2,1,0:T(8,128)(2,1)S(1)}, bf16[1,144,1024]{2,1,0:T(8,128)(2,1)S(1)}, u32[]{:S(2)}, u32[]{:S(2)}) %collective-permute-start.5) | collective-permute-done | bytes 294944 | tf_op jit(solution)/shard_map/ppermute | solution.py:23
  92.8 0.9 collective-permute-start.18
  93.6 1.2 %collective-permute-done.18.refs_3_ = bf16[1,128,1024]{2,1,0:T(8,128)(2,1)S(1)} collective-permute-done((bf16[1,128,1024]{2,1,0:T(8,128)(2,1)S(1)}, bf16[1,128,1024]{2,1,0:T(8,128)(2,1)S(1)}, u32[]{:S(2)}, u32[]{:S(2)}) %collective-permute-start.18) | collective-permute-done | bytes 262176 | tf_op jit(solution)/shard_map/ppermute | solution.py:23
  94.8 0.4 collective-permute-start.6
  95.2 0.1 collective-permute-start.4
  95.3 0.4 collective-permute-start.14
  95.7 0.7 shard_map.122
  96.4 1.3 %shard_map.117.refs_4_ = bf16[1,2048,1024]{2,1,0:T(8,128)(2,1)} custom-call(bf16[1,512,1024]{2,1,0:T(8,128)(2,1)S(1)} %get-tuple-element.39.refs_0_, bf16[1,512,1024]{2,1,0:T(8,128)(2,1)S(1)} %collective-permute-done.19.refs_1_), custom_call_target="tpu_custom_call" | custom-call | flops 1048576 | bytes 4194304 | tf_op jit(solution)/shard_map/pallas_call | solution.py:146
  97.7 1.2 %shard_map.118.refs_4_ = bf16[1,2048,1024]{2,1,0:T(8,128)(2,1)} custom-call(bf16[1,256,1024]{2,1,0:T(8,128)(2,1)S(1)} %collective-permute-done.15.refs_0_, bf16[1,256,1024]{2,1,0:T(8,128)(2,1)S(1)} %collective-permute-done.16.refs_1_, bf16[1,128,1024]{2,1,0:T(8,128)(2,1)S(1)} %collective-permute-done.17.refs_2_, ...), custom_call_target="tpu_custom_call", output_to_operand_aliasing={{}: (4, {})} | custom-call | flops 1048576 | bytes 4194304 | tf_op jit(solution)/shard_map/pallas_call | solution.py:146
  98.9 0.8 shard_map.119
  99.8 2.1 %shard_map.113 = bf16[1,2048,1024]{2,1,0:T(8,128)(2,1)} custom-call(bf16[1,512,1024]{2,1,0:T(8,128)(2,1)S(1)} %get-tuple-element.28.refs_0_, bf16[1,512,1024]{2,1,0:T(8,128)(2,1)S(1)} %collective-permute-done.2.refs_1_, bf16[1,112,1024]{2,1,0:T(8,128)(2,1)S(1)} %collective-permute-done.3.refs_2_, bf16[1,112,1024]{2,1,0:T(8,128)(2,1)S(1)} %collective-permute-done.4.refs_3_, ...), custom_call_target="tpu_custom_call" | custom-call | flops 1048576 | bytes 4194304 | tf_op jit(solution)/shard_map/pallas_call | solution.py:146
  (48 shorter events, 0.5 us)
Async XLA Ops:
  1.3 5.7 %copy-start = (f32[512,1]{0,1:T(1,128)S(1)}, f32[512,1]{0,1:T(1,128)}, u32[]{:S(2)}) copy-start(f32[512,1]{0,1:T(1,128)} %param.12) | copy-start | bytes 6148
  1.3 5.7 %copy-start.1 = (f32[512]{0:T(512)S(1)}, f32[512]{0:T(512)}, u32[]{:S(2)}) copy-start(f32[512]{0:T(512)} %param.13) | copy-start | bytes 6148
  3.6 4.1 %collective-permute-start = (f32[1,1024]{1,0:T(1,128)S(1)}, f32[1,1024]{1,0:T(1,128)S(1)}, u32[]{:S(2)}, u32[]{:S(2)}) collective-permute-start(f32[1,1024]{1,0:T(1,128)S(1)} %get-tuple-element.27), channel_id=1, source_target_pairs={{0,1},{1,0},{2,3},{3,2},{4,5},{5,4},{6,7},{7,6},{8,9},{9,8},{10,11... | collective-permute-start | bytes 12296 | tf_op jit(solution)/shard_map/ppermute | solution.py:23
  7.8 2.6 %collective-permute-start.1 = (f32[1,1536]{1,0:T(1,128)S(1)}, f32[1,1536]{1,0:T(1,128)S(1)}, u32[]{:S(2)}, u32[]{:S(2)}) collective-permute-start(f32[1,1536]{1,0:T(1,128)S(1)} %pad_maximum_fusion.6.refs_1_.refs_4_), channel_id=1, source_target_pairs={{0,2},{1,3},{2,0},{3,1},{4,6},{5,7},{6,4},{7,5},{8,10},{9,11},{10,... | collective-permute-start | bytes 18440 | tf_op jit(solution)/shard_map/ppermute | solution.py:23
  10.4 5.1 %collective-permute-start.20 = (bf16[1,2,1,512]{3,2,1,0:T(2,128)(2,1)S(1)}, bf16[1,2,1,512]{3,2,1,0:T(2,128)(2,1)S(1)}, u32[]{:S(2)}, u32[]{:S(2)}) collective-permute-start(bf16[1,2,1,512]{3,2,1,0:T(2,128)(2,1)S(1)} %constant_dynamic-update-slice_fusion.refs_0_), channel_id=1, source_target_pairs={{0,192},{1,193},{2,66},{3,67},{4,196},{5,197},{6,70},{7,71},{8,200... | collective-permute-start | bytes 6152 | tf_op jit(solution)/shard_map/ppermute | solution.py:220
  15.5 10.4 %collective-permute-start.21 = (bf16[1,2,1,512]{3,2,1,0:T(2,128)(2,1)S(1)}, bf16[1,2,1,512]{3,2,1,0:T(2,128)(2,1)S(1)}, u32[]{:S(2)}, u32[]{:S(2)}) collective-permute-start(bf16[1,2,1,512]{3,2,1,0:T(2,128)(2,1)S(1)} %collective-permute-done.20.refs_1_), channel_id=1, source_target_pairs={{0,192},{1,193},{2,66},{3,67},{4,196},{5,197},{6,70},{7,71},{8,200... | collective-permute-start | bytes 6152 | tf_op jit(solution)/shard_map/ppermute | solution.py:220
  22.9 10.4 %collective-permute-start.9 = (f32[1,1024]{1,0:T(1,128)S(1)}, f32[1,1024]{1,0:T(1,128)S(1)}, u32[]{:S(2)}, u32[]{:S(2)}) collective-permute-start(f32[1,1024]{1,0:T(1,128)S(1)} %add.10), channel_id=1, source_target_pairs={{0,1},{1,0},{2,3},{3,2},{4,5},{5,4},{6,7},{7,6},{8,9},{9,8},{10,11... | collective-permute-start | bytes 12296 | tf_op jit(solution)/shard_map/ppermute | solution.py:23
  25.9 3.4 %collective-permute-start.22 = (bf16[1,2,1,512]{3,2,1,0:T(2,128)(2,1)S(1)}, bf16[1,2,1,512]{3,2,1,0:T(2,128)(2,1)S(1)}, u32[]{:S(2)}, u32[]{:S(2)}) collective-permute-start(bf16[1,2,1,512]{3,2,1,0:T(2,128)(2,1)S(1)} %collective-permute-done.21.refs_2_), channel_id=1, source_target_pairs={{0,192},{1,193},{2,66},{3,67},{4,196},{5,197},{6,70},{7,71},{8,200... | collective-permute-start | bytes 6152 | tf_op jit(solution)/shard_map/ppermute | solution.py:220
  29.3 4.1 %collective-permute-start.23 = (bf16[4,2,1,512]{3,2,1,0:T(2,128)(2,1)S(1)}, bf16[4,2,1,512]{3,2,1,0:T(2,128)(2,1)S(1)}, u32[]{:S(2)}, u32[]{:S(2)}) collective-permute-start(bf16[4,2,1,512]{3,2,1,0:T(2,128)(2,1)S(1)} %shard_map.121), channel_id=1, source_target_pairs={{0,4},{4,0},{8,12},{12,8},{16,20},{20,16},{24,28},{28,24},{32,36},... | collective-permute-start | bytes 24584 | tf_op jit(solution)/shard_map/ppermute | solution.py:23
  30.6 4.1 %collective-permute-start.24 = (bf16[4,2,1,512]{3,2,1,0:T(2,128)(2,1)S(1)}, bf16[4,2,1,512]{3,2,1,0:T(2,128)(2,1)S(1)}, u32[]{:S(2)}, u32[]{:S(2)}) collective-permute-start(bf16[4,2,1,512]{3,2,1,0:T(2,128)(2,1)S(1)} %shard_map.121), channel_id=1, source_target_pairs={{0,8},{4,12},{8,0},{12,4},{16,24},{20,28},{24,16},{28,20},{32,40},... | collective-permute-start | bytes 24584 | tf_op jit(solution)/shard_map/ppermute | solution.py:23
  33.1 3.9 %collective-permute-start.25 = (bf16[4,2,1,512]{3,2,1,0:T(2,128)(2,1)S(1)}, bf16[4,2,1,512]{3,2,1,0:T(2,128)(2,1)S(1)}, u32[]{:S(2)}, u32[]{:S(2)}) collective-permute-start(bf16[4,2,1,512]{3,2,1,0:T(2,128)(2,1)S(1)} %shard_map.121), channel_id=1, source_target_pairs={{0,12},{4,8},{8,4},{12,0},{16,28},{20,24},{24,20},{28,16},{32,44},... | collective-permute-start | bytes 24584 | tf_op jit(solution)/shard_map/ppermute | solution.py:23
  33.3 7.9 %collective-permute-start.10 = (f32[1,1024]{1,0:T(1,128)S(1)}, f32[1,1024]{1,0:T(1,128)S(1)}, u32[]{:S(2)}, u32[]{:S(2)}) collective-permute-start(f32[1,1024]{1,0:T(1,128)S(1)} %add.11.refs_2_), channel_id=1, source_target_pairs={{0,2},{1,3},{2,0},{3,1},{4,6},{5,7},{6,4},{7,5},{8,10},{9,11},{10,... | collective-permute-start | bytes 12296 | tf_op jit(solution)/shard_map/ppermute | solution.py:23
  37.2 8.4 %collective-permute-start.26 = (bf16[4,2,4,512]{3,2,1,0:T(4,128)(2,1)S(1)}, bf16[4,2,4,512]{3,2,1,0:T(4,128)(2,1)S(1)}, u32[]{:S(2)}, u32[]{:S(2)}) collective-permute-start(bf16[4,2,4,512]{3,2,1,0:T(4,128)(2,1)S(1)} %pad_maximum_fusion.3), channel_id=1, source_target_pairs={{0,16},{4,20},{8,24},{12,28},{16,0},{20,4},{24,8},{28,12},{32,48},... | collective-permute-start | bytes 98312 | tf_op jit(solution)/shard_map/ppermute | solution.py:23
  38.6 8.6 %collective-permute-start.27 = (bf16[4,2,4,512]{3,2,1,0:T(4,128)(2,1)S(1)}, bf16[4,2,4,512]{3,2,1,0:T(4,128)(2,1)S(1)}, u32[]{:S(2)}, u32[]{:S(2)}) collective-permute-start(bf16[4,2,4,512]{3,2,1,0:T(4,128)(2,1)S(1)} %pad_maximum_fusion.3), channel_id=1, source_target_pairs={{0,32},{4,36},{8,40},{12,44},{16,48},{20,52},{24,56},{28,60},{32,0... | collective-permute-start | bytes 98312 | tf_op jit(solution)/shard_map/ppermute | solution.py:23
  41.2 6.1 %collective-permute-start.28 = (bf16[4,2,4,512]{3,2,1,0:T(4,128)(2,1)S(1)}, bf16[4,2,4,512]{3,2,1,0:T(4,128)(2,1)S(1)}, u32[]{:S(2)}, u32[]{:S(2)}) collective-permute-start(bf16[4,2,4,512]{3,2,1,0:T(4,128)(2,1)S(1)} %pad_maximum_fusion.3), channel_id=1, source_target_pairs={{0,48},{4,52},{8,56},{12,60},{16,32},{20,36},{24,40},{28,44},{32,1... | collective-permute-start | bytes 98312 | tf_op jit(solution)/shard_map/ppermute | solution.py:23
  42.0 53.2 %collective-permute-start.19 = (bf16[1,512,1024]{2,1,0:T(8,128)(2,1)S(1)}, bf16[1,512,1024]{2,1,0:T(8,128)(2,1)S(1)}, u32[]{:S(2)}, u32[]{:S(2)}) collective-permute-start(bf16[1,512,1024]{2,1,0:T(8,128)(2,1)S(1)} %get-tuple-element.39.refs_0_), channel_id=1, source_target_pairs={{0,1},{1,0},{2,3},{3,2},{4,5},{5,4},{6,7},{7,6},{8,9},{9,8},{10,11... | collective-permute-start | bytes 3145736 | tf_op jit(solution)/shard_map/ppermute | solution.py:23
  45.6 33.3 %collective-permute-start.15 = (bf16[1,256,1024]{2,1,0:T(8,128)(2,1)S(1)}, bf16[1,256,1024]{2,1,0:T(8,128)(2,1)S(1)}, u32[]{:S(2)}, u32[]{:S(2)}) collective-permute-start(bf16[1,256,1024]{2,1,0:T(8,128)(2,1)S(1)} %get-tuple-element.37), channel_id=1, source_target_pairs={{0,2},{1,3},{2,0},{3,1},{4,6},{5,7},{6,4},{7,5},{8,10},{9,11},{10,... | collective-permute-start | bytes 1572872 | tf_op jit(solution)/shard_map/ppermute | solution.py:23
  45.6 30.8 %collective-permute-start.17 = (bf16[1,128,1024]{2,1,0:T(8,128)(2,1)S(1)}, bf16[1,128,1024]{2,1,0:T(8,128)(2,1)S(1)}, u32[]{:S(2)}, u32[]{:S(2)}) collective-permute-start(bf16[1,128,1024]{2,1,0:T(8,128)(2,1)S(1)} %get-tuple-element.38), channel_id=1, source_target_pairs={{0,2},{1,3},{2,0},{3,1},{4,6},{5,7},{6,4},{7,5},{8,10},{9,11},{10,... | collective-permute-start | bytes 786440 | tf_op jit(solution)/shard_map/ppermute | solution.py:23
  47.2 20.3 %collective-permute-start.11 = (bf16[1,64,1024]{2,1,0:T(8,128)(2,1)S(1)}, bf16[1,64,1024]{2,1,0:T(8,128)(2,1)S(1)}, u32[]{:S(2)}, u32[]{:S(2)}) collective-permute-start(bf16[1,64,1024]{2,1,0:T(8,128)(2,1)S(1)} %get-tuple-element.35), channel_id=1, source_target_pairs={{0,2},{1,3},{2,0},{3,1},{4,6},{5,7},{6,4},{7,5},{8,10},{9,11},{10,... | collective-permute-start | bytes 393224 | tf_op jit(solution)/shard_map/ppermute | solution.py:23
  47.3 23.0 %collective-permute-start.13 = (bf16[1,64,1024]{2,1,0:T(8,128)(2,1)S(1)}, bf16[1,64,1024]{2,1,0:T(8,128)(2,1)S(1)}, u32[]{:S(2)}, u32[]{:S(2)}) collective-permute-start(bf16[1,64,1024]{2,1,0:T(8,128)(2,1)S(1)} %get-tuple-element.36), channel_id=1, source_target_pairs={{0,2},{1,3},{2,0},{3,1},{4,6},{5,7},{6,4},{7,5},{8,10},{9,11},{10,... | collective-permute-start | bytes 393224 | tf_op jit(solution)/shard_map/ppermute | solution.py:23
  67.5 7.0 %collective-permute-start.3 = (bf16[1,112,1024]{2,1,0:T(8,128)(2,1)S(1)}, bf16[1,112,1024]{2,1,0:T(8,128)(2,1)S(1)}, u32[]{:S(2)}, u32[]{:S(2)}) collective-permute-start(bf16[1,112,1024]{2,1,0:T(8,128)(2,1)S(1)} %shard_map.112), channel_id=1, source_target_pairs={{0,2},{1,3},{2,0},{3,1},{4,6},{5,7},{6,4},{7,5},{8,10},{9,11},{10,... | collective-permute-start | bytes 688136 | tf_op jit(solution)/shard_map/ppermute | solution.py:23
  70.3 2.3 %collective-permute-start.29 = (bf16[4,2,16,512]{3,2,1,0:T(8,128)(2,1)S(1)}, bf16[4,2,16,512]{3,2,1,0:T(8,128)(2,1)S(1)}, u32[]{:S(2)}, u32[]{:S(2)}) collective-permute-start(bf16[4,2,16,512]{3,2,1,0:T(8,128)(2,1)S(1)} %pad_maximum_fusion.own_ref), channel_id=1, source_target_pairs={{0,1},{1,0},{2,3},{3,2},{4,5},{5,4},{6,7},{7,6},{8,9},{9,8},{10,11... | collective-permute-start | bytes 393224 | tf_op jit(solution)/shard_map/ppermute | solution.py:23
  72.6 21.0 %collective-permute-start.7 = (bf16[1,256,1024]{2,1,0:T(8,128)(2,1)S(1)}, bf16[1,256,1024]{2,1,0:T(8,128)(2,1)S(1)}, u32[]{:S(2)}, u32[]{:S(2)}) collective-permute-start(bf16[1,256,1024]{2,1,0:T(8,128)(2,1)S(1)} %get-tuple-element.30), channel_id=1, source_target_pairs={{0,2},{1,3},{2,0},{3,1},{4,6},{5,7},{6,4},{7,5},{8,10},{9,11},{10,... | collective-permute-start | bytes 1572872 | tf_op jit(solution)/shard_map/ppermute | solution.py:23
  74.5 25.4 %collective-permute-start.2 = (bf16[1,512,1024]{2,1,0:T(8,128)(2,1)S(1)}, bf16[1,512,1024]{2,1,0:T(8,128)(2,1)S(1)}, u32[]{:S(2)}, u32[]{:S(2)}) collective-permute-start(bf16[1,512,1024]{2,1,0:T(8,128)(2,1)S(1)} %get-tuple-element.28.refs_0_), channel_id=1, source_target_pairs={{0,1},{1,0},{2,3},{3,2},{4,5},{5,4},{6,7},{7,6},{8,9},{9,8},{10,11... | collective-permute-start | bytes 3145736 | tf_op jit(solution)/shard_map/ppermute | solution.py:23
  76.4 2.5 %collective-permute-start.12 = (bf16[1,64,1024]{2,1,0:T(8,128)(2,1)S(1)}, bf16[1,64,1024]{2,1,0:T(8,128)(2,1)S(1)}, u32[]{:S(2)}, u32[]{:S(2)}) collective-permute-start(bf16[1,64,1024]{2,1,0:T(8,128)(2,1)S(1)} %collective-permute-done.11.refs_0_), channel_id=1, source_target_pairs={{0,1},{1,0},{2,3},{3,2},{4,5},{5,4},{6,7},{7,6},{8,9},{9,8},{10,11... | collective-permute-start | bytes 393224 | tf_op jit(solution)/shard_map/ppermute | solution.py:23
  78.9 13.9 %collective-permute-start.5 = (bf16[1,144,1024]{2,1,0:T(8,128)(2,1)S(1)}, bf16[1,144,1024]{2,1,0:T(8,128)(2,1)S(1)}, u32[]{:S(2)}, u32[]{:S(2)}) collective-permute-start(bf16[1,144,1024]{2,1,0:T(8,128)(2,1)S(1)} %get-tuple-element.29), channel_id=1, source_target_pairs={{0,2},{1,3},{2,0},{3,1},{4,6},{5,7},{6,4},{7,5},{8,10},{9,11},{10,... | collective-permute-start | bytes 884744 | tf_op jit(solution)/shard_map/ppermute | solution.py:23
  78.9 16.4 %collective-permute-start.16 = (bf16[1,256,1024]{2,1,0:T(8,128)(2,1)S(1)}, bf16[1,256,1024]{2,1,0:T(8,128)(2,1)S(1)}, u32[]{:S(2)}, u32[]{:S(2)}) collective-permute-start(bf16[1,256,1024]{2,1,0:T(8,128)(2,1)S(1)} %collective-permute-done.15.refs_0_), channel_id=1, source_target_pairs={{0,1},{1,0},{2,3},{3,2},{4,5},{5,4},{6,7},{7,6},{8,9},{9,8},{10,11... | collective-permute-start | bytes 1572872 | tf_op jit(solution)/shard_map/ppermute | solution.py:23
  92.8 2.0 %collective-permute-start.18 = (bf16[1,128,1024]{2,1,0:T(8,128)(2,1)S(1)}, bf16[1,128,1024]{2,1,0:T(8,128)(2,1)S(1)}, u32[]{:S(2)}, u32[]{:S(2)}) collective-permute-start(bf16[1,128,1024]{2,1,0:T(8,128)(2,1)S(1)} %collective-permute-done.17.refs_2_), channel_id=1, source_target_pairs={{0,1},{1,0},{2,3},{3,2},{4,5},{5,4},{6,7},{7,6},{8,9},{9,8},{10,11... | collective-permute-start | bytes 786440 | tf_op jit(solution)/shard_map/ppermute | solution.py:23
  93.6 6.2 %collective-permute-start.8 = (bf16[1,256,1024]{2,1,0:T(8,128)(2,1)S(1)}, bf16[1,256,1024]{2,1,0:T(8,128)(2,1)S(1)}, u32[]{:S(2)}, u32[]{:S(2)}) collective-permute-start(bf16[1,256,1024]{2,1,0:T(8,128)(2,1)S(1)} %collective-permute-done.7.refs_6_), channel_id=1, source_target_pairs={{0,1},{1,0},{2,3},{3,2},{4,5},{5,4},{6,7},{7,6},{8,9},{9,8},{10,11... | collective-permute-start | bytes 1572872 | tf_op jit(solution)/shard_map/ppermute | solution.py:23
  94.8 5.0 %collective-permute-start.6 = (bf16[1,144,1024]{2,1,0:T(8,128)(2,1)S(1)}, bf16[1,144,1024]{2,1,0:T(8,128)(2,1)S(1)}, u32[]{:S(2)}, u32[]{:S(2)}) collective-permute-start(bf16[1,144,1024]{2,1,0:T(8,128)(2,1)S(1)} %collective-permute-done.5.refs_4_), channel_id=1, source_target_pairs={{0,1},{1,0},{2,3},{3,2},{4,5},{5,4},{6,7},{7,6},{8,9},{9,8},{10,11... | collective-permute-start | bytes 884744 | tf_op jit(solution)/shard_map/ppermute | solution.py:23
  95.2 4.6 %collective-permute-start.4 = (bf16[1,112,1024]{2,1,0:T(8,128)(2,1)S(1)}, bf16[1,112,1024]{2,1,0:T(8,128)(2,1)S(1)}, u32[]{:S(2)}, u32[]{:S(2)}) collective-permute-start(bf16[1,112,1024]{2,1,0:T(8,128)(2,1)S(1)} %collective-permute-done.3.refs_2_), channel_id=1, source_target_pairs={{0,1},{1,0},{2,3},{3,2},{4,5},{5,4},{6,7},{7,6},{8,9},{9,8},{10,11... | collective-permute-start | bytes 688136 | tf_op jit(solution)/shard_map/ppermute | solution.py:23
  95.3 3.6 %collective-permute-start.14 = (bf16[1,64,1024]{2,1,0:T(8,128)(2,1)S(1)}, bf16[1,64,1024]{2,1,0:T(8,128)(2,1)S(1)}, u32[]{:S(2)}, u32[]{:S(2)}) collective-permute-start(bf16[1,64,1024]{2,1,0:T(8,128)(2,1)S(1)} %collective-permute-done.13.refs_2_), channel_id=1, source_target_pairs={{0,1},{1,0},{2,3},{3,2},{4,5},{5,4},{6,7},{7,6},{8,9},{9,8},{10,11... | collective-permute-start | bytes 393224 | tf_op jit(solution)/shard_map/ppermute | solution.py:23

commit v7 on v5

--- a/solution.py
+++ b/solution.py
@@ -10,8 +10,7 @@
 
 CORE, CHIP = 1, 2
 GATE = (64, 192, 256)
-UP = (256, 128, 112, 16)
-DIRECT = 3
+UP = (256, 128, 64, 64)
 LOADS = 8
 MIB = 1 << 20
 VMEM = pl.BlockSpec(memory_space=pltpu.VMEM)
@@ -162,10 +161,9 @@
     return out
 
 
-def from_all(blocks, whole, direct):
+def from_all(blocks, whole):
     chips = [swap(b, "shard", CHIP) for b in blocks]
-    boths = [swap(b, "shard", CORE) for b in chips[:direct]]
-    boths += [swap(b, "shard", CORE | CHIP) for b in blocks[direct:]]
+    boths = [swap(b, "shard", CORE) for b in chips]
     at = starts([b.shape[1] for b in blocks])
     near = [(whole, 0, 0), (swap(whole, "shard", CORE), CORE, 0)]
     far = [[(c, CHIP, n), (b, CORE | CHIP, n)] for c, b, n in zip(chips, boths, at)]
@@ -233,7 +231,12 @@
         pieces.append(turned(pieces[-1]))
     x = pieces[0]
     x = call(
-        planes_body, jax.ShapeDtypeStruct((4, *x.shape[1:]), x.dtype), [VMEM] * 4, 1, 1 << 10, out_specs=VMEM
+        planes_body,
+        jax.ShapeDtypeStruct((4, *x.shape[1:]), x.dtype),
+        [VMEM] * 4,
+        1,
+        1 << 10,
+        out_specs=VMEM,
     )(*pieces)
     for unit in (1, 4):
         a, b, c = (swap(x, "expert", unit * k) for k in (1, 2, 3))
@@ -263,14 +266,16 @@
     totals_gate = pair, swap(pair, "shard", CHIP)
     gate = narrow(fresh_gate, totals_gate, 0, GATE[:1], False)
     *rest, whole = narrow(fresh_gate, totals_gate, GATE[0], GATE[1:], True)
-    near, far = from_all([*gate, *rest], whole, len(GATE))
+    near, far = from_all([*gate, *rest], whole)
     serve_gate = place(sum(far, near), rows, shape)
 
     fresh_up, sums_up = mean_of(mix_share, w_up, avg_up, 56)
     pair = sums_up + swap(sums_up, "shard", CORE)
     totals_up = pair, swap(pair, "shard", CHIP)
-    *up, whole, scale_up, scale_gate = narrow(fresh_up, totals_up + totals_gate, 0, UP, True, scales=2)
-    near, far = from_all(up, whole, DIRECT)
+    *up, whole, scale_up, scale_gate = narrow(
+        fresh_up, totals_up + totals_gate, 0, UP, True, scales=2
+    )
+    near, far = from_all(up, whole)
     serve_up = place(near, rows, shape)
     serve_up = place(sum(far[:2], []), rows, shape, serve_up)
     serve_up = place(sum(far[2:], []), rows, shape, serve_up)

time: 101 us -> 99.5 us (0.985)
  transfers between devices with their start and end apart: 30 -> 30, of which waited for: 11 -> 12; matrix products, arithmetic and copies ran while one was open for 0% -> 0% of each run, Pallas kernels for 7% -> 7%
where the time goes in v7:
time: 99.5 us; the launch traced here: 99.4 us
  starting transfers between devices  42.9 us (43%)
  waiting for transfers between devices  42.5 us (43%)
  Pallas kernels  11.7 us (12%)
  between operations  1.69 us (2%)
    ppermute x27, waiting for transfers between devices, swap(): return lax.ppermute(x, axis, [(i, i ^ mask) for i in range(n)])  38.4 us
    ppermute x27, starting transfers between devices, swap(): return lax.ppermute(x, axis, [(i, i ^ mask) for i in range(n)])  34.7 us
    ppermute x3, starting transfers between devices, turned(): return lax.ppermute(x, ('expert', 'shard'), pairs)  8.2 us
    pallas_call x4, Pallas kernels, place(): call(functools.partial(place_body, places), jax.ShapeDtypeStruct(shape, b...  5.42 us
    pallas_call x2, Pallas kernels, mean_of(): call(mean_body, (pltpu.VMEM((rows, columns), jnp.float32), pltpu.VMEM((1,...  4.67 us
    ppermute x3, waiting for transfers between devices, turned(): return lax.ppermute(x, ('expert', 'shard'), pairs)  4.09 us
  transfers between devices with their start and end apart: 30, of which 12 were waited for; matrix products, arithmetic and copies ran while one was open for 0% of the time, Pallas kernels for 7%

profile of v7, /device:TPU:1, one launch (start us, length us, event | category | flops | bytes accessed | tf_op | source)
XLA Modules:
  0.0 99.4 jit_solution(10979382565941335563)
XLA Ops:
  1.3 2.3 %shard_map.110 = (f32[512,1024]{1,0:T(8,128)S(1)}, f32[1,1024]{1,0:T(1,128)S(1)}) custom-call(f32[1]{0:T(128)S(6)} %copy.17.share_ref, f32[1,512,1024]{2,1,0:T(8,128)} %w_ref.2, f32[1,512,1024]{2,1,0:T(8,128)} %avg_ref.2), custom_call_target="tpu_custom_call" | custom-call | flops 4194304 | bytes 4194304 | tf_op jit(solution)/shard_map/pallas_call | solution.py:70
  3.6 3.3 %collective-permute-start = (f32[1,1024]{1,0:T(1,128)S(1)}, f32[1,1024]{1,0:T(1,128)S(1)}, u32[]{:S(2)}, u32[]{:S(2)}) collective-permute-start(f32[1,1024]{1,0:T(1,128)S(1)} %get-tuple-element.25), channel_id=1, source_target_pairs={{0,1},{1,0},{2,3},{3,2},{4,5},{5,4},{6,7},{7,6},{8,9},{9,8},{10,11... | collective-permute-start | bytes 12296 | tf_op jit(solution)/shard_map/ppermute | solution.py:23
  7.0 0.8 collective-permute-done
  7.8 0.1 collective-permute-start.1
  7.9 2.4 %collective-permute-done.1.refs_1_.refs_3_ = f32[1,1536]{1,0:T(1,128)S(1)} collective-permute-done((f32[1,1536]{1,0:T(1,128)S(1)}, f32[1,1536]{1,0:T(1,128)S(1)}, u32[]{:S(2)}, u32[]{:S(2)}) %collective-permute-start.1) | collective-permute-done | bytes 6176 | tf_op jit(solution)/shard_map/ppermute | solution.py:23
  10.4 4.4 %collective-permute-start.20 = (bf16[1,2,1,512]{3,2,1,0:T(2,128)(2,1)S(1)}, bf16[1,2,1,512]{3,2,1,0:T(2,128)(2,1)S(1)}, u32[]{:S(2)}, u32[]{:S(2)}) collective-permute-start(bf16[1,2,1,512]{3,2,1,0:T(2,128)(2,1)S(1)} %constant_dynamic-update-slice_fusion.refs_0_), channel_id=1, source_target_pairs={{0,192},{1,193},{2,66},{3,67},{4,196},{5,197},{6,70},{7,71},{8,200... | collective-permute-start | bytes 6152 | tf_op jit(solution)/shard_map/ppermute | solution.py:218
  14.8 0.8 collective-permute-done.20.refs_1_
  15.5 3.8 %collective-permute-start.21 = (bf16[1,2,1,512]{3,2,1,0:T(2,128)(2,1)S(1)}, bf16[1,2,1,512]{3,2,1,0:T(2,128)(2,1)S(1)}, u32[]{:S(2)}, u32[]{:S(2)}) collective-permute-start(bf16[1,2,1,512]{3,2,1,0:T(2,128)(2,1)S(1)} %collective-permute-done.20.refs_1_), channel_id=1, source_target_pairs={{0,192},{1,193},{2,66},{3,67},{4,196},{5,197},{6,70},{7,71},{8,200... | collective-permute-start | bytes 6152 | tf_op jit(solution)/shard_map/ppermute | solution.py:218
  19.4 2.3 %shard_map.114 = (f32[512,1024]{1,0:T(8,128)S(1)}, f32[1,1024]{1,0:T(1,128)S(1)}) custom-call(f32[1]{0:T(128)S(6)} %copy.17.share_ref, f32[1,512,1024]{2,1,0:T(8,128)} %w_ref.3, f32[1,512,1024]{2,1,0:T(8,128)} %avg_ref.3), custom_call_target="tpu_custom_call" | custom-call | flops 4194304 | bytes 4194304 | tf_op jit(solution)/shard_map/pallas_call | solution.py:70
  21.7 3.0 %collective-permute-start.9 = (f32[1,1024]{1,0:T(1,128)S(1)}, f32[1,1024]{1,0:T(1,128)S(1)}, u32[]{:S(2)}, u32[]{:S(2)}) collective-permute-start(f32[1,1024]{1,0:T(1,128)S(1)} %get-tuple-element.30), channel_id=1, source_target_pairs={{0,1},{1,0},{2,3},{3,2},{4,5},{5,4},{6,7},{7,6},{8,9},{9,8},{10,11... | collective-permute-start | bytes 12296 | tf_op jit(solution)/shard_map/ppermute | solution.py:23
  24.7 3.3 %collective-permute-done.22.refs_3_ = bf16[1,2,1,512]{3,2,1,0:T(2,128)(2,1)S(1)} collective-permute-done((bf16[1,2,1,512]{3,2,1,0:T(2,128)(2,1)S(1)}, bf16[1,2,1,512]{3,2,1,0:T(2,128)(2,1)S(1)}, u32[]{:S(2)}, u32[]{:S(2)}) %collective-permute-start.22) | collective-permute-done | bytes 2080 | tf_op jit(solution)/shard_map/ppermute | solution.py:218
  28.1 1.3 %collective-permute-start.23 = (bf16[4,2,1,512]{3,2,1,0:T(2,128)(2,1)S(1)}, bf16[4,2,1,512]{3,2,1,0:T(2,128)(2,1)S(1)}, u32[]{:S(2)}, u32[]{:S(2)}) collective-permute-start(bf16[4,2,1,512]{3,2,1,0:T(2,128)(2,1)S(1)} %shard_map.120), channel_id=1, source_target_pairs={{0,4},{4,0},{8,12},{12,8},{16,20},{20,16},{24,28},{28,24},{32,36},... | collective-permute-start | bytes 24584 | tf_op jit(solution)/shard_map/ppermute | solution.py:23
  29.4 2.5 %collective-permute-start.24 = (bf16[4,2,1,512]{3,2,1,0:T(2,128)(2,1)S(1)}, bf16[4,2,1,512]{3,2,1,0:T(2,128)(2,1)S(1)}, u32[]{:S(2)}, u32[]{:S(2)}) collective-permute-start(bf16[4,2,1,512]{3,2,1,0:T(2,128)(2,1)S(1)} %shard_map.120), channel_id=1, source_target_pairs={{0,8},{4,12},{8,0},{12,4},{16,24},{20,28},{24,16},{28,20},{32,40},... | collective-permute-start | bytes 24584 | tf_op jit(solution)/shard_map/ppermute | solution.py:23
  31.8 0.2 collective-permute-start.25
  32.1 0.1 collective-permute-start.10
  32.2 1.3 %collective-permute-done.24 = bf16[4,2,1,512]{3,2,1,0:T(2,128)(2,1)S(1)} collective-permute-done((bf16[4,2,1,512]{3,2,1,0:T(2,128)(2,1)S(1)}, bf16[4,2,1,512]{3,2,1,0:T(2,128)(2,1)S(1)}, u32[]{:S(2)}, u32[]{:S(2)}) %collective-permute-start.24) | collective-permute-done | bytes 8224 | tf_op jit(solution)/shard_map/ppermute | solution.py:23
  33.5 2.3 %collective-permute-done.25 = bf16[4,2,1,512]{3,2,1,0:T(2,128)(2,1)S(1)} collective-permute-done((bf16[4,2,1,512]{3,2,1,0:T(2,128)(2,1)S(1)}, bf16[4,2,1,512]{3,2,1,0:T(2,128)(2,1)S(1)}, u32[]{:S(2)}, u32[]{:S(2)}) %collective-permute-start.25) | collective-permute-done | bytes 8224 | tf_op jit(solution)/shard_map/ppermute | solution.py:23
  36.0 1.4 %collective-permute-start.26 = (bf16[4,2,4,512]{3,2,1,0:T(4,128)(2,1)S(1)}, bf16[4,2,4,512]{3,2,1,0:T(4,128)(2,1)S(1)}, u32[]{:S(2)}, u32[]{:S(2)}) collective-permute-start(bf16[4,2,4,512]{3,2,1,0:T(4,128)(2,1)S(1)} %pad_maximum_fusion.3), channel_id=1, source_target_pairs={{0,16},{4,20},{8,24},{12,28},{16,0},{20,4},{24,8},{28,12},{32,48},... | collective-permute-start | bytes 98312 | tf_op jit(solution)/shard_map/ppermute | solution.py:23
  37.4 2.6 %collective-permute-start.27 = (bf16[4,2,4,512]{3,2,1,0:T(4,128)(2,1)S(1)}, bf16[4,2,4,512]{3,2,1,0:T(4,128)(2,1)S(1)}, u32[]{:S(2)}, u32[]{:S(2)}) collective-permute-start(bf16[4,2,4,512]{3,2,1,0:T(4,128)(2,1)S(1)} %pad_maximum_fusion.3), channel_id=1, source_target_pairs={{0,32},{4,36},{8,40},{12,44},{16,48},{20,52},{24,56},{28,60},{32,0... | collective-permute-start | bytes 98312 | tf_op jit(solution)/shard_map/ppermute | solution.py:23
  40.0 0.7 shard_map.115
  40.7 3.6 %collective-permute-start.19 = (bf16[1,512,1024]{2,1,0:T(8,128)(2,1)S(1)}, bf16[1,512,1024]{2,1,0:T(8,128)(2,1)S(1)}, u32[]{:S(2)}, u32[]{:S(2)}) collective-permute-start(bf16[1,512,1024]{2,1,0:T(8,128)(2,1)S(1)} %get-tuple-element.35.refs_0_), channel_id=1, source_target_pairs={{0,1},{1,0},{2,3},{3,2},{4,5},{5,4},{6,7},{7,6},{8,9},{9,8},{10,11... | collective-permute-start | bytes 3145736 | tf_op jit(solution)/shard_map/ppermute | solution.py:23
  44.4 1.0 %collective-permute-start.17 = (bf16[1,128,1024]{2,1,0:T(8,128)(2,1)S(1)}, bf16[1,128,1024]{2,1,0:T(8,128)(2,1)S(1)}, u32[]{:S(2)}, u32[]{:S(2)}) collective-permute-start(bf16[1,128,1024]{2,1,0:T(8,128)(2,1)S(1)} %get-tuple-element.34), channel_id=1, source_target_pairs={{0,2},{1,3},{2,0},{3,1},{4,6},{5,7},{6,4},{7,5},{8,10},{9,11},{10,... | collective-permute-start | bytes 786440 | tf_op jit(solution)/shard_map/ppermute | solution.py:23
  45.4 0.6 collective-permute-start.11
  46.0 1.0 %collective-permute-start.13 = (bf16[1,64,1024]{2,1,0:T(8,128)(2,1)S(1)}, bf16[1,64,1024]{2,1,0:T(8,128)(2,1)S(1)}, u32[]{:S(2)}, u32[]{:S(2)}) collective-permute-start(bf16[1,64,1024]{2,1,0:T(8,128)(2,1)S(1)} %get-tuple-element.32), channel_id=1, source_target_pairs={{0,2},{1,3},{2,0},{3,1},{4,6},{5,7},{6,4},{7,5},{8,10},{9,11},{10,... | collective-permute-start | bytes 393224 | tf_op jit(solution)/shard_map/ppermute | solution.py:23
  47.0 0.5 collective-permute-start.3
  47.6 7.4 %collective-permute-done.11.refs_0_ = bf16[1,64,1024]{2,1,0:T(8,128)(2,1)S(1)} collective-permute-done((bf16[1,64,1024]{2,1,0:T(8,128)(2,1)S(1)}, bf16[1,64,1024]{2,1,0:T(8,128)(2,1)S(1)}, u32[]{:S(2)}, u32[]{:S(2)}) %collective-permute-start.11) | collective-permute-done | bytes 131104 | tf_op jit(solution)/shard_map/ppermute | solution.py:23
  55.0 1.3 %collective-permute-start.29 = (bf16[4,2,16,512]{3,2,1,0:T(8,128)(2,1)S(1)}, bf16[4,2,16,512]{3,2,1,0:T(8,128)(2,1)S(1)}, u32[]{:S(2)}, u32[]{:S(2)}) collective-permute-start(bf16[4,2,16,512]{3,2,1,0:T(8,128)(2,1)S(1)} %pad_maximum_fusion.own_ref), channel_id=1, source_target_pairs={{0,1},{1,0},{2,3},{3,2},{4,5},{5,4},{6,7},{7,6},{8,9},{9,8},{10,11... | collective-permute-start | bytes 393224 | tf_op jit(solution)/shard_map/ppermute | solution.py:23
  56.3 1.5 %collective-permute-done.13.refs_2_ = bf16[1,64,1024]{2,1,0:T(8,128)(2,1)S(1)} collective-permute-done((bf16[1,64,1024]{2,1,0:T(8,128)(2,1)S(1)}, bf16[1,64,1024]{2,1,0:T(8,128)(2,1)S(1)}, u32[]{:S(2)}, u32[]{:S(2)}) %collective-permute-start.13) | collective-permute-done | bytes 131104 | tf_op jit(solution)/shard_map/ppermute | solution.py:23
  57.8 1.0 %collective-permute-start.15 = (bf16[1,256,1024]{2,1,0:T(8,128)(2,1)S(1)}, bf16[1,256,1024]{2,1,0:T(8,128)(2,1)S(1)}, u32[]{:S(2)}, u32[]{:S(2)}) collective-permute-start(bf16[1,256,1024]{2,1,0:T(8,128)(2,1)S(1)} %get-tuple-element.33), channel_id=1, source_target_pairs={{0,2},{1,3},{2,0},{3,1},{4,6},{5,7},{6,4},{7,5},{8,10},{9,11},{10,... | collective-permute-start | bytes 1572872 | tf_op jit(solution)/shard_map/ppermute | solution.py:23
  58.8 1.8 %collective-permute-done.3.refs_2_ = bf16[1,64,1024]{2,1,0:T(8,128)(2,1)S(1)} collective-permute-done((bf16[1,64,1024]{2,1,0:T(8,128)(2,1)S(1)}, bf16[1,64,1024]{2,1,0:T(8,128)(2,1)S(1)}, u32[]{:S(2)}, u32[]{:S(2)}) %collective-permute-start.3) | collective-permute-done | bytes 131104 | tf_op jit(solution)/shard_map/ppermute | solution.py:23
  60.6 1.3 %collective-permute-start.12 = (bf16[1,64,1024]{2,1,0:T(8,128)(2,1)S(1)}, bf16[1,64,1024]{2,1,0:T(8,128)(2,1)S(1)}, u32[]{:S(2)}, u32[]{:S(2)}) collective-permute-start(bf16[1,64,1024]{2,1,0:T(8,128)(2,1)S(1)} %collective-permute-done.11.refs_0_), channel_id=1, source_target_pairs={{0,1},{1,0},{2,3},{3,2},{4,5},{5,4},{6,7},{7,6},{8,9},{9,8},{10,11... | collective-permute-start | bytes 393224 | tf_op jit(solution)/shard_map/ppermute | solution.py:23
  62.0 0.1 shard_map.111
  62.1 1.1 %collective-permute-start.5 = (bf16[1,192,1024]{2,1,0:T(8,128)(2,1)S(1)}, bf16[1,192,1024]{2,1,0:T(8,128)(2,1)S(1)}, u32[]{:S(2)}, u32[]{:S(2)}) collective-permute-start(bf16[1,192,1024]{2,1,0:T(8,128)(2,1)S(1)} %get-tuple-element.27), channel_id=1, source_target_pairs={{0,2},{1,3},{2,0},{3,1},{4,6},{5,7},{6,4},{7,5},{8,10},{9,11},{10,... | collective-permute-start | bytes 1179656 | tf_op jit(solution)/shard_map/ppermute | solution.py:23
  63.2 0.5 collective-permute-start.7
  63.7 0.6 collective-permute-start.2
  64.3 6.9 %collective-permute-done.15.refs_0_ = bf16[1,256,1024]{2,1,0:T(8,128)(2,1)S(1)} collective-permute-done((bf16[1,256,1024]{2,1,0:T(8,128)(2,1)S(1)}, bf16[1,256,1024]{2,1,0:T(8,128)(2,1)S(1)}, u32[]{:S(2)}, u32[]{:S(2)}) %collective-permute-start.15) | collective-permute-done | bytes 524320 | tf_op jit(solution)/shard_map/ppermute | solution.py:23
  71.1 2.8 %collective-permute-start.16 = (bf16[1,256,1024]{2,1,0:T(8,128)(2,1)S(1)}, bf16[1,256,1024]{2,1,0:T(8,128)(2,1)S(1)}, u32[]{:S(2)}, u32[]{:S(2)}) collective-permute-start(bf16[1,256,1024]{2,1,0:T(8,128)(2,1)S(1)} %collective-permute-done.15.refs_0_), channel_id=1, source_target_pairs={{0,1},{1,0},{2,3},{3,2},{4,5},{5,4},{6,7},{7,6},{8,9},{9,8},{10,11... | collective-permute-start | bytes 1572872 | tf_op jit(solution)/shard_map/ppermute | solution.py:23
  73.9 5.6 %collective-permute-done.5.refs_4_ = bf16[1,192,1024]{2,1,0:T(8,128)(2,1)S(1)} collective-permute-done((bf16[1,192,1024]{2,1,0:T(8,128)(2,1)S(1)}, bf16[1,192,1024]{2,1,0:T(8,128)(2,1)S(1)}, u32[]{:S(2)}, u32[]{:S(2)}) %collective-permute-start.5) | collective-permute-done | bytes 393248 | tf_op jit(solution)/shard_map/ppermute | solution.py:23
  79.5 2.8 %collective-permute-start.18 = (bf16[1,128,1024]{2,1,0:T(8,128)(2,1)S(1)}, bf16[1,128,1024]{2,1,0:T(8,128)(2,1)S(1)}, u32[]{:S(2)}, u32[]{:S(2)}) collective-permute-start(bf16[1,128,1024]{2,1,0:T(8,128)(2,1)S(1)} %collective-permute-done.17.refs_2_), channel_id=1, source_target_pairs={{0,1},{1,0},{2,3},{3,2},{4,5},{5,4},{6,7},{7,6},{8,9},{9,8},{10,11... | collective-permute-start | bytes 786440 | tf_op jit(solution)/shard_map/ppermute | solution.py:23
  82.4 8.4 %collective-permute-done.7.refs_6_ = bf16[1,256,1024]{2,1,0:T(8,128)(2,1)S(1)} collective-permute-done((bf16[1,256,1024]{2,1,0:T(8,128)(2,1)S(1)}, bf16[1,256,1024]{2,1,0:T(8,128)(2,1)S(1)}, u32[]{:S(2)}, u32[]{:S(2)}) %collective-permute-start.7) | collective-permute-done | bytes 524320 | tf_op jit(solution)/shard_map/ppermute | solution.py:23
  90.8 1.6 %collective-permute-start.8 = (bf16[1,256,1024]{2,1,0:T(8,128)(2,1)S(1)}, bf16[1,256,1024]{2,1,0:T(8,128)(2,1)S(1)}, u32[]{:S(2)}, u32[]{:S(2)}) collective-permute-start(bf16[1,256,1024]{2,1,0:T(8,128)(2,1)S(1)} %collective-permute-done.7.refs_6_), channel_id=1, source_target_pairs={{0,1},{1,0},{2,3},{3,2},{4,5},{5,4},{6,7},{7,6},{8,9},{9,8},{10,11... | collective-permute-start | bytes 1572872 | tf_op jit(solution)/shard_map/ppermute | solution.py:23
  92.4 0.5 collective-permute-start.14
  92.9 0.1 collective-permute-start.4
  93.0 0.7 shard_map.121
  93.7 1.3 %shard_map.116.refs_4_ = bf16[1,2048,1024]{2,1,0:T(8,128)(2,1)} custom-call(bf16[1,512,1024]{2,1,0:T(8,128)(2,1)S(1)} %get-tuple-element.35.refs_0_, bf16[1,512,1024]{2,1,0:T(8,128)(2,1)S(1)} %collective-permute-done.19.refs_1_), custom_call_target="tpu_custom_call" | custom-call | flops 1048576 | bytes 4194304 | tf_op jit(solution)/shard_map/pallas_call | solution.py:144
  95.1 1.2 %shard_map.117.refs_4_ = bf16[1,2048,1024]{2,1,0:T(8,128)(2,1)} custom-call(bf16[1,256,1024]{2,1,0:T(8,128)(2,1)S(1)} %collective-permute-done.15.refs_0_, bf16[1,256,1024]{2,1,0:T(8,128)(2,1)S(1)} %collective-permute-done.16.refs_1_, bf16[1,128,1024]{2,1,0:T(8,128)(2,1)S(1)} %collective-permute-done.17.refs_2_, ...), custom_call_target="tpu_custom_call", output_to_operand_aliasing={{}: (4, {})} | custom-call | flops 1048576 | bytes 4194304 | tf_op jit(solution)/shard_map/pallas_call | solution.py:144
  96.3 0.8 shard_map.118
  97.2 2.1 %shard_map.113 = bf16[1,2048,1024]{2,1,0:T(8,128)(2,1)} custom-call(bf16[1,512,1024]{2,1,0:T(8,128)(2,1)S(1)} %get-tuple-element.26.refs_0_, bf16[1,512,1024]{2,1,0:T(8,128)(2,1)S(1)} %collective-permute-done.2.refs_1_, bf16[1,64,1024]{2,1,0:T(8,128)(2,1)S(1)} %collective-permute-done.3.refs_2_, bf16[1,64,1024]{2,1,0:T(8,128)(2,1)S(1)} %collective-permute-done.4.refs_3_, ...), custom_call_target="tpu_custom_call" | custom-call | flops 1048576 | bytes 4194304 | tf_op jit(solution)/shard_map/pallas_call | solution.py:144
  (46 shorter events, 0.7 us)
Async XLA Ops:
  1.3 5.7 %copy-start = (f32[512,1]{0,1:T(1,128)S(1)}, f32[512,1]{0,1:T(1,128)}, u32[]{:S(2)}) copy-start(f32[512,1]{0,1:T(1,128)} %param.12) | copy-start | bytes 6148
  1.3 5.7 %copy-start.1 = (f32[512]{0:T(512)S(1)}, f32[512]{0:T(512)}, u32[]{:S(2)}) copy-start(f32[512]{0:T(512)} %param.13) | copy-start | bytes 6148
  3.6 4.1 %collective-permute-start = (f32[1,1024]{1,0:T(1,128)S(1)}, f32[1,1024]{1,0:T(1,128)S(1)}, u32[]{:S(2)}, u32[]{:S(2)}) collective-permute-start(f32[1,1024]{1,0:T(1,128)S(1)} %get-tuple-element.25), channel_id=1, source_target_pairs={{0,1},{1,0},{2,3},{3,2},{4,5},{5,4},{6,7},{7,6},{8,9},{9,8},{10,11... | collective-permute-start | bytes 12296 | tf_op jit(solution)/shard_map/ppermute | solution.py:23
  7.8 2.6 %collective-permute-start.1 = (f32[1,1536]{1,0:T(1,128)S(1)}, f32[1,1536]{1,0:T(1,128)S(1)}, u32[]{:S(2)}, u32[]{:S(2)}) collective-permute-start(f32[1,1536]{1,0:T(1,128)S(1)} %pad_maximum_fusion.6.refs_0_.refs_2_), channel_id=1, source_target_pairs={{0,2},{1,3},{2,0},{3,1},{4,6},{5,7},{6,4},{7,5},{8,10},{9,11},{10,... | collective-permute-start | bytes 18440 | tf_op jit(solution)/shard_map/ppermute | solution.py:23
  10.4 5.1 %collective-permute-start.20 = (bf16[1,2,1,512]{3,2,1,0:T(2,128)(2,1)S(1)}, bf16[1,2,1,512]{3,2,1,0:T(2,128)(2,1)S(1)}, u32[]{:S(2)}, u32[]{:S(2)}) collective-permute-start(bf16[1,2,1,512]{3,2,1,0:T(2,128)(2,1)S(1)} %constant_dynamic-update-slice_fusion.refs_0_), channel_id=1, source_target_pairs={{0,192},{1,193},{2,66},{3,67},{4,196},{5,197},{6,70},{7,71},{8,200... | collective-permute-start | bytes 6152 | tf_op jit(solution)/shard_map/ppermute | solution.py:218
  15.5 9.2 %collective-permute-start.21 = (bf16[1,2,1,512]{3,2,1,0:T(2,128)(2,1)S(1)}, bf16[1,2,1,512]{3,2,1,0:T(2,128)(2,1)S(1)}, u32[]{:S(2)}, u32[]{:S(2)}) collective-permute-start(bf16[1,2,1,512]{3,2,1,0:T(2,128)(2,1)S(1)} %collective-permute-done.20.refs_1_), channel_id=1, source_target_pairs={{0,192},{1,193},{2,66},{3,67},{4,196},{5,197},{6,70},{7,71},{8,200... | collective-permute-start | bytes 6152 | tf_op jit(solution)/shard_map/ppermute | solution.py:218
  21.7 10.4 %collective-permute-start.9 = (f32[1,1024]{1,0:T(1,128)S(1)}, f32[1,1024]{1,0:T(1,128)S(1)}, u32[]{:S(2)}, u32[]{:S(2)}) collective-permute-start(f32[1,1024]{1,0:T(1,128)S(1)} %get-tuple-element.30), channel_id=1, source_target_pairs={{0,1},{1,0},{2,3},{3,2},{4,5},{5,4},{6,7},{7,6},{8,9},{9,8},{10,11... | collective-permute-start | bytes 12296 | tf_op jit(solution)/shard_map/ppermute | solution.py:23
  24.7 3.4 %collective-permute-start.22 = (bf16[1,2,1,512]{3,2,1,0:T(2,128)(2,1)S(1)}, bf16[1,2,1,512]{3,2,1,0:T(2,128)(2,1)S(1)}, u32[]{:S(2)}, u32[]{:S(2)}) collective-permute-start(bf16[1,2,1,512]{3,2,1,0:T(2,128)(2,1)S(1)} %collective-permute-done.21.refs_2_), channel_id=1, source_target_pairs={{0,192},{1,193},{2,66},{3,67},{4,196},{5,197},{6,70},{7,71},{8,200... | collective-permute-start | bytes 6152 | tf_op jit(solution)/shard_map/ppermute | solution.py:218
  28.1 4.1 %collective-permute-start.23 = (bf16[4,2,1,512]{3,2,1,0:T(2,128)(2,1)S(1)}, bf16[4,2,1,512]{3,2,1,0:T(2,128)(2,1)S(1)}, u32[]{:S(2)}, u32[]{:S(2)}) collective-permute-start(bf16[4,2,1,512]{3,2,1,0:T(2,128)(2,1)S(1)} %shard_map.120), channel_id=1, source_target_pairs={{0,4},{4,0},{8,12},{12,8},{16,20},{20,16},{24,28},{28,24},{32,36},... | collective-permute-start | bytes 24584 | tf_op jit(solution)/shard_map/ppermute | solution.py:23
  29.4 4.1 %collective-permute-start.24 = (bf16[4,2,1,512]{3,2,1,0:T(2,128)(2,1)S(1)}, bf16[4,2,1,512]{3,2,1,0:T(2,128)(2,1)S(1)}, u32[]{:S(2)}, u32[]{:S(2)}) collective-permute-start(bf16[4,2,1,512]{3,2,1,0:T(2,128)(2,1)S(1)} %shard_map.120), channel_id=1, source_target_pairs={{0,8},{4,12},{8,0},{12,4},{16,24},{20,28},{24,16},{28,20},{32,40},... | collective-permute-start | bytes 24584 | tf_op jit(solution)/shard_map/ppermute | solution.py:23
  31.8 3.9 %collective-permute-start.25 = (bf16[4,2,1,512]{3,2,1,0:T(2,128)(2,1)S(1)}, bf16[4,2,1,512]{3,2,1,0:T(2,128)(2,1)S(1)}, u32[]{:S(2)}, u32[]{:S(2)}) collective-permute-start(bf16[4,2,1,512]{3,2,1,0:T(2,128)(2,1)S(1)} %shard_map.120), channel_id=1, source_target_pairs={{0,12},{4,8},{8,4},{12,0},{16,28},{20,24},{24,20},{28,16},{32,44},... | collective-permute-start | bytes 24584 | tf_op jit(solution)/shard_map/ppermute | solution.py:23
  32.1 8.0 %collective-permute-start.10 = (f32[1,1024]{1,0:T(1,128)S(1)}, f32[1,1024]{1,0:T(1,128)S(1)}, u32[]{:S(2)}, u32[]{:S(2)}) collective-permute-start(f32[1,1024]{1,0:T(1,128)S(1)} %add.7.refs_0_), channel_id=1, source_target_pairs={{0,2},{1,3},{2,0},{3,1},{4,6},{5,7},{6,4},{7,5},{8,10},{9,11},{10,... | collective-permute-start | bytes 12296 | tf_op jit(solution)/shard_map/ppermute | solution.py:23
  36.0 9.4 %collective-permute-start.26 = (bf16[4,2,4,512]{3,2,1,0:T(4,128)(2,1)S(1)}, bf16[4,2,4,512]{3,2,1,0:T(4,128)(2,1)S(1)}, u32[]{:S(2)}, u32[]{:S(2)}) collective-permute-start(bf16[4,2,4,512]{3,2,1,0:T(4,128)(2,1)S(1)} %pad_maximum_fusion.3), channel_id=1, source_target_pairs={{0,16},{4,20},{8,24},{12,28},{16,0},{20,4},{24,8},{28,12},{32,48},... | collective-permute-start | bytes 98312 | tf_op jit(solution)/shard_map/ppermute | solution.py:23
  37.4 8.6 %collective-permute-start.27 = (bf16[4,2,4,512]{3,2,1,0:T(4,128)(2,1)S(1)}, bf16[4,2,4,512]{3,2,1,0:T(4,128)(2,1)S(1)}, u32[]{:S(2)}, u32[]{:S(2)}) collective-permute-start(bf16[4,2,4,512]{3,2,1,0:T(4,128)(2,1)S(1)} %pad_maximum_fusion.3), channel_id=1, source_target_pairs={{0,32},{4,36},{8,40},{12,44},{16,48},{20,52},{24,56},{28,60},{32,0... | collective-permute-start | bytes 98312 | tf_op jit(solution)/shard_map/ppermute | solution.py:23
  40.0 7.0 %collective-permute-start.28 = (bf16[4,2,4,512]{3,2,1,0:T(4,128)(2,1)S(1)}, bf16[4,2,4,512]{3,2,1,0:T(4,128)(2,1)S(1)}, u32[]{:S(2)}, u32[]{:S(2)}) collective-permute-start(bf16[4,2,4,512]{3,2,1,0:T(4,128)(2,1)S(1)} %pad_maximum_fusion.3), channel_id=1, source_target_pairs={{0,48},{4,52},{8,56},{12,60},{16,32},{20,36},{24,40},{28,44},{32,1... | collective-permute-start | bytes 98312 | tf_op jit(solution)/shard_map/ppermute | solution.py:23
  40.7 51.7 %collective-permute-start.19 = (bf16[1,512,1024]{2,1,0:T(8,128)(2,1)S(1)}, bf16[1,512,1024]{2,1,0:T(8,128)(2,1)S(1)}, u32[]{:S(2)}, u32[]{:S(2)}) collective-permute-start(bf16[1,512,1024]{2,1,0:T(8,128)(2,1)S(1)} %get-tuple-element.35.refs_0_), channel_id=1, source_target_pairs={{0,1},{1,0},{2,3},{3,2},{4,5},{5,4},{6,7},{7,6},{8,9},{9,8},{10,11... | collective-permute-start | bytes 3145736 | tf_op jit(solution)/shard_map/ppermute | solution.py:23
  44.4 18.9 %collective-permute-start.17 = (bf16[1,128,1024]{2,1,0:T(8,128)(2,1)S(1)}, bf16[1,128,1024]{2,1,0:T(8,128)(2,1)S(1)}, u32[]{:S(2)}, u32[]{:S(2)}) collective-permute-start(bf16[1,128,1024]{2,1,0:T(8,128)(2,1)S(1)} %get-tuple-element.34), channel_id=1, source_target_pairs={{0,2},{1,3},{2,0},{3,1},{4,6},{5,7},{6,4},{7,5},{8,10},{9,11},{10,... | collective-permute-start | bytes 786440 | tf_op jit(solution)/shard_map/ppermute | solution.py:23
  45.4 9.6 %collective-permute-start.11 = (bf16[1,64,1024]{2,1,0:T(8,128)(2,1)S(1)}, bf16[1,64,1024]{2,1,0:T(8,128)(2,1)S(1)}, u32[]{:S(2)}, u32[]{:S(2)}) collective-permute-start(bf16[1,64,1024]{2,1,0:T(8,128)(2,1)S(1)} %get-tuple-element.31), channel_id=1, source_target_pairs={{0,2},{1,3},{2,0},{3,1},{4,6},{5,7},{6,4},{7,5},{8,10},{9,11},{10,... | collective-permute-start | bytes 393224 | tf_op jit(solution)/shard_map/ppermute | solution.py:23
  46.0 11.9 %collective-permute-start.13 = (bf16[1,64,1024]{2,1,0:T(8,128)(2,1)S(1)}, bf16[1,64,1024]{2,1,0:T(8,128)(2,1)S(1)}, u32[]{:S(2)}, u32[]{:S(2)}) collective-permute-start(bf16[1,64,1024]{2,1,0:T(8,128)(2,1)S(1)} %get-tuple-element.32), channel_id=1, source_target_pairs={{0,2},{1,3},{2,0},{3,1},{4,6},{5,7},{6,4},{7,5},{8,10},{9,11},{10,... | collective-permute-start | bytes 393224 | tf_op jit(solution)/shard_map/ppermute | solution.py:23
  47.0 13.7 %collective-permute-start.3 = (bf16[1,64,1024]{2,1,0:T(8,128)(2,1)S(1)}, bf16[1,64,1024]{2,1,0:T(8,128)(2,1)S(1)}, u32[]{:S(2)}, u32[]{:S(2)}) collective-permute-start(bf16[1,64,1024]{2,1,0:T(8,128)(2,1)S(1)} %shard_map.112), channel_id=1, source_target_pairs={{0,2},{1,3},{2,0},{3,1},{4,6},{5,7},{6,4},{7,5},{8,10},{9,11},{10,... | collective-permute-start | bytes 393224 | tf_op jit(solution)/shard_map/ppermute | solution.py:23
  55.0 7.1 %collective-permute-start.29 = (bf16[4,2,16,512]{3,2,1,0:T(8,128)(2,1)S(1)}, bf16[4,2,16,512]{3,2,1,0:T(8,128)(2,1)S(1)}, u32[]{:S(2)}, u32[]{:S(2)}) collective-permute-start(bf16[4,2,16,512]{3,2,1,0:T(8,128)(2,1)S(1)} %pad_maximum_fusion.own_ref), channel_id=1, source_target_pairs={{0,1},{1,0},{2,3},{3,2},{4,5},{5,4},{6,7},{7,6},{8,9},{9,8},{10,11... | collective-permute-start | bytes 393224 | tf_op jit(solution)/shard_map/ppermute | solution.py:23
  57.8 13.3 %collective-permute-start.15 = (bf16[1,256,1024]{2,1,0:T(8,128)(2,1)S(1)}, bf16[1,256,1024]{2,1,0:T(8,128)(2,1)S(1)}, u32[]{:S(2)}, u32[]{:S(2)}) collective-permute-start(bf16[1,256,1024]{2,1,0:T(8,128)(2,1)S(1)} %get-tuple-element.33), channel_id=1, source_target_pairs={{0,2},{1,3},{2,0},{3,1},{4,6},{5,7},{6,4},{7,5},{8,10},{9,11},{10,... | collective-permute-start | bytes 1572872 | tf_op jit(solution)/shard_map/ppermute | solution.py:23
  60.6 3.0 %collective-permute-start.12 = (bf16[1,64,1024]{2,1,0:T(8,128)(2,1)S(1)}, bf16[1,64,1024]{2,1,0:T(8,128)(2,1)S(1)}, u32[]{:S(2)}, u32[]{:S(2)}) collective-permute-start(bf16[1,64,1024]{2,1,0:T(8,128)(2,1)S(1)} %collective-permute-done.11.refs_0_), channel_id=1, source_target_pairs={{0,1},{1,0},{2,3},{3,2},{4,5},{5,4},{6,7},{7,6},{8,9},{9,8},{10,11... | collective-permute-start | bytes 393224 | tf_op jit(solution)/shard_map/ppermute | solution.py:23
  62.1 17.4 %collective-permute-start.5 = (bf16[1,192,1024]{2,1,0:T(8,128)(2,1)S(1)}, bf16[1,192,1024]{2,1,0:T(8,128)(2,1)S(1)}, u32[]{:S(2)}, u32[]{:S(2)}) collective-permute-start(bf16[1,192,1024]{2,1,0:T(8,128)(2,1)S(1)} %get-tuple-element.27), channel_id=1, source_target_pairs={{0,2},{1,3},{2,0},{3,1},{4,6},{5,7},{6,4},{7,5},{8,10},{9,11},{10,... | collective-permute-start | bytes 1179656 | tf_op jit(solution)/shard_map/ppermute | solution.py:23
  63.2 27.6 %collective-permute-start.7 = (bf16[1,256,1024]{2,1,0:T(8,128)(2,1)S(1)}, bf16[1,256,1024]{2,1,0:T(8,128)(2,1)S(1)}, u32[]{:S(2)}, u32[]{:S(2)}) collective-permute-start(bf16[1,256,1024]{2,1,0:T(8,128)(2,1)S(1)} %get-tuple-element.28), channel_id=1, source_target_pairs={{0,2},{1,3},{2,0},{3,1},{4,6},{5,7},{6,4},{7,5},{8,10},{9,11},{10,... | collective-permute-start | bytes 1572872 | tf_op jit(solution)/shard_map/ppermute | solution.py:23
  63.7 33.5 %collective-permute-start.2 = (bf16[1,512,1024]{2,1,0:T(8,128)(2,1)S(1)}, bf16[1,512,1024]{2,1,0:T(8,128)(2,1)S(1)}, u32[]{:S(2)}, u32[]{:S(2)}) collective-permute-start(bf16[1,512,1024]{2,1,0:T(8,128)(2,1)S(1)} %get-tuple-element.26.refs_0_), channel_id=1, source_target_pairs={{0,1},{1,0},{2,3},{3,2},{4,5},{5,4},{6,7},{7,6},{8,9},{9,8},{10,11... | collective-permute-start | bytes 3145736 | tf_op jit(solution)/shard_map/ppermute | solution.py:23
  71.1 21.8 %collective-permute-start.16 = (bf16[1,256,1024]{2,1,0:T(8,128)(2,1)S(1)}, bf16[1,256,1024]{2,1,0:T(8,128)(2,1)S(1)}, u32[]{:S(2)}, u32[]{:S(2)}) collective-permute-start(bf16[1,256,1024]{2,1,0:T(8,128)(2,1)S(1)} %collective-permute-done.15.refs_0_), channel_id=1, source_target_pairs={{0,1},{1,0},{2,3},{3,2},{4,5},{5,4},{6,7},{7,6},{8,9},{9,8},{10,11... | collective-permute-start | bytes 1572872 | tf_op jit(solution)/shard_map/ppermute | solution.py:23
  79.5 12.9 %collective-permute-start.18 = (bf16[1,128,1024]{2,1,0:T(8,128)(2,1)S(1)}, bf16[1,128,1024]{2,1,0:T(8,128)(2,1)S(1)}, u32[]{:S(2)}, u32[]{:S(2)}) collective-permute-start(bf16[1,128,1024]{2,1,0:T(8,128)(2,1)S(1)} %collective-permute-done.17.refs_2_), channel_id=1, source_target_pairs={{0,1},{1,0},{2,3},{3,2},{4,5},{5,4},{6,7},{7,6},{8,9},{9,8},{10,11... | collective-permute-start | bytes 786440 | tf_op jit(solution)/shard_map/ppermute | solution.py:23
  90.8 6.4 %collective-permute-start.8 = (bf16[1,256,1024]{2,1,0:T(8,128)(2,1)S(1)}, bf16[1,256,1024]{2,1,0:T(8,128)(2,1)S(1)}, u32[]{:S(2)}, u32[]{:S(2)}) collective-permute-start(bf16[1,256,1024]{2,1,0:T(8,128)(2,1)S(1)} %collective-permute-done.7.refs_6_), channel_id=1, source_target_pairs={{0,1},{1,0},{2,3},{3,2},{4,5},{5,4},{6,7},{7,6},{8,9},{9,8},{10,11... | collective-permute-start | bytes 1572872 | tf_op jit(solution)/shard_map/ppermute | solution.py:23
  92.4 4.7 %collective-permute-start.6 = (bf16[1,192,1024]{2,1,0:T(8,128)(2,1)S(1)}, bf16[1,192,1024]{2,1,0:T(8,128)(2,1)S(1)}, u32[]{:S(2)}, u32[]{:S(2)}) collective-permute-start(bf16[1,192,1024]{2,1,0:T(8,128)(2,1)S(1)} %collective-permute-done.5.refs_4_), channel_id=1, source_target_pairs={{0,1},{1,0},{2,3},{3,2},{4,5},{5,4},{6,7},{7,6},{8,9},{9,8},{10,11... | collective-permute-start | bytes 1179656 | tf_op jit(solution)/shard_map/ppermute | solution.py:23
  92.4 3.9 %collective-permute-start.14 = (bf16[1,64,1024]{2,1,0:T(8,128)(2,1)S(1)}, bf16[1,64,1024]{2,1,0:T(8,128)(2,1)S(1)}, u32[]{:S(2)}, u32[]{:S(2)}) collective-permute-start(bf16[1,64,1024]{2,1,0:T(8,128)(2,1)S(1)} %collective-permute-done.13.refs_2_), channel_id=1, source_target_pairs={{0,1},{1,0},{2,3},{3,2},{4,5},{5,4},{6,7},{7,6},{8,9},{9,8},{10,11... | collective-permute-start | bytes 393224 | tf_op jit(solution)/shard_map/ppermute | solution.py:23
  92.9 4.2 %collective-permute-start.4 = (bf16[1,64,1024]{2,1,0:T(8,128)(2,1)S(1)}, bf16[1,64,1024]{2,1,0:T(8,128)(2,1)S(1)}, u32[]{:S(2)}, u32[]{:S(2)}) collective-permute-start(bf16[1,64,1024]{2,1,0:T(8,128)(2,1)S(1)} %collective-permute-done.3.refs_2_), channel_id=1, source_target_pairs={{0,1},{1,0},{2,3},{3,2},{4,5},{5,4},{6,7},{7,6},{8,9},{9,8},{10,11... | collective-permute-start | bytes 393224 | tf_op jit(solution)/shard_map/ppermute | solution.py:23
